TPU v7x, 256 devices: a whole 4x4x8 slice. The times are simulated.
256 devices in a mesh: gx: 8 (over z_lo, core), gy: 4 (over x), gz: 8 (over y, z_hi).
Axes of the slice: x: 4, y: 4, z: 8 (z_hi: 2, z_lo: 4; z = z_hi * 4 + z_lo), core: 2. Of those that a mesh axis runs over, the one named last changes fastest.
Arguments:
- displacement: float32 [3, 48, 24, 3072], P(None, 'gx', 'gy', 'gz'), may hold values from -0.18 to 0.18
- size_field_modes: float32 [27, 16, 8, 1024], P(None, 'gx', 'gy', 'gz'), may hold values from -6 to 6
- velocity: float32 [3, 16, 8, 1024], P(None, 'gx', 'gy', 'gz'), may hold values from -1 to 1
Outputs:
- advected_field: float32 [27, 16, 8, 1024], P(None, 'gx', 'gy', 'gz')
- gradient: float32 [3, 48, 24, 3072], P(None, 'gx', 'gy', 'gz')
- checks: float32 [3], replicated
All inputs are finite; a program needn't handle non-finite values. Where the computation divides by a largest or mean magnitude, that divisor is 1e-20 or more.
Results may differ from a plain program's by a relative error of at most 0.0001.
Values sent between devices are 32-bit elements; how exact they have to be, the bound alone decides.
No kernel may reach another device: no remote copies, remote signals or barrier semaphores. Data moves between devices by JAX's collectives and lax.ppermute only.
A program may use at most 64 MiB of HBM per device.

v0:
```python
import jax
import jax.numpy as jnp
import numpy as np
from jax import lax
from jax.sharding import Mesh
from jax.sharding import PartitionSpec as P

SUBSTEPS = 4
GX = ("gx_0", "gx_1")
GZ = ("gz_0", "gz_1")
GX_GY_GZ = ("gx_0", "gx_1", "gy", "gz_0", "gz_1")


root_half = 0.7071067811865476
root_three_half = 1.224744871391589
root_five_half = 1.5811388300841898
plus_values = (0.7071067811865476, 1.224744871391589, 1.5811388300841898)
minus_values = (0.7071067811865476, -1.224744871391589, 1.5811388300841898)
stiffness = ((0.0, 0.0, 0.0), (1.7320508075688772, 0.0, 0.0), (0.0, 3.872983346207417, 0.0))
courant = 0.1
theta_size = 0.3
trial_step = 0.05


def passed_along(x, axis, by):
    count = lax.axis_size(axis)
    return lax.ppermute(x, axis, [(i, (i + by) % count) for i in range(count)])


def one_axis_at_a_time(x, axes):
    for axis in axes:
        x = lax.pmax(x, axis)
    return x


def with_halo(x, sides, width):
    edges = {}
    for axis, dim in sides:
        count, length = (lax.axis_size(axis), x.shape[dim])
        up = [(i, (i + 1) % count) for i in range(count)]
        last = lax.slice_in_dim(x, length - width, length, axis=dim)
        leading = lax.slice_in_dim(x, 0, width, axis=dim)
        edges[dim] = (
            lax.ppermute(last, axis, up),
            lax.ppermute(leading, axis, [(b, a) for a, b in up]),
        )
    done = []
    for _, dim in sides:
        low, high = edges[dim]
        around = [(width, width) if d in done else (0, 0) for d in range(x.ndim)]
        x = jnp.concatenate([jnp.pad(low, around), x, jnp.pad(high, around)], axis=dim)
        done.append(dim)
    return x


def one_axis_at_a_time_2(x, axes):
    for axis in axes:
        x = lax.psum(x, axis)
    return x


def build_tables():
    points = np.array(
        [-0.8611363115940526, -0.3399810435848563, 0.3399810435848563, 0.8611363115940526]
    )
    weights = np.array(
        [0.3478548451374538, 0.6521451548625461, 0.6521451548625461, 0.3478548451374538]
    )
    points = 0.5 * (points + 1.0)
    weights = 0.5 * weights
    node_points = np.array([0.0, 1.0 / 3.0, 2.0 / 3.0, 1.0])
    value_table = np.zeros((4, 4))
    slope_table = np.zeros((4, 4))
    for column in range(4):
        others = [node_points[member] for member in range(4) if member != column]
        denominator = np.prod([node_points[column] - member for member in others])
        for quad_row in range(4):
            gauss_point = points[quad_row]
            value_table[quad_row, column] = (
                np.prod([gauss_point - member for member in others]) / denominator
            )
            slope_table[quad_row, column] = (
                sum(
                    (
                        np.prod(
                            [
                                gauss_point - others[position]
                                for position in range(3)
                                if position != skipped
                            ]
                        )
                        for skipped in range(3)
                    )
                )
                / denominator
            )
    centred = 2.0 * points - 1.0
    legendre_table = np.stack(
        [
            np.full(4, root_half),
            root_three_half * centred,
            root_five_half * 0.5 * (3.0 * centred**2 - 1.0),
        ],
        axis=1,
    )
    cube_table = (weights[:, None, None] * weights[None, :, None] * weights[None, None, :]).reshape(
        4, 4, 4, 1, 1, 1
    )
    return (value_table, slope_table, legendre_table, cube_table)


def as_table(operand):
    return jnp.asarray(np.asarray(operand), jnp.float32)


def contract(weights_table, operand, along):
    product = jnp.tensordot(
        as_table(weights_table), operand, axes=([1], [along]), precision=lax.Precision.HIGHEST
    )
    return jnp.moveaxis(product, 0, along)


def trace_along(modal_coefficients, vector, direction):
    return jnp.tensordot(
        as_table(vector),
        modal_coefficients,
        axes=([0], [direction]),
        precision=lax.Precision.HIGHEST,
    )


def spread_shape(vector, direction):
    broadcast_shape = [1] * 6
    broadcast_shape[direction] = 3
    return as_table(vector).reshape(broadcast_shape)


def boundary_terms(modal_coefficients, local_speed, right_ext, left_ext, speed_ext, direction):
    extent = modal_coefficients.shape[3 + direction]
    face_speed = 0.5 * (
        lax.slice_in_dim(speed_ext, 0, extent + 1, axis=direction)
        + lax.slice_in_dim(speed_ext, 1, extent + 2, axis=direction)
    )
    flux = (
        jnp.maximum(face_speed, 0.0)[None, None] * right_ext
        + jnp.minimum(face_speed, 0.0)[None, None] * left_ext
    )
    flux_left = lax.slice_in_dim(flux, 0, extent, axis=2 + direction)
    flux_right = lax.slice_in_dim(flux, 1, extent + 1, axis=2 + direction)
    lifted = contract(stiffness, modal_coefficients, direction)
    faces = spread_shape(plus_values, direction) * jnp.expand_dims(
        flux_right, direction
    ) - spread_shape(minus_values, direction) * jnp.expand_dims(flux_left, direction)
    return local_speed[None, None, None] * lifted - faces


def element_energy(corners, modal_coefficients):
    lagrange_values, lagrange_slopes, legendre_values, cube_weights = build_tables()
    along_value = contract(lagrange_values, corners, 1)
    along_slope = contract(lagrange_slopes, corners, 1)
    value_value = contract(lagrange_values, along_value, 2)
    jac_first = contract(lagrange_values, contract(lagrange_values, along_slope, 2), 3)
    jac_second = contract(lagrange_values, contract(lagrange_slopes, along_value, 2), 3)
    jac_third = contract(lagrange_slopes, value_value, 3)
    columns = (jac_first, jac_second, jac_third)
    sample = contract(
        legendre_values,
        contract(legendre_values, contract(legendre_values, modal_coefficients, 0), 1),
        2,
    )
    target_size = jnp.exp(theta_size * sample)
    inverse = 1.0 / target_size
    mapped = [
        [
            ((1.0 if component == column else 0.0) + columns[column][component]) * inverse
            for column in range(3)
        ]
        for component in range(3)
    ]
    metric = jnp.zeros_like(sample)
    for first_column in range(3):
        for second_column in range(3):
            gram_entry = (
                mapped[0][first_column] * mapped[0][second_column]
                + mapped[1][first_column] * mapped[1][second_column]
                + mapped[2][first_column] * mapped[2][second_column]
            )
            deviation = gram_entry - (1.0 if first_column == second_column else 0.0)
            metric = metric + deviation * deviation
    return jnp.sum(as_table(cube_weights) * target_size**3 * metric)


def element_corners(padded):
    gathered = padded
    for along, stack_axis in ((1, 1), (3, 2), (5, 3)):
        extent = (gathered.shape[along] - 1) // 3
        gathered = jnp.stack(
            [
                lax.slice_in_dim(
                    gathered, node_offset, node_offset + 3 * extent - 2, stride=3, axis=along
                )
                for node_offset in range(4)
            ],
            axis=stack_axis,
        )
    return gathered


def pad_one(operand, node_offset, along):
    config = [(0, 0, 0)] * operand.ndim
    config[along] = (node_offset, 3 - node_offset, 2)
    return lax.pad(operand, jnp.zeros((), operand.dtype), config)


def spread_corners(corner_grad):
    spread = corner_grad
    for stack_axis, along in ((3, 5), (2, 3), (1, 1)):
        pieces = [
            pad_one(
                lax.index_in_dim(spread, node_offset, axis=stack_axis, keepdims=False),
                node_offset,
                along,
            )
            for node_offset in range(4)
        ]
        spread = pieces[0] + pieces[1] + pieces[2] + pieces[3]
    return spread


def keep_rim(operand, direction, first_axis):
    for other_axis in range(3):
        if other_axis != direction:
            along = first_axis + other_axis
            operand = lax.slice_in_dim(operand, 1, operand.shape[along] - 1, axis=along)
    return operand


def trace_pair(modal_coefficients, direction):
    element_axis = 2 + direction
    extent = modal_coefficients.shape[3 + direction]
    right_trace = trace_along(modal_coefficients, plus_values, direction)
    left_trace = trace_along(modal_coefficients, minus_values, direction)
    last_right = lax.slice_in_dim(right_trace, extent - 1, extent, axis=element_axis)
    first_left = lax.slice_in_dim(left_trace, 0, 1, axis=element_axis)
    if direction == 0:
        from_low = passed_along(last_right, GX, 1)
        from_high = passed_along(first_left, GX, -1)
    elif direction == 1:
        from_low = passed_along(last_right, "gy", 1)
        from_high = passed_along(first_left, "gy", -1)
    else:
        from_low = passed_along(last_right, GZ, 1)
        from_high = passed_along(first_left, GZ, -1)
    right_ext = jnp.concatenate([from_low, right_trace], axis=element_axis)
    left_ext = jnp.concatenate([left_trace, from_high], axis=element_axis)
    return (right_ext, left_ext)


def upper_rim(nodal):
    received = passed_along(lax.slice_in_dim(nodal, 0, 1, axis=1), GX, -1)
    nodal = jnp.concatenate([nodal, received], axis=1)
    received = passed_along(lax.slice_in_dim(nodal, 0, 1, axis=2), "gy", -1)
    nodal = jnp.concatenate([nodal, received], axis=2)
    received = passed_along(lax.slice_in_dim(nodal, 0, 1, axis=3), GZ, -1)
    return jnp.concatenate([nodal, received], axis=3)


def on_device(displacement, size_field_modes, velocity):
    extent_x = size_field_modes.shape[1]
    extent_y = size_field_modes.shape[2]
    extent_z = size_field_modes.shape[3]
    modal_coefficients = size_field_modes.reshape(3, 3, 3, extent_x, extent_y, extent_z)
    fastest = one_axis_at_a_time(jnp.max(jnp.sum(jnp.abs(velocity), axis=0)), GX_GY_GZ)
    time_step = courant / jnp.maximum(fastest, 0.25)
    speed_rim = with_halo(velocity, ((GX, 1), ("gy", 2), (GZ, 3)), 1)
    speed_ext = [keep_rim(speed_rim[direction], direction, 0) for direction in range(3)]

    def advection_rate(current_field):
        pairs = [trace_pair(current_field, direction) for direction in range(3)]
        accumulated = jnp.zeros_like(current_field)
        for direction in range(3):
            accumulated = accumulated + boundary_terms(
                current_field,
                velocity[direction],
                pairs[direction][0],
                pairs[direction][1],
                speed_ext[direction],
                direction,
            )
        return 2.0 * accumulated

    for substep in range(SUBSTEPS):
        midway = modal_coefficients + time_step * advection_rate(modal_coefficients)
        modal_coefficients = 0.5 * modal_coefficients + 0.5 * (
            midway + time_step * advection_rate(midway)
        )
    widened_nodes = upper_rim(displacement)
    energy_local, corner_grad = jax.value_and_grad(element_energy)(
        element_corners(widened_nodes), modal_coefficients
    )
    elements = float(
        extent_x * extent_y * extent_z * lax.axis_size(GX) * lax.axis_size("gy") * lax.axis_size(GZ)
    )
    entries = 81.0 * elements
    energy_total = one_axis_at_a_time_2(energy_local, GX_GY_GZ)
    assembled = spread_corners(corner_grad)
    limit_x = assembled.shape[1] - 1
    received = passed_along(lax.slice_in_dim(assembled, limit_x, limit_x + 1, axis=1), GX, 1)
    assembled = jnp.concatenate(
        [
            lax.slice_in_dim(assembled, 0, 1, axis=1) + received,
            lax.slice_in_dim(assembled, 1, limit_x, axis=1),
        ],
        axis=1,
    )
    limit_y = assembled.shape[2] - 1
    received = passed_along(lax.slice_in_dim(assembled, limit_y, limit_y + 1, axis=2), "gy", 1)
    assembled = jnp.concatenate(
        [
            lax.slice_in_dim(assembled, 0, 1, axis=2) + received,
            lax.slice_in_dim(assembled, 1, limit_y, axis=2),
        ],
        axis=2,
    )
    limit_z = assembled.shape[3] - 1
    received = passed_along(lax.slice_in_dim(assembled, limit_z, limit_z + 1, axis=3), GZ, 1)
    gradient = jnp.concatenate(
        [
            lax.slice_in_dim(assembled, 0, 1, axis=3) + received,
            lax.slice_in_dim(assembled, 1, limit_z, axis=3),
        ],
        axis=3,
    )
    square_local = jnp.sum(gradient * gradient)
    square_total = one_axis_at_a_time_2(square_local, GX_GY_GZ)
    step_length = trial_step / jnp.sqrt(1.0 + square_total / entries)
    widened_trial = upper_rim(displacement - step_length * gradient)
    trial_local = element_energy(element_corners(widened_trial), modal_coefficients)
    trial_total = one_axis_at_a_time_2(trial_local, GX_GY_GZ)
    checks = jnp.stack([energy_total / elements, square_total / entries, trial_total / elements])
    return (modal_coefficients.reshape(27, extent_x, extent_y, extent_z), gradient, checks)


def solution(mesh):
    finer = Mesh(
        mesh.devices.reshape(4, 2, mesh.shape["gy"], 4, 2), ("gx_0", "gx_1", "gy", "gz_0", "gz_1")
    )
    return jax.shard_map(
        on_device,
        mesh=finer,
        in_specs=(P(None, GX, "gy", GZ), P(None, GX, "gy", GZ), P(None, GX, "gy", GZ)),
        out_specs=(P(None, GX, "gy", GZ), P(None, GX, "gy", GZ), P()),
        check_vma=False,
    )
```

profile of v0, /device:TPU:1, one launch (start us, length us, event | category | flops | bytes accessed | tf_op | source)
XLA Modules:
  0.0 456.1 jit_solution(2346756452224678851)
XLA Ops:
  8.1 5.8 %collective-permute-start = (f32[3,2,2,1]{3,2,1,0:T(2,128)S(1)}, f32[3,2,2,1]{3,2,1,0:T(2,128)S(1)}, u32[]{:S(2)}, u32[]{:S(2)}) collective-permute-start(f32[3,2,2,1]{3,2,1,0:T(2,128)S(1)} %get-tuple-element.128), channel_id=1, source_target_pairs={{0,1},{1,2},{2,3},{3,4},{4,5},{5,6},{6,7},{7,0},{8,9},{9,10},{10,1... | collective-permute-start | bytes 152 | tf_op jit(solution)/shard_map/ppermute | solution.py:44
  17.6 9.8 %pmax.35 = f32[]{:T(128)} all-reduce(f32[]{:T(128)} %reduce_max.9), channel_id=1, replica_groups=mesh['gx_0'=4,'gx_1'=2,'gy'=4,'gz_0'=4,'gz_1'=2] {'gx_0'}, use_global_device_ids=true, to_apply=%region_2.0 | all-reduce | flops 1 | bytes 8 | tf_op jit(solution)/shard_map/pmax | solution.py:32
  27.6 5.3 %pmax.36 = f32[]{:T(128)} all-reduce(f32[]{:T(128)} %pmax.35), channel_id=1, replica_groups=mesh['gx_0'=4,'gx_1'=2,'gy'=4,'gz_0'=4,'gz_1'=2] {'gx_1'}, use_global_device_ids=true, to_apply=%region_3.0 | all-reduce | flops 1 | bytes 8 | tf_op jit(solution)/shard_map/pmax | solution.py:32
  33.2 7.9 %pmax.37 = f32[]{:T(128)} all-reduce(f32[]{:T(128)} %pmax.36), channel_id=1, replica_groups=mesh['gx_0'=4,'gx_1'=2,'gy'=4,'gz_0'=4,'gz_1'=2] {'gy'}, use_global_device_ids=true, to_apply=%region_4.0 | all-reduce | flops 1 | bytes 8 | tf_op jit(solution)/shard_map/pmax | solution.py:32
  41.1 9.3 %pmax.38 = f32[]{:T(128)} all-reduce(f32[]{:T(128)} %pmax.37), channel_id=1, replica_groups=mesh['gx_0'=4,'gx_1'=2,'gy'=4,'gz_0'=4,'gz_1'=2] {'gz_0'}, use_global_device_ids=true, to_apply=%region_5.0 | all-reduce | flops 1 | bytes 8 | tf_op jit(solution)/shard_map/pmax | solution.py:32
  50.5 8.3 %pmax.39 = f32[]{:T(128)} all-reduce(f32[]{:T(128)} %pmax.38), channel_id=1, replica_groups=mesh['gx_0'=4,'gx_1'=2,'gy'=4,'gz_0'=4,'gz_1'=2] {'gz_1'}, use_global_device_ids=true, to_apply=%region_6.0 | all-reduce | flops 1 | bytes 8 | tf_op jit(solution)/shard_map/pmax | solution.py:32
  60.6 5.5 %collective-permute-done.5 = f32[3,2,2,1]{3,2,1,0:T(2,128)S(1)} collective-permute-done((f32[3,2,2,1]{3,2,1,0:T(2,128)S(1)}, f32[3,2,2,1]{3,2,1,0:T(2,128)S(1)}, u32[]{:S(2)}, u32[]{:S(2)}) %collective-permute-start.5) | collective-permute-done | bytes 80 | tf_op jit(solution)/shard_map/ppermute | solution.py:45
  66.2 6.7 %collective-permute-start.7 = (f32[3,3,1,2,128]{4,3,2,1,0:T(2,128)S(1)}, f32[3,3,1,2,128]{4,3,2,1,0:T(2,128)S(1)}, u32[]{:S(2)}, u32[]{:S(2)}) collective-permute-start(f32[3,3,1,2,128]{4,3,2,1,0:T(2,128)S(1)} %slice.822), channel_id=1, source_target_pairs={{0,224},{32,0},{64,32},{96,64},{128,96},{160,128},{192,160},{224,1... | collective-permute-start | bytes 27656 | tf_op jit(solution)/shard_map/ppermute | solution.py:27
  75.3 6.7 %collective-permute-start.11 = (f32[3,3,2,2,1]{4,0,3,2,1:T(4,128)S(1)}, f32[3,3,2,2,1]{4,0,3,2,1:T(4,128)S(1)}, u32[]{:S(2)}, u32[]{:S(2)}) collective-permute-start(f32[3,3,2,2,1]{4,0,3,2,1:T(4,128)S(1)} %bitcast.1062), channel_id=1, source_target_pairs={{0,7},{1,0},{2,1},{3,2},{4,3},{5,4},{6,5},{7,6},{8,15},{9,8},{10,9... | collective-permute-start | bytes 440 | tf_op jit(solution)/shard_map/ppermute | solution.py:27
  94.4 7.5 %collective-permute-start.17 = (f32[3,3,2,2,1]{4,0,3,2,1:T(4,128)S(1)}, f32[3,3,2,2,1]{4,0,3,2,1:T(4,128)S(1)}, u32[]{:S(2)}, u32[]{:S(2)}) collective-permute-start(f32[3,3,2,2,1]{4,0,3,2,1:T(4,128)S(1)} %bitcast.1068), channel_id=1, source_target_pairs={{0,7},{1,0},{2,1},{3,2},{4,3},{5,4},{6,5},{7,6},{8,15},{9,8},{10,9... | collective-permute-start | bytes 440 | tf_op jit(solution)/shard_map/ppermute | solution.py:27
  114.5 5.9 %collective-permute-start.23 = (f32[3,3,2,2,1]{4,0,3,2,1:T(4,128)S(1)}, f32[3,3,2,2,1]{4,0,3,2,1:T(4,128)S(1)}, u32[]{:S(2)}, u32[]{:S(2)}) collective-permute-start(f32[3,3,2,2,1]{4,0,3,2,1:T(4,128)S(1)} %bitcast.1074), channel_id=1, source_target_pairs={{0,7},{1,0},{2,1},{3,2},{4,3},{5,4},{6,5},{7,6},{8,15},{9,8},{10,9... | collective-permute-start | bytes 440 | tf_op jit(solution)/shard_map/ppermute | solution.py:27
  121.5 8.7 %collective-permute-start.21 = (f32[3,3,2,1,128]{4,0,3,2,1:T(4,128)S(1)}, f32[3,3,2,1,128]{4,0,3,2,1:T(4,128)S(1)}, u32[]{:S(2)}, u32[]{:S(2)}) collective-permute-start(f32[3,3,2,1,128]{4,0,3,2,1:T(4,128)S(1)} %slice.856), channel_id=1, source_target_pairs={{0,24},{8,0},{16,8},{24,16},{1,25},{9,1},{17,9},{25,17},{2,26},{10... | collective-permute-start | bytes 27656 | tf_op jit(solution)/shard_map/ppermute | solution.py:27
  139.8 7.5 %collective-permute-start.29 = (f32[3,3,2,2,1]{4,0,3,2,1:T(4,128)S(1)}, f32[3,3,2,2,1]{4,0,3,2,1:T(4,128)S(1)}, u32[]{:S(2)}, u32[]{:S(2)}) collective-permute-start(f32[3,3,2,2,1]{4,0,3,2,1:T(4,128)S(1)} %bitcast.1064), channel_id=1, source_target_pairs={{0,7},{1,0},{2,1},{3,2},{4,3},{5,4},{6,5},{7,6},{8,15},{9,8},{10,9... | collective-permute-start | bytes 440 | tf_op jit(solution)/shard_map/ppermute | solution.py:27
  158.7 7.5 %collective-permute-start.35 = (f32[3,3,2,2,1]{4,0,3,2,1:T(4,128)S(1)}, f32[3,3,2,2,1]{4,0,3,2,1:T(4,128)S(1)}, u32[]{:S(2)}, u32[]{:S(2)}) collective-permute-start(f32[3,3,2,2,1]{4,0,3,2,1:T(4,128)S(1)} %bitcast.1070), channel_id=1, source_target_pairs={{0,7},{1,0},{2,1},{3,2},{4,3},{5,4},{6,5},{7,6},{8,15},{9,8},{10,9... | collective-permute-start | bytes 440 | tf_op jit(solution)/shard_map/ppermute | solution.py:27
  177.9 6.8 %collective-permute-start.41 = (f32[3,3,2,2,1]{4,0,3,2,1:T(4,128)S(1)}, f32[3,3,2,2,1]{4,0,3,2,1:T(4,128)S(1)}, u32[]{:S(2)}, u32[]{:S(2)}) collective-permute-start(f32[3,3,2,2,1]{4,0,3,2,1:T(4,128)S(1)} %bitcast.1072), channel_id=1, source_target_pairs={{0,7},{1,0},{2,1},{3,2},{4,3},{5,4},{6,5},{7,6},{8,15},{9,8},{10,9... | collective-permute-start | bytes 440 | tf_op jit(solution)/shard_map/ppermute | solution.py:27
  192.2 3.5 collective-permute-start.43
  197.8 5.8 %collective-permute-start.47 = (f32[3,3,2,2,1]{4,0,3,2,1:T(4,128)S(1)}, f32[3,3,2,2,1]{4,0,3,2,1:T(4,128)S(1)}, u32[]{:S(2)}, u32[]{:S(2)}) collective-permute-start(f32[3,3,2,2,1]{4,0,3,2,1:T(4,128)S(1)} %bitcast.1076), channel_id=1, source_target_pairs={{0,7},{1,0},{2,1},{3,2},{4,3},{5,4},{6,5},{7,6},{8,15},{9,8},{10,9... | collective-permute-start | bytes 440 | tf_op jit(solution)/shard_map/ppermute | solution.py:27
  206.4 6.3 %collective-permute-start.56 = (f32[3,7,7,1]{3,2,1,0:T(8,128)S(1)}, f32[3,7,7,1]{3,2,1,0:T(8,128)S(1)}, u32[]{:S(2)}, u32[]{:S(2)}) collective-permute-start(f32[3,7,7,1]{3,2,1,0:T(8,128)S(1)} %pad_maximum_fusion.11), channel_id=1, source_target_pairs={{0,7},{1,0},{2,1},{3,2},{4,3},{5,4},{6,5},{7,6},{8,15},{9,8},{10,9... | collective-permute-start | bytes 1772 | tf_op jit(solution)/shard_map/ppermute | solution.py:27
  215.8 3.9 slice.763
  219.7 3.9 slice.762
  223.5 3.9 slice.761
  227.4 3.9 slice.760
  242.0 3.0 collective-permute-start.49
  247.6 4.0 collective-permute-start.52
  251.6 4.2 collective-permute-start.53
  272.5 8.1 %pad.91 = f32[3,4,4,2,2,385]{5,1,4,3,2,0:T(4,128)S(1)} pad(f32[3,4,4,2,2,128]{5,1,4,3,2,0:T(4,128)S(1)} %get-tuple-element.47, f32[]{:T(128)} %constant.19.clone.1), padding=0_0_0x0_0_0x0_0_0x0_0_0x0_0_0x1_2_2 | pad | bytes 393988 | tf_op jit(solution)/shard_map/pad | solution.py:212
  280.6 7.8 %pad.90 = f32[3,4,4,2,2,385]{5,1,4,3,2,0:T(4,128)S(1)} pad(f32[3,4,4,2,2,128]{5,1,4,3,2,0:T(4,128)S(1)} %get-tuple-element.48, f32[]{:T(128)} %constant.19.clone.1), padding=0_0_0x0_0_0x0_0_0x0_0_0x0_0_0x0_3_2 | pad | bytes 393988 | tf_op jit(solution)/shard_map/pad | solution.py:212
  288.4 7.7 %pad.93 = f32[3,4,4,2,2,385]{5,1,4,3,2,0:T(4,128)S(1)} pad(f32[3,4,4,2,2,128]{5,1,4,3,2,0:T(4,128)S(1)} %get-tuple-element.49, f32[]{:T(128)} %constant.19.clone.1), padding=0_0_0x0_0_0x0_0_0x0_0_0x0_0_0x3_0_2 | pad | bytes 393988 | tf_op jit(solution)/shard_map/pad | solution.py:212
  296.2 7.8 %pad.92 = f32[3,4,4,2,2,385]{5,1,4,3,2,0:T(4,128)S(1)} pad(f32[3,4,4,2,2,128]{5,1,4,3,2,0:T(4,128)S(1)} %get-tuple-element.50, f32[]{:T(128)} %constant.19.clone.1), padding=0_0_0x0_0_0x0_0_0x0_0_0x0_0_0x2_1_2 | pad | bytes 393988 | tf_op jit(solution)/shard_map/pad | solution.py:212
  310.6 4.1 collective-permute-done.58
  317.9 6.3 %collective-permute-done.59 = f32[3,6,6,1]{3,1,2,0:T(8,128)S(1)} collective-permute-done((f32[3,6,6,1]{3,1,2,0:T(8,128)S(1)}, f32[3,6,6,1]{3,1,2,0:T(8,128)S(1)}, u32[]{:S(2)}, u32[]{:S(2)}) %collective-permute-start.59) | collective-permute-done | bytes 464 | tf_op jit(solution)/shard_map/ppermute | solution.py:27
  324.9 11.6 %psum.110 = f32[]{:T(128)} all-reduce(f32[]{:T(128)} %get-tuple-element.21), channel_id=1, replica_groups=mesh['gx_0'=4,'gx_1'=2,'gy'=4,'gz_0'=4,'gz_1'=2] {'gx_0'}, use_global_device_ids=true, to_apply=%region_14.15 | all-reduce | flops 1 | bytes 8 | tf_op jit(solution)/shard_map/psum | solution.py:58
  336.5 6.9 %psum.111 = f32[]{:T(128)} all-reduce(f32[]{:T(128)} %psum.110), channel_id=1, replica_groups=mesh['gx_0'=4,'gx_1'=2,'gy'=4,'gz_0'=4,'gz_1'=2] {'gx_1'}, use_global_device_ids=true, to_apply=%region_15.16 | all-reduce | flops 1 | bytes 8 | tf_op jit(solution)/shard_map/psum | solution.py:58
  343.4 6.7 %psum.112 = f32[]{:T(128)} all-reduce(f32[]{:T(128)} %psum.111), channel_id=1, replica_groups=mesh['gx_0'=4,'gx_1'=2,'gy'=4,'gz_0'=4,'gz_1'=2] {'gy'}, use_global_device_ids=true, to_apply=%region_16.17 | all-reduce | flops 1 | bytes 8 | tf_op jit(solution)/shard_map/psum | solution.py:58
  350.1 9.3 %psum.113 = f32[]{:T(128)} all-reduce(f32[]{:T(128)} %psum.112), channel_id=1, replica_groups=mesh['gx_0'=4,'gx_1'=2,'gy'=4,'gz_0'=4,'gz_1'=2] {'gz_0'}, use_global_device_ids=true, to_apply=%region_17.18 | all-reduce | flops 1 | bytes 8 | tf_op jit(solution)/shard_map/psum | solution.py:58
  359.4 8.3 %psum.114 = f32[]{:T(128)} all-reduce(f32[]{:T(128)} %psum.113), channel_id=1, replica_groups=mesh['gx_0'=4,'gx_1'=2,'gy'=4,'gz_0'=4,'gz_1'=2] {'gz_1'}, use_global_device_ids=true, to_apply=%region_18.19 | all-reduce | flops 1 | bytes 8 | tf_op jit(solution)/shard_map/psum | solution.py:58
  368.5 5.2 %collective-permute-start.60 = (f32[3,1,6,384]{3,1,2,0:T(1,128)S(1)}, f32[3,1,6,384]{3,1,2,0:T(1,128)S(1)}, u32[]{:S(2)}, u32[]{:S(2)}) collective-permute-start(f32[3,1,6,384]{3,1,2,0:T(1,128)S(1)} %slice.951), channel_id=1, source_target_pairs={{0,224},{32,0},{64,32},{96,64},{128,96},{160,128},{192,160},{224,1... | collective-permute-start | bytes 82952 | tf_op jit(solution)/shard_map/ppermute | solution.py:27
  373.7 3.1 collective-permute-done.60
  383.1 6.3 %collective-permute-done.62 = f32[3,7,7,1]{3,1,2,0:T(8,128)S(1)} collective-permute-done((f32[3,7,7,1]{3,1,2,0:T(8,128)S(1)}, f32[3,7,7,1]{3,1,2,0:T(8,128)S(1)}, u32[]{:S(2)}, u32[]{:S(2)}) %collective-permute-start.62) | collective-permute-done | bytes 620 | tf_op jit(solution)/shard_map/ppermute | solution.py:27
  391.4 3.9 slice.808
  395.3 3.9 slice.807
  399.1 3.9 slice.806
  403.0 3.9 slice.805
  415.5 8.2 %all-reduce.27 = (f32[]{:T(128)}, f32[]{:T(128)}) all-reduce(f32[]{:T(128)} %get-tuple-element.10, f32[]{:T(128)} %get-tuple-element.9), channel_id=1, replica_groups=mesh['gx_0'=4,'gx_1'=2,'gy'=4,'gz_0'=4,'gz_1'=2] {'gx_0'}, use_global_device_ids=true, to_apply=%region_20.21 | all-reduce | flops 2 | bytes 16 | tf_op jit(solution)/shard_map/psum | solution.py:58
  423.7 5.8 %all-reduce.29 = (f32[]{:T(128)}, f32[]{:T(128)}) all-reduce(f32[]{:T(128)} %get-tuple-element.15, f32[]{:T(128)} %get-tuple-element.16), channel_id=1, replica_groups=mesh['gx_0'=4,'gx_1'=2,'gy'=4,'gz_0'=4,'gz_1'=2] {'gx_1'}, use_global_device_ids=true, to_apply=%region_21.22 | all-reduce | flops 2 | bytes 16 | tf_op jit(solution)/shard_map/psum | solution.py:58
  429.5 9.5 %all-reduce.26 = (f32[]{:T(128)}, f32[]{:T(128)}) all-reduce(f32[]{:T(128)} %get-tuple-element.19, f32[]{:T(128)} %get-tuple-element.20), channel_id=1, replica_groups=mesh['gx_0'=4,'gx_1'=2,'gy'=4,'gz_0'=4,'gz_1'=2] {'gy'}, use_global_device_ids=true, to_apply=%region_22.23 | all-reduce | flops 2 | bytes 16 | tf_op jit(solution)/shard_map/psum | solution.py:58
  439.0 6.6 %all-reduce.25 = (f32[]{:T(128)}, f32[]{:T(128)}) all-reduce(f32[]{:T(128)} %get-tuple-element.13, f32[]{:T(128)} %get-tuple-element.14), channel_id=1, replica_groups=mesh['gx_0'=4,'gx_1'=2,'gy'=4,'gz_0'=4,'gz_1'=2] {'gz_0'}, use_global_device_ids=true, to_apply=%region_23.24 | all-reduce | flops 2 | bytes 16 | tf_op jit(solution)/shard_map/psum | solution.py:58
  445.6 8.4 %all-reduce.28 = (f32[]{:T(128)}, f32[]{:T(128)}) all-reduce(f32[]{:T(128)} %get-tuple-element.11, f32[]{:T(128)} %get-tuple-element.12), channel_id=1, replica_groups=mesh['gx_0'=4,'gx_1'=2,'gy'=4,'gz_0'=4,'gz_1'=2] {'gz_1'}, use_global_device_ids=true, to_apply=%region_24.25 | all-reduce | flops 2 | bytes 16 | tf_op jit(solution)/shard_map/psum | solution.py:58
  (424 shorter events, 145.4 us)
Async XLA Ops:
  1.4 71.4 %collective-permute-start.1 = (f32[3,2,1,128]{3,2,1,0:T(1,128)S(1)}, f32[3,2,1,128]{3,2,1,0:T(1,128)S(1)}, u32[]{:S(2)}, u32[]{:S(2)}) collective-permute-start(f32[3,2,1,128]{3,2,1,0:T(1,128)S(1)} %get-tuple-element.130), channel_id=1, source_target_pairs={{0,8},{8,16},{16,24},{24,0},{1,9},{9,17},{17,25},{25,1},{2,10},{10... | collective-permute-start | bytes 9224 | tf_op jit(solution)/shard_map/ppermute | solution.py:44
  3.5 70.8 %collective-permute-start.4 = (f32[3,2,1,128]{3,2,1,0:T(1,128)S(1)}, f32[3,2,1,128]{3,2,1,0:T(1,128)S(1)}, u32[]{:S(2)}, u32[]{:S(2)}) collective-permute-start(f32[3,2,1,128]{3,2,1,0:T(1,128)S(1)} %get-tuple-element.131), channel_id=1, source_target_pairs={{8,0},{16,8},{24,16},{0,24},{9,1},{17,9},{25,17},{1,25},{10,2},{18... | collective-permute-start | bytes 9224 | tf_op jit(solution)/shard_map/ppermute | solution.py:45
  4.9 69.6 %collective-permute-start.2 = (f32[3,1,2,128]{3,2,1,0:T(2,128)S(1)}, f32[3,1,2,128]{3,2,1,0:T(2,128)S(1)}, u32[]{:S(2)}, u32[]{:S(2)}) collective-permute-start(f32[3,1,2,128]{3,2,1,0:T(2,128)S(1)} %get-tuple-element.126), channel_id=1, source_target_pairs={{0,32},{32,64},{64,96},{96,128},{128,160},{160,192},{192,224},{224... | collective-permute-start | bytes 9224 | tf_op jit(solution)/shard_map/ppermute | solution.py:44
  7.8 67.5 %collective-permute-start.3 = (f32[3,1,2,128]{3,2,1,0:T(2,128)S(1)}, f32[3,1,2,128]{3,2,1,0:T(2,128)S(1)}, u32[]{:S(2)}, u32[]{:S(2)}) collective-permute-start(f32[3,1,2,128]{3,2,1,0:T(2,128)S(1)} %get-tuple-element.127), channel_id=1, source_target_pairs={{32,0},{64,32},{96,64},{128,96},{160,128},{192,160},{224,192},{0,2... | collective-permute-start | bytes 9224 | tf_op jit(solution)/shard_map/ppermute | solution.py:45
  8.1 51.6 %collective-permute-start = (f32[3,2,2,1]{3,2,1,0:T(2,128)S(1)}, f32[3,2,2,1]{3,2,1,0:T(2,128)S(1)}, u32[]{:S(2)}, u32[]{:S(2)}) collective-permute-start(f32[3,2,2,1]{3,2,1,0:T(2,128)S(1)} %get-tuple-element.128), channel_id=1, source_target_pairs={{0,1},{1,2},{2,3},{3,4},{4,5},{5,6},{6,7},{7,0},{8,9},{9,10},{10,1... | collective-permute-start | bytes 152 | tf_op jit(solution)/shard_map/ppermute | solution.py:44
  66.2 19.6 %collective-permute-start.7 = (f32[3,3,1,2,128]{4,3,2,1,0:T(2,128)S(1)}, f32[3,3,1,2,128]{4,3,2,1,0:T(2,128)S(1)}, u32[]{:S(2)}, u32[]{:S(2)}) collective-permute-start(f32[3,3,1,2,128]{4,3,2,1,0:T(2,128)S(1)} %slice.822), channel_id=1, source_target_pairs={{0,224},{32,0},{64,32},{96,64},{128,96},{160,128},{192,160},{224,1... | collective-permute-start | bytes 27656 | tf_op jit(solution)/shard_map/ppermute | solution.py:27
  72.8 12.9 %collective-permute-start.6 = (f32[3,3,1,2,128]{4,3,2,1,0:T(2,128)S(1)}, f32[3,3,1,2,128]{4,3,2,1,0:T(2,128)S(1)}, u32[]{:S(2)}, u32[]{:S(2)}) collective-permute-start(f32[3,3,1,2,128]{4,3,2,1,0:T(2,128)S(1)} %slice.821), channel_id=1, source_target_pairs={{0,32},{32,64},{64,96},{96,128},{128,160},{160,192},{192,224},{224... | collective-permute-start | bytes 27656 | tf_op jit(solution)/shard_map/ppermute | solution.py:27
  74.3 11.5 %collective-permute-start.9 = (f32[3,3,2,1,128]{4,0,3,2,1:T(4,128)S(1)}, f32[3,3,2,1,128]{4,0,3,2,1:T(4,128)S(1)}, u32[]{:S(2)}, u32[]{:S(2)}) collective-permute-start(f32[3,3,2,1,128]{4,0,3,2,1:T(4,128)S(1)} %slice.829), channel_id=1, source_target_pairs={{0,24},{8,0},{16,8},{24,16},{1,25},{9,1},{17,9},{25,17},{2,26},{10... | collective-permute-start | bytes 27656 | tf_op jit(solution)/shard_map/ppermute | solution.py:27
  74.5 8.8 %collective-permute-start.10 = (f32[3,3,2,2,1]{4,0,3,2,1:T(4,128)S(1)}, f32[3,3,2,2,1]{4,0,3,2,1:T(4,128)S(1)}, u32[]{:S(2)}, u32[]{:S(2)}) collective-permute-start(f32[3,3,2,2,1]{4,0,3,2,1:T(4,128)S(1)} %slice.835), channel_id=1, source_target_pairs={{0,1},{1,2},{2,3},{3,4},{4,5},{5,6},{6,7},{7,0},{8,9},{9,10},{10,1... | collective-permute-start | bytes 440 | tf_op jit(solution)/shard_map/ppermute | solution.py:27
  75.3 9.3 %collective-permute-start.11 = (f32[3,3,2,2,1]{4,0,3,2,1:T(4,128)S(1)}, f32[3,3,2,2,1]{4,0,3,2,1:T(4,128)S(1)}, u32[]{:S(2)}, u32[]{:S(2)}) collective-permute-start(f32[3,3,2,2,1]{4,0,3,2,1:T(4,128)S(1)} %bitcast.1062), channel_id=1, source_target_pairs={{0,7},{1,0},{2,1},{3,2},{4,3},{5,4},{6,5},{7,6},{8,15},{9,8},{10,9... | collective-permute-start | bytes 440 | tf_op jit(solution)/shard_map/ppermute | solution.py:27
  84.6 55.2 %collective-permute-start.54 = (f32[3,1,6,384]{3,2,1,0:T(8,128)S(1)}, f32[3,1,6,384]{3,2,1,0:T(8,128)S(1)}, u32[]{:S(2)}, u32[]{:S(2)}) collective-permute-start(f32[3,1,6,384]{3,2,1,0:T(8,128)S(1)} %slice.749), channel_id=1, source_target_pairs={{0,224},{32,0},{64,32},{96,64},{128,96},{160,128},{192,160},{224,1... | collective-permute-start | bytes 82952 | tf_op jit(solution)/shard_map/ppermute | solution.py:27
  90.4 14.4 %collective-permute-start.13 = (f32[3,3,1,2,128]{4,3,2,1,0:T(2,128)S(1)}, f32[3,3,1,2,128]{4,3,2,1,0:T(2,128)S(1)}, u32[]{:S(2)}, u32[]{:S(2)}) collective-permute-start(f32[3,3,1,2,128]{4,3,2,1,0:T(2,128)S(1)} %slice.840), channel_id=1, source_target_pairs={{0,224},{32,0},{64,32},{96,64},{128,96},{160,128},{192,160},{224,1... | collective-permute-start | bytes 27656 | tf_op jit(solution)/shard_map/ppermute | solution.py:27
  92.0 12.8 %collective-permute-start.12 = (f32[3,3,1,2,128]{4,3,2,1,0:T(2,128)S(1)}, f32[3,3,1,2,128]{4,3,2,1,0:T(2,128)S(1)}, u32[]{:S(2)}, u32[]{:S(2)}) collective-permute-start(f32[3,3,1,2,128]{4,3,2,1,0:T(2,128)S(1)} %slice.839), channel_id=1, source_target_pairs={{0,32},{32,64},{64,96},{96,128},{128,160},{160,192},{192,224},{224... | collective-permute-start | bytes 27656 | tf_op jit(solution)/shard_map/ppermute | solution.py:27
  94.4 8.7 %collective-permute-start.16 = (f32[3,3,2,2,1]{4,0,3,2,1:T(4,128)S(1)}, f32[3,3,2,2,1]{4,0,3,2,1:T(4,128)S(1)}, u32[]{:S(2)}, u32[]{:S(2)}) collective-permute-start(f32[3,3,2,2,1]{4,0,3,2,1:T(4,128)S(1)} %slice.847), channel_id=1, source_target_pairs={{0,1},{1,2},{2,3},{3,4},{4,5},{5,6},{6,7},{7,0},{8,9},{9,10},{10,1... | collective-permute-start | bytes 440 | tf_op jit(solution)/shard_map/ppermute | solution.py:27
  94.4 8.7 %collective-permute-start.17 = (f32[3,3,2,2,1]{4,0,3,2,1:T(4,128)S(1)}, f32[3,3,2,2,1]{4,0,3,2,1:T(4,128)S(1)}, u32[]{:S(2)}, u32[]{:S(2)}) collective-permute-start(f32[3,3,2,2,1]{4,0,3,2,1:T(4,128)S(1)} %bitcast.1068), channel_id=1, source_target_pairs={{0,7},{1,0},{2,1},{3,2},{4,3},{5,4},{6,5},{7,6},{8,15},{9,8},{10,9... | collective-permute-start | bytes 440 | tf_op jit(solution)/shard_map/ppermute | solution.py:27
  109.5 22.4 %collective-permute-start.19 = (f32[3,3,1,2,128]{4,3,2,1,0:T(2,128)S(1)}, f32[3,3,1,2,128]{4,3,2,1,0:T(2,128)S(1)}, u32[]{:S(2)}, u32[]{:S(2)}) collective-permute-start(f32[3,3,1,2,128]{4,3,2,1,0:T(2,128)S(1)} %slice.852), channel_id=1, source_target_pairs={{0,224},{32,0},{64,32},{96,64},{128,96},{160,128},{192,160},{224,1... | collective-permute-start | bytes 27656 | tf_op jit(solution)/shard_map/ppermute | solution.py:27
  110.6 21.2 %collective-permute-start.18 = (f32[3,3,1,2,128]{4,3,2,1,0:T(2,128)S(1)}, f32[3,3,1,2,128]{4,3,2,1,0:T(2,128)S(1)}, u32[]{:S(2)}, u32[]{:S(2)}) collective-permute-start(f32[3,3,1,2,128]{4,3,2,1,0:T(2,128)S(1)} %slice.851), channel_id=1, source_target_pairs={{0,32},{32,64},{64,96},{96,128},{128,160},{160,192},{192,224},{224... | collective-permute-start | bytes 27656 | tf_op jit(solution)/shard_map/ppermute | solution.py:27
  112.6 8.9 %collective-permute-start.22 = (f32[3,3,2,2,1]{4,0,3,2,1:T(4,128)S(1)}, f32[3,3,2,2,1]{4,0,3,2,1:T(4,128)S(1)}, u32[]{:S(2)}, u32[]{:S(2)}) collective-permute-start(f32[3,3,2,2,1]{4,0,3,2,1:T(4,128)S(1)} %slice.859), channel_id=1, source_target_pairs={{0,1},{1,2},{2,3},{3,4},{4,5},{5,6},{6,7},{7,0},{8,9},{9,10},{10,1... | collective-permute-start | bytes 440 | tf_op jit(solution)/shard_map/ppermute | solution.py:27
  114.5 15.8 %collective-permute-start.23 = (f32[3,3,2,2,1]{4,0,3,2,1:T(4,128)S(1)}, f32[3,3,2,2,1]{4,0,3,2,1:T(4,128)S(1)}, u32[]{:S(2)}, u32[]{:S(2)}) collective-permute-start(f32[3,3,2,2,1]{4,0,3,2,1:T(4,128)S(1)} %bitcast.1074), channel_id=1, source_target_pairs={{0,7},{1,0},{2,1},{3,2},{4,3},{5,4},{6,5},{7,6},{8,15},{9,8},{10,9... | collective-permute-start | bytes 440 | tf_op jit(solution)/shard_map/ppermute | solution.py:27
  121.5 11.3 %collective-permute-start.21 = (f32[3,3,2,1,128]{4,0,3,2,1:T(4,128)S(1)}, f32[3,3,2,1,128]{4,0,3,2,1:T(4,128)S(1)}, u32[]{:S(2)}, u32[]{:S(2)}) collective-permute-start(f32[3,3,2,1,128]{4,0,3,2,1:T(4,128)S(1)} %slice.856), channel_id=1, source_target_pairs={{0,24},{8,0},{16,8},{24,16},{1,25},{9,1},{17,9},{25,17},{2,26},{10... | collective-permute-start | bytes 27656 | tf_op jit(solution)/shard_map/ppermute | solution.py:27
  136.7 14.6 %collective-permute-start.25 = (f32[3,3,1,2,128]{4,3,2,1,0:T(2,128)S(1)}, f32[3,3,1,2,128]{4,3,2,1,0:T(2,128)S(1)}, u32[]{:S(2)}, u32[]{:S(2)}) collective-permute-start(f32[3,3,1,2,128]{4,3,2,1,0:T(2,128)S(1)} %slice.864), channel_id=1, source_target_pairs={{0,224},{32,0},{64,32},{96,64},{128,96},{160,128},{192,160},{224,1... | collective-permute-start | bytes 27656 | tf_op jit(solution)/shard_map/ppermute | solution.py:27
  138.3 13.1 %collective-permute-start.24 = (f32[3,3,1,2,128]{4,3,2,1,0:T(2,128)S(1)}, f32[3,3,1,2,128]{4,3,2,1,0:T(2,128)S(1)}, u32[]{:S(2)}, u32[]{:S(2)}) collective-permute-start(f32[3,3,1,2,128]{4,3,2,1,0:T(2,128)S(1)} %slice.863), channel_id=1, source_target_pairs={{0,32},{32,64},{64,96},{96,128},{128,160},{160,192},{192,224},{224... | collective-permute-start | bytes 27656 | tf_op jit(solution)/shard_map/ppermute | solution.py:27
  139.5 11.9 %collective-permute-start.27 = (f32[3,3,2,1,128]{4,0,3,2,1:T(4,128)S(1)}, f32[3,3,2,1,128]{4,0,3,2,1:T(4,128)S(1)}, u32[]{:S(2)}, u32[]{:S(2)}) collective-permute-start(f32[3,3,2,1,128]{4,0,3,2,1:T(4,128)S(1)} %slice.868), channel_id=1, source_target_pairs={{0,24},{8,0},{16,8},{24,16},{1,25},{9,1},{17,9},{25,17},{2,26},{10... | collective-permute-start | bytes 27656 | tf_op jit(solution)/shard_map/ppermute | solution.py:27
  139.8 8.7 %collective-permute-start.28 = (f32[3,3,2,2,1]{4,0,3,2,1:T(4,128)S(1)}, f32[3,3,2,2,1]{4,0,3,2,1:T(4,128)S(1)}, u32[]{:S(2)}, u32[]{:S(2)}) collective-permute-start(f32[3,3,2,2,1]{4,0,3,2,1:T(4,128)S(1)} %slice.871), channel_id=1, source_target_pairs={{0,1},{1,2},{2,3},{3,4},{4,5},{5,6},{6,7},{7,0},{8,9},{9,10},{10,1... | collective-permute-start | bytes 440 | tf_op jit(solution)/shard_map/ppermute | solution.py:27
  139.8 10.0 %collective-permute-start.29 = (f32[3,3,2,2,1]{4,0,3,2,1:T(4,128)S(1)}, f32[3,3,2,2,1]{4,0,3,2,1:T(4,128)S(1)}, u32[]{:S(2)}, u32[]{:S(2)}) collective-permute-start(f32[3,3,2,2,1]{4,0,3,2,1:T(4,128)S(1)} %bitcast.1064), channel_id=1, source_target_pairs={{0,7},{1,0},{2,1},{3,2},{4,3},{5,4},{6,5},{7,6},{8,15},{9,8},{10,9... | collective-permute-start | bytes 440 | tf_op jit(solution)/shard_map/ppermute | solution.py:27
  149.8 56.5 %collective-permute-start.55 = (f32[3,7,1,384]{3,2,1,0:T(1,128)S(1)}, f32[3,7,1,384]{3,2,1,0:T(1,128)S(1)}, u32[]{:S(2)}, u32[]{:S(2)}) collective-permute-start(f32[3,7,1,384]{3,2,1,0:T(1,128)S(1)} %slice.923), channel_id=1, source_target_pairs={{0,24},{8,0},{16,8},{24,16},{1,25},{9,1},{17,9},{25,17},{2,26},{10... | collective-permute-start | bytes 96776 | tf_op jit(solution)/shard_map/ppermute | solution.py:27
  154.9 14.4 %collective-permute-start.31 = (f32[3,3,1,2,128]{4,3,2,1,0:T(2,128)S(1)}, f32[3,3,1,2,128]{4,3,2,1,0:T(2,128)S(1)}, u32[]{:S(2)}, u32[]{:S(2)}) collective-permute-start(f32[3,3,1,2,128]{4,3,2,1,0:T(2,128)S(1)} %slice.876), channel_id=1, source_target_pairs={{0,224},{32,0},{64,32},{96,64},{128,96},{160,128},{192,160},{224,1... | collective-permute-start | bytes 27656 | tf_op jit(solution)/shard_map/ppermute | solution.py:27
  157.9 11.4 %collective-permute-start.30 = (f32[3,3,1,2,128]{4,3,2,1,0:T(2,128)S(1)}, f32[3,3,1,2,128]{4,3,2,1,0:T(2,128)S(1)}, u32[]{:S(2)}, u32[]{:S(2)}) collective-permute-start(f32[3,3,1,2,128]{4,3,2,1,0:T(2,128)S(1)} %slice.875), channel_id=1, source_target_pairs={{0,32},{32,64},{64,96},{96,128},{128,160},{160,192},{192,224},{224... | collective-permute-start | bytes 27656 | tf_op jit(solution)/shard_map/ppermute | solution.py:27
  158.2 9.4 %collective-permute-start.34 = (f32[3,3,2,2,1]{4,0,3,2,1:T(4,128)S(1)}, f32[3,3,2,2,1]{4,0,3,2,1:T(4,128)S(1)}, u32[]{:S(2)}, u32[]{:S(2)}) collective-permute-start(f32[3,3,2,2,1]{4,0,3,2,1:T(4,128)S(1)} %slice.883), channel_id=1, source_target_pairs={{0,1},{1,2},{2,3},{3,4},{4,5},{5,6},{6,7},{7,0},{8,9},{9,10},{10,1... | collective-permute-start | bytes 440 | tf_op jit(solution)/shard_map/ppermute | solution.py:27
  158.7 9.0 %collective-permute-start.35 = (f32[3,3,2,2,1]{4,0,3,2,1:T(4,128)S(1)}, f32[3,3,2,2,1]{4,0,3,2,1:T(4,128)S(1)}, u32[]{:S(2)}, u32[]{:S(2)}) collective-permute-start(f32[3,3,2,2,1]{4,0,3,2,1:T(4,128)S(1)} %bitcast.1070), channel_id=1, source_target_pairs={{0,7},{1,0},{2,1},{3,2},{4,3},{5,4},{6,5},{7,6},{8,15},{9,8},{10,9... | collective-permute-start | bytes 440 | tf_op jit(solution)/shard_map/ppermute | solution.py:27
  174.1 13.4 %collective-permute-start.37 = (f32[3,3,1,2,128]{4,3,2,1,0:T(2,128)S(1)}, f32[3,3,1,2,128]{4,3,2,1,0:T(2,128)S(1)}, u32[]{:S(2)}, u32[]{:S(2)}) collective-permute-start(f32[3,3,1,2,128]{4,3,2,1,0:T(2,128)S(1)} %slice.888), channel_id=1, source_target_pairs={{0,224},{32,0},{64,32},{96,64},{128,96},{160,128},{192,160},{224,1... | collective-permute-start | bytes 27656 | tf_op jit(solution)/shard_map/ppermute | solution.py:27
  176.6 10.9 %collective-permute-start.36 = (f32[3,3,1,2,128]{4,3,2,1,0:T(2,128)S(1)}, f32[3,3,1,2,128]{4,3,2,1,0:T(2,128)S(1)}, u32[]{:S(2)}, u32[]{:S(2)}) collective-permute-start(f32[3,3,1,2,128]{4,3,2,1,0:T(2,128)S(1)} %slice.887), channel_id=1, source_target_pairs={{0,32},{32,64},{64,96},{96,128},{128,160},{160,192},{192,224},{224... | collective-permute-start | bytes 27656 | tf_op jit(solution)/shard_map/ppermute | solution.py:27
  177.1 8.7 %collective-permute-start.40 = (f32[3,3,2,2,1]{4,0,3,2,1:T(4,128)S(1)}, f32[3,3,2,2,1]{4,0,3,2,1:T(4,128)S(1)}, u32[]{:S(2)}, u32[]{:S(2)}) collective-permute-start(f32[3,3,2,2,1]{4,0,3,2,1:T(4,128)S(1)} %slice.895), channel_id=1, source_target_pairs={{0,1},{1,2},{2,3},{3,4},{4,5},{5,6},{6,7},{7,0},{8,9},{9,10},{10,1... | collective-permute-start | bytes 440 | tf_op jit(solution)/shard_map/ppermute | solution.py:27
  177.9 7.9 %collective-permute-start.41 = (f32[3,3,2,2,1]{4,0,3,2,1:T(4,128)S(1)}, f32[3,3,2,2,1]{4,0,3,2,1:T(4,128)S(1)}, u32[]{:S(2)}, u32[]{:S(2)}) collective-permute-start(f32[3,3,2,2,1]{4,0,3,2,1:T(4,128)S(1)} %bitcast.1072), channel_id=1, source_target_pairs={{0,7},{1,0},{2,1},{3,2},{4,3},{5,4},{6,5},{7,6},{8,15},{9,8},{10,9... | collective-permute-start | bytes 440 | tf_op jit(solution)/shard_map/ppermute | solution.py:27
  192.2 47.1 %collective-permute-start.43 = (f32[3,3,1,2,128]{4,3,2,1,0:T(2,128)S(1)}, f32[3,3,1,2,128]{4,3,2,1,0:T(2,128)S(1)}, u32[]{:S(2)}, u32[]{:S(2)}) collective-permute-start(f32[3,3,1,2,128]{4,3,2,1,0:T(2,128)S(1)} %slice.900), channel_id=1, source_target_pairs={{0,224},{32,0},{64,32},{96,64},{128,96},{160,128},{192,160},{224,1... | collective-permute-start | bytes 27656 | tf_op jit(solution)/shard_map/ppermute | solution.py:27
  195.7 43.6 %collective-permute-start.42 = (f32[3,3,1,2,128]{4,3,2,1,0:T(2,128)S(1)}, f32[3,3,1,2,128]{4,3,2,1,0:T(2,128)S(1)}, u32[]{:S(2)}, u32[]{:S(2)}) collective-permute-start(f32[3,3,1,2,128]{4,3,2,1,0:T(2,128)S(1)} %slice.899), channel_id=1, source_target_pairs={{0,32},{32,64},{64,96},{96,128},{128,160},{160,192},{192,224},{224... | collective-permute-start | bytes 27656 | tf_op jit(solution)/shard_map/ppermute | solution.py:27
  196.0 8.7 %collective-permute-start.46 = (f32[3,3,2,2,1]{4,0,3,2,1:T(4,128)S(1)}, f32[3,3,2,2,1]{4,0,3,2,1:T(4,128)S(1)}, u32[]{:S(2)}, u32[]{:S(2)}) collective-permute-start(f32[3,3,2,2,1]{4,0,3,2,1:T(4,128)S(1)} %slice.907), channel_id=1, source_target_pairs={{0,1},{1,2},{2,3},{3,4},{4,5},{5,6},{6,7},{7,0},{8,9},{9,10},{10,1... | collective-permute-start | bytes 440 | tf_op jit(solution)/shard_map/ppermute | solution.py:27
  204.8 34.6 %collective-permute-start.45 = (f32[3,3,2,1,128]{4,0,3,2,1:T(4,128)S(1)}, f32[3,3,2,1,128]{4,0,3,2,1:T(4,128)S(1)}, u32[]{:S(2)}, u32[]{:S(2)}) collective-permute-start(f32[3,3,2,1,128]{4,0,3,2,1:T(4,128)S(1)} %slice.904), channel_id=1, source_target_pairs={{0,24},{8,0},{16,8},{24,16},{1,25},{9,1},{17,9},{25,17},{2,26},{10... | collective-permute-start | bytes 27656 | tf_op jit(solution)/shard_map/ppermute | solution.py:27
  204.8 34.6 %collective-permute-start.44 = (f32[3,3,2,1,128]{4,0,3,2,1:T(4,128)S(1)}, f32[3,3,2,1,128]{4,0,3,2,1:T(4,128)S(1)}, u32[]{:S(2)}, u32[]{:S(2)}) collective-permute-start(f32[3,3,2,1,128]{4,0,3,2,1:T(4,128)S(1)} %slice.903), channel_id=1, source_target_pairs={{0,8},{8,16},{16,24},{24,0},{1,9},{9,17},{17,25},{25,1},{2,10},{10... | collective-permute-start | bytes 27656 | tf_op jit(solution)/shard_map/ppermute | solution.py:27
  206.4 8.4 %collective-permute-start.56 = (f32[3,7,7,1]{3,2,1,0:T(8,128)S(1)}, f32[3,7,7,1]{3,2,1,0:T(8,128)S(1)}, u32[]{:S(2)}, u32[]{:S(2)}) collective-permute-start(f32[3,7,7,1]{3,2,1,0:T(8,128)S(1)} %pad_maximum_fusion.11), channel_id=1, source_target_pairs={{0,7},{1,0},{2,1},{3,2},{4,3},{5,4},{6,5},{7,6},{8,15},{9,8},{10,9... | collective-permute-start | bytes 1772 | tf_op jit(solution)/shard_map/ppermute | solution.py:27
  242.0 16.8 %collective-permute-start.49 = (f32[3,3,1,2,128]{4,3,2,1,0:T(2,128)S(1)}, f32[3,3,1,2,128]{4,3,2,1,0:T(2,128)S(1)}, u32[]{:S(2)}, u32[]{:S(2)}) collective-permute-start(f32[3,3,1,2,128]{4,3,2,1,0:T(2,128)S(1)} %slice.912), channel_id=1, source_target_pairs={{0,224},{32,0},{64,32},{96,64},{128,96},{160,128},{192,160},{224,1... | collective-permute-start | bytes 27656 | tf_op jit(solution)/shard_map/ppermute | solution.py:27
  245.0 13.7 %collective-permute-start.48 = (f32[3,3,1,2,128]{4,3,2,1,0:T(2,128)S(1)}, f32[3,3,1,2,128]{4,3,2,1,0:T(2,128)S(1)}, u32[]{:S(2)}, u32[]{:S(2)}) collective-permute-start(f32[3,3,1,2,128]{4,3,2,1,0:T(2,128)S(1)} %slice.911), channel_id=1, source_target_pairs={{0,32},{32,64},{64,96},{96,128},{128,160},{160,192},{192,224},{224... | collective-permute-start | bytes 27656 | tf_op jit(solution)/shard_map/ppermute | solution.py:27
  245.0 13.8 %collective-permute-start.51 = (f32[3,3,2,1,128]{4,0,3,2,1:T(4,128)S(1)}, f32[3,3,2,1,128]{4,0,3,2,1:T(4,128)S(1)}, u32[]{:S(2)}, u32[]{:S(2)}) collective-permute-start(f32[3,3,2,1,128]{4,0,3,2,1:T(4,128)S(1)} %slice.916), channel_id=1, source_target_pairs={{0,24},{8,0},{16,8},{24,16},{1,25},{9,1},{17,9},{25,17},{2,26},{10... | collective-permute-start | bytes 27656 | tf_op jit(solution)/shard_map/ppermute | solution.py:27
  247.6 9.4 %collective-permute-start.52 = (f32[3,3,2,2,1]{4,0,3,2,1:T(4,128)S(1)}, f32[3,3,2,2,1]{4,0,3,2,1:T(4,128)S(1)}, u32[]{:S(2)}, u32[]{:S(2)}) collective-permute-start(f32[3,3,2,2,1]{4,0,3,2,1:T(4,128)S(1)} %slice.919), channel_id=1, source_target_pairs={{0,1},{1,2},{2,3},{3,4},{4,5},{5,6},{6,7},{7,0},{8,9},{9,10},{10,1... | collective-permute-start | bytes 440 | tf_op jit(solution)/shard_map/ppermute | solution.py:27
  251.6 7.0 %collective-permute-start.53 = (f32[3,3,2,2,1]{4,0,3,2,1:T(4,128)S(1)}, f32[3,3,2,2,1]{4,0,3,2,1:T(4,128)S(1)}, u32[]{:S(2)}, u32[]{:S(2)}) collective-permute-start(f32[3,3,2,2,1]{4,0,3,2,1:T(4,128)S(1)} %bitcast.1066), channel_id=1, source_target_pairs={{0,7},{1,0},{2,1},{3,2},{4,3},{5,4},{6,5},{7,6},{8,15},{9,8},{10,9... | collective-permute-start | bytes 440 | tf_op jit(solution)/shard_map/ppermute | solution.py:27
  314.8 9.3 %collective-permute-start.59 = (f32[3,6,6,1]{3,1,2,0:T(8,128)S(1)}, f32[3,6,6,1]{3,1,2,0:T(8,128)S(1)}, u32[]{:S(2)}, u32[]{:S(2)}) collective-permute-start(f32[3,6,6,1]{3,1,2,0:T(8,128)S(1)} %slice.949), channel_id=1, source_target_pairs={{0,1},{1,2},{2,3},{3,4},{4,5},{5,6},{6,7},{7,0},{8,9},{9,10},{10,1... | collective-permute-start | bytes 1304 | tf_op jit(solution)/shard_map/ppermute | solution.py:27
  368.5 8.4 %collective-permute-start.60 = (f32[3,1,6,384]{3,1,2,0:T(1,128)S(1)}, f32[3,1,6,384]{3,1,2,0:T(1,128)S(1)}, u32[]{:S(2)}, u32[]{:S(2)}) collective-permute-start(f32[3,1,6,384]{3,1,2,0:T(1,128)S(1)} %slice.951), channel_id=1, source_target_pairs={{0,224},{32,0},{64,32},{96,64},{128,96},{160,128},{192,160},{224,1... | collective-permute-start | bytes 82952 | tf_op jit(solution)/shard_map/ppermute | solution.py:27
  380.0 9.4 %collective-permute-start.62 = (f32[3,7,7,1]{3,1,2,0:T(8,128)S(1)}, f32[3,7,7,1]{3,1,2,0:T(8,128)S(1)}, u32[]{:S(2)}, u32[]{:S(2)}) collective-permute-start(f32[3,7,7,1]{3,1,2,0:T(8,128)S(1)} %pad_maximum_fusion.9), channel_id=1, source_target_pairs={{0,7},{1,0},{2,1},{3,2},{4,3},{5,4},{6,5},{7,6},{8,15},{9,8},{10,9... | collective-permute-start | bytes 1772 | tf_op jit(solution)/shard_map/ppermute | solution.py:27
  (27 other events, 116.8 us)
where the time goes:
time: 465 us; the launch traced here: 456 us
  starting transfers between devices  149 us (32%)
  blocking collectives  122 us (26%)
  local copies, waits for them, and re-layouts  74 us (16%)
  waiting for transfers between devices  54.4 us (12%)
  matrix products  42 us (9%)
  other arithmetic  8.4 us (2%)
  between operations  5.77 us (1%)
    ppermute x57, starting transfers between devices, passed_along(): return lax.ppermute(x, axis, [(i, (i + by) % count) for i in range(count)])  136 us
    psum x10, blocking collectives, one_axis_at_a_time_2(): x = lax.psum(x, axis)  81.3 us
    ppermute x57, waiting for transfers between devices, passed_along(): return lax.ppermute(x, axis, [(i, (i + by) % count) for i in range(count)])  48.8 us
    pmax x5, blocking collectives, one_axis_at_a_time(): x = lax.pmax(x, axis)  40.6 us
    pad x12, local copies, waits for them, and re-layouts, pad_one(): return lax.pad(operand, jnp.zeros((), operand.dtype), config)  33.2 us
    slice x12, local copies, waits for them, and re-layouts, element_corners(): lax.slice_in_dim(gathered, node_offset, node_offset + 3 * extent - 2, str...  31.8 us
    dot_general x51, matrix products, contract(): jnp.tensordot(as_table(weights_table), operand, axes=([1], [along]), prec...  29.6 us
    dot_general x48, matrix products, trace_along(): jnp.tensordot(as_table(vector), modal_coefficients, axes=([0], [direction...  12.5 us
  transfers between devices with their start and end apart: 63, of which 28 were waited for; matrix products, arithmetic and copies ran while one was open for 10% of the time, Pallas kernels for 0%

commit v1 on v0

v1 whole, which is shorter than its diff:
```python
import jax
import jax.numpy as jnp
import numpy as np
from jax import lax
from jax.experimental import pallas as pl
from jax.experimental.pallas import tpu as pltpu
from jax.sharding import Mesh
from jax.sharding import PartitionSpec as P

SUBSTEPS = 4
GX = ("gx_0", "gx_1")
GZ = ("gz_0", "gz_1")
XY = ("gx_0", "gx_1", "gy")

NZ = 8
NXY = 32
HALO_ROWS = 16
IN_ROWS = 48
X_ROW = 24
MAX_ROW = 47
OUT_ROWS = 16

p0 = 0.7071067811865476
p1 = 1.224744871391589
p2 = 1.5811388300841898
root3 = 1.7320508075688772
root15 = 3.872983346207417
courant = 0.1
theta_size = 0.3
trial_step = 0.05


def build_tables():
    points = np.array(
        [-0.8611363115940526, -0.3399810435848563, 0.3399810435848563, 0.8611363115940526]
    )
    weights = np.array(
        [0.3478548451374538, 0.6521451548625461, 0.6521451548625461, 0.3478548451374538]
    )
    points = 0.5 * (points + 1.0)
    weights = 0.5 * weights
    node_points = np.array([0.0, 1.0 / 3.0, 2.0 / 3.0, 1.0])
    value_table = np.zeros((4, 4))
    slope_table = np.zeros((4, 4))
    for column in range(4):
        others = [node_points[member] for member in range(4) if member != column]
        denominator = np.prod([node_points[column] - member for member in others])
        for quad_row in range(4):
            gauss_point = points[quad_row]
            value_table[quad_row, column] = (
                np.prod([gauss_point - member for member in others]) / denominator
            )
            slope_table[quad_row, column] = (
                sum(
                    np.prod(
                        [gauss_point - others[position] for position in range(3) if position != skipped]
                    )
                    for skipped in range(3)
                )
                / denominator
            )
    centred = 2.0 * points - 1.0
    legendre_table = np.stack(
        [
            np.full(4, p0),
            p1 * centred,
            p2 * 0.5 * (3.0 * centred**2 - 1.0),
        ],
        axis=1,
    )
    return value_table, slope_table, legendre_table, weights


VALUES, SLOPES, LEGENDRE, WEIGHTS = build_tables()


def iota(shape, dim):
    return lax.broadcasted_iota(jnp.int32, shape, dim)


def lanes(x, by):
    return pltpu.roll(x, (-by) % 128, x.ndim - 1)


def rows(x, by):
    return pltpu.roll(x, (-by) % 8, x.ndim - 2)


class Shifts:
    def __init__(self, *lead):
        r, l = iota((*lead, 8, 128), len(lead)), iota((*lead, 8, 128), len(lead) + 1)
        self.a0 = ((r >> 1) & 1) == 0
        self.b0 = (r & 1) == 0
        self.low = r < 4
        self.j = l & 3
        self.i = (l >> 2) & 7
        self.z = l >> 5

    def swap_x(self, x):
        return jnp.where(self.a0, rows(x, 2), rows(x, -2))

    def swap_y(self, x):
        return jnp.where(self.b0, rows(x, 1), rows(x, -1))

    def next(self, x, d):
        if d == 0:
            s = self.swap_x(x)
            return jnp.where(self.a0, s, jnp.where(self.i < 7, lanes(s, 4), lanes(s, -28)))
        if d == 1:
            s = self.swap_y(x)
            return jnp.where(self.b0, s, jnp.where(self.j < 3, lanes(s, 1), lanes(s, -3)))
        s = lanes(x, 32)
        t = rows(s, 4)
        if x.ndim == 3:
            t = jnp.where(self.low, t, jnp.concatenate([t[1:], t[:1]], axis=0))
        return jnp.where(self.z < 3, s, t)

    def prev(self, x, d):
        if d == 0:
            s = self.swap_x(x)
            return jnp.where(self.a0, jnp.where(self.i > 0, lanes(s, -4), lanes(s, 28)), s)
        if d == 1:
            s = self.swap_y(x)
            return jnp.where(self.b0, jnp.where(self.j > 0, lanes(s, -1), lanes(s, 3)), s)
        s = lanes(x, -32)
        t = rows(s, 4)
        if x.ndim == 3:
            t = jnp.where(self.low, jnp.concatenate([t[-1:], t[:-1]], axis=0), t)
        return jnp.where(self.z > 0, s, t)


def halves(x):
    return (x[0] + x[3], x[1] + x[2], x[0] - x[3], x[1] - x[2])


def apply_table(table, sign, half):
    ea, eb, oa, ob = half
    out = [None] * 4
    for p in range(2):
        even = float(0.5 * (table[p, 0] + table[p, 3])) * ea + float(0.5 * (table[p, 1] + table[p, 2])) * eb
        odd = float(0.5 * (table[p, 0] - table[p, 3])) * oa + float(0.5 * (table[p, 1] - table[p, 2])) * ob
        out[p] = even + odd
        out[3 - p] = even - odd if sign > 0 else odd - even
    return out


def transpose_kernel(g_ref, u_ref, v_ref, x_ref, tuv_ref, tx_ref, halo_ref, uv_s, x_s):
    zero = jnp.zeros((24, 384), jnp.float32)
    uv_s[0:108, :] = u_ref[...]
    uv_s[108:120, :] = v_ref[...]
    uv_s[120:128, :] = zero[0:8, 0:128]
    x_s[0:108, :] = x_ref[...]
    x_s[108:128, :] = zero[0:20]
    tuv_ref[...] = uv_s[...].T
    for n in range(3):
        tx_ref[128 * n : 128 * n + 128, :] = x_s[:, 128 * n : 128 * n + 128].T
    speed = jnp.abs(v_ref[0:4, :]) + jnp.abs(v_ref[4:8, :]) + jnp.abs(v_ref[8:12, :])
    fastest = jnp.broadcast_to(jnp.max(speed, axis=(0, 1), keepdims=True), (1, 128))
    for n in range(NZ):
        halo_ref[n, :, :] = zero[0:16, 0:128]
        halo_ref[n, 13:14, :] = fastest
    up = lax.rem(g_ref[0] + 1, NZ)
    down = lax.rem(g_ref[0] + NZ - 1, NZ)
    halo_ref[up, 0:9, :] = tuv_ref[119:128, :]
    halo_ref[up, 9:12, :] = tx_ref[381:384, :]
    halo_ref[down, 0:9, :] = tuv_ref[0:9, :]
    halo_ref[down, 9:13, :] = tx_ref[0:4, :]


def pack_kernel(g_ref, tuv_ref, tx_ref, halo_ref, out_ref, uv_s, x_s):
    below = lax.rem(g_ref[0] + NZ - 1, NZ)
    above = lax.rem(g_ref[0] + 1, NZ)
    uv_s[0:16, :] = jnp.zeros((16, 128), jnp.float32)
    uv_s[144:160, :] = jnp.zeros((16, 128), jnp.float32)
    x_s[0:8, :] = jnp.zeros((8, 128), jnp.float32)
    x_s[392:408, :] = jnp.zeros((16, 128), jnp.float32)
    uv_s[16:144, :] = tuv_ref[...]
    x_s[8:392, :] = tx_ref[...]
    uv_s[7:16, :] = halo_ref[below, 0:9, :]
    uv_s[144:153, :] = halo_ref[above, 0:9, :]
    x_s[5:8, :] = halo_ref[below, 9:12, :]
    x_s[392:396, :] = halo_ref[above, 9:13, :]
    fastest = halo_ref[0, 13:14, :]
    for n in range(1, NZ):
        fastest = jnp.maximum(fastest, halo_ref[n, 13:14, :])
    for k in range(NXY):
        at = IN_ROWS * k
        out_ref[at : at + 24, :] = uv_s[4 * k + 7 : 4 * k + 31, :]
        out_ref[at + 24 : at + 48, :] = x_s[12 * k + 5 : 12 * k + 29, :]
        out_ref[at + MAX_ROW : at + MAX_ROW + 1, :] = fastest


def corner_fill(ref, sh):
    def one(c, carry):
        at = c * 64
        for kx in range(3):
            for ky in range(3):
                ref[at + kx * 16 + ky * 4 + 3] = sh.next(ref[at + kx * 16 + ky * 4], 2)
        for kx in range(3):
            for kz in range(4):
                ref[at + kx * 16 + 12 + kz] = sh.next(ref[at + kx * 16 + kz], 1)
        for ky in range(4):
            for kz in range(4):
                ref[at + 48 + ky * 4 + kz] = sh.next(ref[at + ky * 4 + kz], 0)
        return carry

    lax.fori_loop(0, 3, one, 0)


def corner_fold(ref, sh):
    def one(c, carry):
        at = c * 64
        for ky in range(4):
            for kz in range(4):
                n = at + ky * 4 + kz
                ref[n] = ref[n] + sh.prev(ref[n + 48], 0)
        for kx in range(3):
            for kz in range(4):
                n = at + kx * 16 + kz
                ref[n] = ref[n] + sh.prev(ref[n + 12], 1)
        for kx in range(3):
            for ky in range(3):
                n = at + kx * 16 + ky * 4
                ref[n] = ref[n] + sh.prev(ref[n + 3], 2)
        return carry

    lax.fori_loop(0, 3, one, 0)


def slopes_at_points(src, dst, a_s, b_s):
    def one(c, carry):
        at = c * 64
        for line in range(16):
            h = halves([src[at + k * 16 + line] for k in range(4)])
            v = apply_table(VALUES, 1, h)
            s = apply_table(SLOPES, -1, h)
            for p in range(4):
                a_s[p * 16 + line] = v[p]
                a_s[64 + p * 16 + line] = s[p]
        for p in range(4):
            for kz in range(4):
                hv = halves([a_s[p * 16 + k * 4 + kz] for k in range(4)])
                hs = halves([a_s[64 + p * 16 + k * 4 + kz] for k in range(4)])
                sv = apply_table(VALUES, 1, hs)
                vs = apply_table(SLOPES, -1, hv)
                vv = apply_table(VALUES, 1, hv)
                for r in range(4):
                    b_s[p * 16 + r * 4 + kz] = sv[r]
                    b_s[64 + p * 16 + r * 4 + kz] = vs[r]
                    b_s[128 + p * 16 + r * 4 + kz] = vv[r]
        for pr in range(16):
            for col in range(3):
                h = halves([b_s[64 * col + pr * 4 + k] for k in range(4)])
                out = apply_table(SLOPES, -1, h) if col == 2 else apply_table(VALUES, 1, h)
                for t in range(4):
                    dst[c * 192 + 64 * col + pr * 4 + t] = out[t]
        return carry

    lax.fori_loop(0, 3, one, 0)


def points_to_corners(src, dst, a_s, b_s):
    values_t, slopes_t = VALUES.T, SLOPES.T

    def one(c, carry):
        at = c * 64
        for pr in range(16):
            for col in range(3):
                h = halves([src[c * 192 + 64 * col + pr * 4 + t] for t in range(4)])
                out = apply_table(slopes_t, -1, h) if col == 2 else apply_table(values_t, 1, h)
                for k in range(4):
                    b_s[64 * col + pr * 4 + k] = out[k]
        for p in range(4):
            for kz in range(4):
                sv = apply_table(values_t, 1, halves([b_s[p * 16 + r * 4 + kz] for r in range(4)]))
                vs = apply_table(slopes_t, -1, halves([b_s[64 + p * 16 + r * 4 + kz] for r in range(4)]))
                vv = apply_table(values_t, 1, halves([b_s[128 + p * 16 + r * 4 + kz] for r in range(4)]))
                for k in range(4):
                    a_s[p * 16 + k * 4 + kz] = vv[k] + vs[k]
                    a_s[64 + p * 16 + k * 4 + kz] = sv[k]
        for line in range(16):
            v = apply_table(values_t, 1, halves([a_s[p * 16 + line] for p in range(4)]))
            s = apply_table(slopes_t, -1, halves([a_s[64 + p * 16 + line] for p in range(4)]))
            for k in range(4):
                dst[at + k * 16 + line] = v[k] + s[k]
        return carry

    lax.fori_loop(0, 3, one, 0)


def legendre_line(u):
    base = p0 * u[0]
    out = [None] * 4
    for p in range(2):
        even = base + float(LEGENDRE[p, 2]) * u[2]
        odd = float(LEGENDRE[p, 1]) * u[1]
        out[p] = even + odd
        out[3 - p] = even - odd
    return out


def sample_sizes(u_s, size_s, a_s):
    for bc in range(9):
        out = legendre_line([u_s[a * 9 + bc, 1] for a in range(3)])
        for p in range(4):
            a_s[p * 9 + bc] = out[p]
    for p in range(4):
        grid = [[None] * 3 for _ in range(4)]
        for c in range(3):
            out = legendre_line([a_s[p * 9 + b * 3 + c] for b in range(3)])
            for r in range(4):
                grid[r][c] = out[r]
        for r in range(4):
            out = legendre_line(grid[r])
            for t in range(4):
                size_s[p * 16 + r * 4 + t] = jnp.exp(theta_size * out[t])


PAIRS = ((0, 0), (1, 1), (2, 2), (0, 1), (0, 2), (1, 2))
AT = {pair: n for n, pair in enumerate(PAIRS)} | {(b, a): n for n, (a, b) in enumerate(PAIRS)}


def dot6(x, y):
    return x[0] * y[0] + x[1] * y[1] + x[2] * y[2] + 2.0 * (x[3] * y[3] + x[4] * y[4] + x[5] * y[5])


def weight_of(pr):
    def w(k):
        return jnp.where((k == 0) | (k == 3), jnp.float32(WEIGHTS[0]), jnp.float32(WEIGHTS[1]))

    return w(pr >> 2) * w(pr & 3)


def jacobian(j_s, q):
    jac = [[j_s[c * 192 + col * 64 + q] for col in range(3)] for c in range(3)]
    for c in range(3):
        jac[c][c] = jac[c][c] + 1.0
    return jac


def stress(j_s, size_s, g_s, p_s):
    def one(pr, energy):
        pair_weight = weight_of(pr)
        for t in range(4):
            q = pr * 4 + t
            jac = jacobian(j_s, q)
            size = size_s[q]
            inverse = 1.0 / size
            inverse2 = inverse * inverse
            weighted = (pair_weight * float(WEIGHTS[t])) * size
            dev = []
            for n, (a, b) in enumerate(PAIRS):
                gram = (jac[0][a] * jac[0][b] + jac[1][a] * jac[1][b] + jac[2][a] * jac[2][b]) * inverse2
                dev.append(gram - 1.0 if a == b else gram)
                g_s[n * 64 + q] = dev[n]
            energy = energy + weighted * size * size * dot6(dev, dev)
            scaled = [4.0 * weighted * d for d in dev]
            for c in range(3):
                for col in range(3):
                    p_s[c * 192 + col * 64 + q] = (
                        jac[c][0] * scaled[AT[0, col]]
                        + jac[c][1] * scaled[AT[1, col]]
                        + jac[c][2] * scaled[AT[2, col]]
                    )
        return energy

    return lax.fori_loop(0, 16, one, jnp.zeros((8, 128), jnp.float32))


def trial_terms(j_s, size_s, g_s, d_s):
    def one(pr, sums):
        e2, e3, e4 = sums
        pair_weight = weight_of(pr)
        for t in range(4):
            q = pr * 4 + t
            jac = jacobian(j_s, q)
            der = [[d_s[c * 192 + col * 64 + q] for col in range(3)] for c in range(3)]
            size = size_s[q]
            inverse = 1.0 / size
            inverse2 = inverse * inverse
            weighted = (pair_weight * float(WEIGHTS[t])) * size * size * size
            dev, first, second = [], [], []
            for n, (a, b) in enumerate(PAIRS):
                dev.append(g_s[n * 64 + q])
                if a == b:
                    f = 2.0 * (jac[0][a] * der[0][a] + jac[1][a] * der[1][a] + jac[2][a] * der[2][a])
                else:
                    f = (
                        jac[0][a] * der[0][b] + jac[1][a] * der[1][b] + jac[2][a] * der[2][b]
                        + jac[0][b] * der[0][a] + jac[1][b] * der[1][a] + jac[2][b] * der[2][a]
                    )
                first.append(f * inverse2)
                second.append((der[0][a] * der[0][b] + der[1][a] * der[1][b] + der[2][a] * der[2][b]) * inverse2)
            e2 = e2 + weighted * (dot6(first, first) + 2.0 * dot6(dev, second))
            e3 = e3 - 2.0 * weighted * dot6(first, second)
            e4 = e4 + weighted * dot6(second, second)
        return e2, e3, e4

    zero = jnp.zeros((8, 128), jnp.float32)
    return lax.fori_loop(0, 16, one, (zero, zero, zero))


def remap(u_s, v_s, mid_s, face_s, time_step, sh):
    for d in range(3):
        v = v_s[d]
        face = 0.5 * (v + sh.next(v, d))
        face_s[4 * d] = 2.0 * time_step * jnp.maximum(face, 0.0)
        face_s[4 * d + 1] = 2.0 * time_step * jnp.minimum(face, 0.0)
        face_s[4 * d + 2] = (2.0 * root3) * time_step * v
        face_s[4 * d + 3] = (2.0 * root15) * time_step * v

    def terms(src, d, m, step):
        u0, u1, u2 = src[m], src[m + step], src[m + 2 * step]
        even = p0 * u0 + p2 * u2
        odd = p1 * u1
        flux = face_s[4 * d] * (even + odd) + face_s[4 * d + 1] * sh.next(even - odd, d)
        before = sh.prev(flux, d)
        jump = before - flux
        return (
            p0 * jump,
            face_s[4 * d + 2] * u0 - p1 * (flux + before),
            face_s[4 * d + 3] * u1 + p2 * jump,
        )

    def substep(_, carry):
        for d, step, starts in (
            (0, 9, range(9)),
            (1, 3, (0, 1, 2, 9, 10, 11, 18, 19, 20)),
            (2, 1, range(0, 27, 3)),
        ):
            for m in starts:
                for n, term in enumerate(terms(u_s, d, m, step)):
                    at = m + n * step
                    mid_s[at] = (u_s[at] if d == 0 else mid_s[at]) + term
        for d, step, starts in (
            (0, 9, range(9)),
            (1, 3, (0, 1, 2, 9, 10, 11, 18, 19, 20)),
            (2, 1, range(0, 27, 3)),
        ):
            for m in starts:
                for n, term in enumerate(terms(mid_s, d, m, step)):
                    at = m + n * step
                    old = 0.5 * (u_s[at] + mid_s[at]) if d == 0 else u_s[at]
                    u_s[at] = old + 0.5 * term
        return carry

    lax.fori_loop(0, SUBSTEPS, substep, 0)


def main_kernel(
    in_ref, out_ref, t_s, u_s, v_s, mid_s, face_s, x_s, a_s, b_s, j_s, p_s, g_s, size_s
):
    sh = Shifts()
    for zz in range(6):
        stacked = jnp.concatenate(
            [in_ref[pl.ds(4 * zz + z, NXY, stride=IN_ROWS), :] for z in range(4)], axis=0
        )
        t_s[...] = stacked.T
        half = 4 * (zz % 2)
        for m in range(27):
            u_s[m, zz // 2, half : half + 4, :] = t_s[4 * m : 4 * m + 4, :]
        for d in range(3):
            v_s[d, zz // 2, half : half + 4, :] = t_s[108 + 4 * d : 112 + 4 * d, :]
    for kz in range(3):
        for part in range(2):
            stacked = jnp.concatenate(
                [
                    in_ref[pl.ds(X_ROW + 3 * (4 * part + z) + kz, NXY, stride=IN_ROWS), :]
                    for z in range(4)
                ],
                axis=0,
            )
            t_s[...] = stacked.T
            half = 4 * part
            for n in range(27):
                c, kx, ky = n // 9, (n // 3) % 3, n % 3
                x_s[c * 64 + kx * 16 + ky * 4 + kz, half : half + 4, :] = t_s[4 * n : 4 * n + 4, :]
    fastest = jnp.max(in_ref[pl.ds(MAX_ROW, NXY, stride=IN_ROWS), :], axis=0, keepdims=True)
    time_step = jnp.broadcast_to(courant / jnp.maximum(fastest, 0.25), (8, 128))
    remap(u_s, v_s, mid_s, face_s, time_step, Shifts(3))

    corner_fill(x_s, sh)
    slopes_at_points(x_s, j_s, a_s, b_s)
    sample_sizes(u_s, size_s, a_s)
    energy = stress(j_s, size_s, g_s, p_s)
    points_to_corners(p_s, x_s, a_s, b_s)
    corner_fold(x_s, sh)
    own = jnp.where(sh.low, sh.z, 1 - sh.z) > 0
    square = jnp.zeros((8, 128), jnp.float32)
    for n in range(27):
        for kz in range(3):
            grad = x_s[(n // 9) * 64 + ((n // 3) % 3) * 16 + (n % 3) * 4 + kz]
            square = square + grad * grad
    corner_fill(x_s, sh)
    slopes_at_points(x_s, p_s, a_s, b_s)
    sums = (energy, square) + trial_terms(j_s, size_s, g_s, p_s)
    t_s[108:128, :] = jnp.zeros((20, 128), jnp.float32)
    for n, part in enumerate(sums):
        total = jnp.sum(jnp.where(own, part, 0.0), axis=(0, 1), keepdims=True)
        t_s[108 + n : 109 + n, :] = jnp.broadcast_to(total, (1, 128))
    for part in range(2):
        half = 4 * part
        layers = ((1, 0), (2, 1), (3, 2)) if part == 0 else ((0, 3),)
        for m in range(27):
            t_s[4 * m : 4 * m + 4, :] = u_s[m, 1, half : half + 4, :]
        back = t_s[...].T
        for z, layer in layers:
            out_ref[pl.ds(layer, NXY, stride=OUT_ROWS), :] = back[32 * z : 32 * z + 32, :]
        for kz in range(3):
            for n in range(27):
                c, kx, ky = n // 9, (n // 3) % 3, n % 3
                t_s[4 * n : 4 * n + 4, :] = x_s[c * 64 + kx * 16 + ky * 4 + kz, half : half + 4, :]
            back = t_s[...].T
            for z, layer in layers:
                out_ref[pl.ds(4 + 3 * layer + kz, NXY, stride=OUT_ROWS), :] = back[32 * z : 32 * z + 32, :]


def unpack_kernel(in_ref, u_ref, g_ref, sums_ref, u_s, g_s):
    for layer in range(4):
        u_s[pl.ds(layer, NXY, stride=4), :] = in_ref[pl.ds(layer, NXY, stride=OUT_ROWS), :]
    for r in range(12):
        g_s[pl.ds(r, NXY, stride=12), :] = in_ref[pl.ds(4 + r, NXY, stride=OUT_ROWS), :]
    sums_ref[...] = jnp.sum(in_ref[pl.ds(0, NXY, stride=OUT_ROWS), :], axis=0, keepdims=True)
    u_ref[...] = u_s[...].T[0:108, :]
    for n in range(3):
        g_ref[:, 128 * n : 128 * n + 128] = g_s[128 * n : 128 * n + 128, :].T[0:108, :]


def shape(*dims):
    return jax.ShapeDtypeStruct(dims, jnp.float32)


def vmem(*dims):
    return pltpu.VMEM(dims, jnp.float32)


SMEM = pl.BlockSpec(memory_space=pltpu.SMEM)
VMEM = pl.BlockSpec(memory_space=pltpu.VMEM)


def on_device(displacement, size_field_modes, velocity):
    at_z = lax.axis_index(GZ).reshape(1).astype(jnp.int32)
    u = size_field_modes.reshape(108, 128)
    v = velocity.reshape(12, 128)
    x = displacement.reshape(3, 2, 3, 2, 3, 384).transpose(0, 2, 4, 1, 3, 5).reshape(108, 384)
    tuv, tx, halo = pl.pallas_call(
        transpose_kernel,
        out_shape=(shape(128, 128), shape(384, 128), shape(NZ, HALO_ROWS, 128)),
        in_specs=[SMEM, VMEM, VMEM, VMEM],
        out_specs=(VMEM, VMEM, VMEM),
        scratch_shapes=[vmem(128, 128), vmem(128, 384)],
        name="transpose",
    )(at_z, u, v, x)
    halo = lax.all_to_all(halo, GZ, 0, 0)
    packed = pl.pallas_call(
        pack_kernel,
        out_shape=shape(NXY * IN_ROWS, 128),
        in_specs=[SMEM, VMEM, VMEM, VMEM],
        out_specs=VMEM,
        scratch_shapes=[vmem(160, 128), vmem(408, 128)],
        name="pack",
    )(at_z, tuv, tx, halo)
    spread = lax.all_to_all(packed.reshape(NXY, IN_ROWS, 128), XY, 0, 0)
    result = pl.pallas_call(
        main_kernel,
        out_shape=shape(NXY * OUT_ROWS, 128),
        in_specs=[VMEM],
        out_specs=VMEM,
        scratch_shapes=[
            vmem(128, 128),
            vmem(27, 3, 8, 128),
            vmem(3, 3, 8, 128),
            vmem(27, 3, 8, 128),
            vmem(12, 3, 8, 128),
            vmem(192, 8, 128),
            vmem(128, 8, 128),
            vmem(192, 8, 128),
            vmem(576, 8, 128),
            vmem(576, 8, 128),
            vmem(384, 8, 128),
            vmem(64, 8, 128),
        ],
        name="remap_and_gradient",
    )(spread.reshape(NXY * IN_ROWS, 128))
    result = lax.all_to_all(result.reshape(NXY, OUT_ROWS, 128), XY, 0, 0)
    advected, gradient, sums = pl.pallas_call(
        unpack_kernel,
        out_shape=(shape(108, 128), shape(108, 384), shape(1, 128)),
        in_specs=[VMEM],
        out_specs=(VMEM, VMEM, VMEM),
        scratch_shapes=[vmem(128, 128), vmem(384, 128)],
        name="unpack",
    )(result.reshape(NXY * OUT_ROWS, 128))
    sums = lax.all_to_all(jnp.broadcast_to(sums[None], (NZ, 1, 128)), GZ, 0, 0)
    sums = jnp.sum(sums, axis=0)[0]
    e0, square, e2, e3, e4 = (sums[108 + n] for n in range(5))
    elements = float(512 * NXY * NZ)
    entries = 81.0 * elements
    step = trial_step / jnp.sqrt(1.0 + square / entries)
    trial = e0 + step * (-square + step * (e2 + step * (e3 + step * e4)))
    checks = jnp.stack([e0 / elements, square / entries, trial / elements])
    gradient = gradient.reshape(3, 3, 3, 2, 2, 384).transpose(0, 3, 1, 4, 2, 5).reshape(3, 6, 6, 384)
    return advected.reshape(27, 2, 2, 128), gradient, checks


def solution(mesh):
    finer = Mesh(
        mesh.devices.reshape(4, 2, mesh.shape["gy"], 4, 2), ("gx_0", "gx_1", "gy", "gz_0", "gz_1")
    )
    return jax.shard_map(
        on_device,
        mesh=finer,
        in_specs=(P(None, GX, "gy", GZ), P(None, GX, "gy", GZ), P(None, GX, "gy", GZ)),
        out_specs=(P(None, GX, "gy", GZ), P(None, GX, "gy", GZ), P()),
        check_vma=False,
    )
```

time: 465 us -> 121 us (0.26); the launches traced: 456 us -> 120 us
  starting transfers between devices: 149 us -> 3.32 us
  local copies, waits for them, and re-layouts: 74 us -> 9.82 us
  blocking collectives: 122 us -> 66.3 us
  waiting for transfers between devices: 54.4 us -> 5.6 us
  matrix products: 42 us -> 0 us
  Pallas kernels: 0 us -> 29.3 us
  other arithmetic: 8.4 us -> 0.6 us
    ppermute x63 -> x0, starting transfers between devices: 149 us -> none  [the longest x57 136 us: passed_along(): return lax.ppermute(x, axis, [(i, (i + by) % count) for i in range(count)])]
    psum x10 -> x0, blocking collectives: 81.3 us -> none  [one_axis_at_a_time_2(): x = lax.psum(x, axis)]
    all_to_all x0 -> x3, blocking collectives: none -> 66.3 us  [the longest x1 29.6 us: on_device(): spread = lax.all_to_all(packed.reshape(NXY, IN_ROWS, 128), XY, 0, 0)]
    ppermute x63 -> x0, waiting for transfers between devices: 54.4 us -> none  [the longest x57 48.8 us: passed_along(): return lax.ppermute(x, axis, [(i, (i + by) % count) for i in range(count)])]
    dot_general x99 -> x0, matrix products: 42 us -> none  [the longest x51 29.6 us: contract(): jnp.tensordot(as_table(weights_table), operand, axes=([1], [along]), prec...]
    pmax x5 -> x0, blocking collectives: 40.6 us -> none  [one_axis_at_a_time(): x = lax.pmax(x, axis)]
    slice x88 -> x1, local copies, waits for them, and re-layouts: 34.8 us -> 0.67 us  [on_device(): e0, square, e2, e3, e4 = (sums[108 + n] for n in range(5))]
    pad x12 -> x0, local copies, waits for them, and re-layouts: 33.2 us -> none  [pad_one(): return lax.pad(operand, jnp.zeros((), operand.dtype), config)]
  transfers between devices with their start and end apart: 63 -> 1, of which waited for: 28 -> 1; matrix products, arithmetic and copies ran while one was open for 10% -> 3% of each run, Pallas kernels for 0% -> 0%
where the time goes in v1:
time: 121 us; the launch traced here: 120 us
  blocking collectives  66.3 us (55%)
  Pallas kernels  29.3 us (24%)
  local copies, waits for them, and re-layouts  9.82 us (8%)
  waiting for transfers between devices  5.6 us (5%)
  between operations  5.23 us (4%)
  starting transfers between devices  3.32 us (3%)
    all_to_all x1, blocking collectives, on_device(): spread = lax.all_to_all(packed.reshape(NXY, IN_ROWS, 128), XY, 0, 0)  29.6 us
    pallas_call x1, Pallas kernels, on_device(): pl.pallas_call(main_kernel, out_shape=shape(NXY * OUT_ROWS, 128), in_spec...  23.7 us
    all_to_all x1, blocking collectives, on_device(): halo = lax.all_to_all(halo, GZ, 0, 0)  20.8 us
    all_to_all x1, blocking collectives, on_device(): result = lax.all_to_all(result.reshape(NXY, OUT_ROWS, 128), XY, 0, 0)  15.8 us
    all_to_all x1, waiting for transfers between devices, on_device(): sums = lax.all_to_all(jnp.broadcast_to(sums[None], (NZ, 1, 128)), GZ, 0, 0)  5.6 us
    all_to_all x1, starting transfers between devices, on_device(): sums = lax.all_to_all(jnp.broadcast_to(sums[None], (NZ, 1, 128)), GZ, 0, 0)  3.32 us
    unnamed x6, local copies, waits for them, and re-layouts  3.07 us
  transfers between devices with their start and end apart: 1, of which 1 were waited for; matrix products, arithmetic and copies ran while one was open for 3% of the time, Pallas kernels for 0%

profile of v1, /device:TPU:1, one launch (start us, length us, event | category | flops | bytes accessed | tf_op | source)
XLA Modules:
  0.0 120.1 jit_solution(8501438750761505303)
XLA Ops:
  0.6 0.0 copy-start
  0.6 0.7 copy-done
  1.3 0.6 reshape.67.v_ref
  1.9 1.5 %reshape.66.u_ref = f32[108,128]{1,0:T(8,128)} reshape(f32[27,2,2,128]{3,2,1,0:T(2,128)} %param.4) | data formatting | bytes 110592 | tf_op jit(solution)/shard_map/reshape | solution.py:543
  3.4 1.0 copy.16
  4.4 0.1 copy.17
  4.5 0.8 reshape.69.x_ref
  5.3 1.8 %transpose.10 = (f32[128,128]{1,0:T(8,128)}, f32[384,128]{1,0:T(8,128)}, f32[8,16,128]{2,1,0:T(8,128)}) custom-call(s32[1]{0:T(128)} %bitcast.g_ref, f32[108,128]{1,0:T(8,128)} %reshape.66.u_ref, f32[12,128]{1,0:T(8,128)} %reshape.67.v_ref, f32[108,384]{1,0:T(8,128)} %reshape.69.x_ref), custom_call_target="tpu_custom_call" | custom-call | tf_op jit(solution)/shard_map/transpose/pallas_call | solution.py:546
  7.1 20.8 %all_to_all.20.halo_ref = f32[8,16,128]{2,1,0:T(8,128)} all-to-all(f32[8,16,128]{2,1,0:T(8,128)} %get-tuple-element.11), channel_id=1, replica_groups=mesh['gx_0'=4,'gx_1'=2,'gy'=4,'gz_0'=4,'gz_1'=2] {'gz_0','gz_1'}, dimensions={0} | all-to-all | bytes 131072 | tf_op jit(solution)/shard_map/all_to_all | solution.py:554
  28.0 1.9 %pack.1 = f32[1536,128]{1,0:T(8,128)} custom-call(s32[1]{0:T(128)} %bitcast.g_ref, f32[128,128]{1,0:T(8,128)} %get-tuple-element.9.tuv_ref, f32[384,128]{1,0:T(8,128)} %get-tuple-element.10.tx_ref, f32[8,16,128]{2,1,0:T(8,128)} %all_to_all.20.halo_ref), custom_call_target="tpu_custom_call" | custom-call | tf_op jit(solution)/shard_map/pack/pallas_call | solution.py:555
  29.9 29.6 %all_to_all.21 = f32[32,48,128]{2,1,0:T(8,128)} all-to-all(f32[32,48,128]{2,1,0:T(8,128)} %bitcast.24), channel_id=1, replica_groups=mesh['gx_0'=4,'gx_1'=2,'gy'=4,'gz_0'=4,'gz_1'=2] {'gx_0','gx_1','gy'}, dimensions={0} | all-to-all | bytes 1572864 | tf_op jit(solution)/shard_map/all_to_all | solution.py:563
  59.5 23.7 %remap_and_gradient.1 = f32[512,128]{1,0:T(8,128)} custom-call(f32[1536,128]{1,0:T(8,128)} %bitcast.23), custom_call_target="tpu_custom_call" | custom-call | tf_op jit(solution)/shard_map/remap_and_gradient/pallas_call | solution.py:564
  83.2 15.8 %all_to_all.22 = f32[32,16,128]{2,1,0:T(8,128)} all-to-all(f32[32,16,128]{2,1,0:T(8,128)} %bitcast.26), channel_id=1, replica_groups=mesh['gx_0'=4,'gx_1'=2,'gy'=4,'gz_0'=4,'gz_1'=2] {'gx_0','gx_1','gy'}, dimensions={0} | all-to-all | bytes 524288 | tf_op jit(solution)/shard_map/all_to_all | solution.py:585
  99.0 1.8 %unpack.1 = (f32[108,128]{1,0:T(8,128)}, f32[108,384]{1,0:T(8,128)}, f32[1,128]{1,0:T(1,128)}) custom-call(f32[512,128]{1,0:T(8,128)} %bitcast.25), custom_call_target="tpu_custom_call" | custom-call | tf_op jit(solution)/shard_map/unpack/pallas_call | solution.py:586
  100.8 0.0 copy-start.1
  100.8 0.7 copy-done.1
  101.5 0.6 broadcast_in_dim.9
  102.1 3.3 %all-to-all-start.3 = ((f32[8,1,128]{2,1,0:T(1,128)}), f32[8,1,128]{2,1,0:T(1,128)S(1)}, u32[]{:S(2)}, u32[]{:S(2)}) async-start(f32[8,1,128]{2,1,0:T(1,128)} %broadcast_in_dim.9), calls=%async_computation.3 | async-start | bytes 8192 | tf_op jit(solution)/shard_map/all_to_all | solution.py:594
  105.4 1.5 %reshape.74 = f32[27,2,2,128]{3,2,1,0:T(2,128)} reshape(f32[108,128]{1,0:T(8,128)} %get-tuple-element.12) | data formatting | bytes 110592 | tf_op jit(solution)/shard_map/reshape | solution.py:603
  106.9 1.0 reshape.75
  107.9 0.1 copy.18
  108.0 0.7 copy.20
  108.7 5.6 %all-to-all-done.3 = f32[8,1,128]{2,1,0:T(1,128)S(1)} async-done(((f32[8,1,128]{2,1,0:T(1,128)}), f32[8,1,128]{2,1,0:T(1,128)S(1)}, u32[]{:S(2)}, u32[]{:S(2)}) %all-to-all-start.3) | async-done | bytes 4128 | tf_op jit(solution)/shard_map/all_to_all | solution.py:594
  114.3 0.7 fusion
  119.5 0.6 pad_maximum_fusion
  (1 shorter events, 0.0 us)
Async XLA Ops:
  0.6 0.7 copy-start
  100.8 0.7 copy-start.1
  102.1 12.2 %all-to-all-start.3 = ((f32[8,1,128]{2,1,0:T(1,128)}), f32[8,1,128]{2,1,0:T(1,128)S(1)}, u32[]{:S(2)}, u32[]{:S(2)}) async-start(f32[8,1,128]{2,1,0:T(1,128)} %broadcast_in_dim.9), calls=%async_computation.3 | async-start | bytes 8192 | tf_op jit(solution)/shard_map/all_to_all | solution.py:594

commit v2 on v1

--- a/solution.py
+++ b/solution.py
@@ -16,8 +16,7 @@
 NXY = 32
 HALO_ROWS = 16
 IN_ROWS = 48
-X_ROW = 24
-MAX_ROW = 47
+SUM_LANE = 120
 OUT_ROWS = 16
 
 p0 = 0.7071067811865476
@@ -86,47 +85,24 @@
     return pltpu.roll(x, (-by) % 8, x.ndim - 2)
 
 
-class Shifts:
-    def __init__(self, *lead):
-        r, l = iota((*lead, 8, 128), len(lead)), iota((*lead, 8, 128), len(lead) + 1)
-        self.a0 = ((r >> 1) & 1) == 0
-        self.b0 = (r & 1) == 0
-        self.low = r < 4
-        self.j = l & 3
-        self.i = (l >> 2) & 7
-        self.z = l >> 5
-
-    def swap_x(self, x):
-        return jnp.where(self.a0, rows(x, 2), rows(x, -2))
-
-    def swap_y(self, x):
-        return jnp.where(self.b0, rows(x, 1), rows(x, -1))
-
-    def next(self, x, d):
-        if d == 0:
-            s = self.swap_x(x)
-            return jnp.where(self.a0, s, jnp.where(self.i < 7, lanes(s, 4), lanes(s, -28)))
-        if d == 1:
-            s = self.swap_y(x)
-            return jnp.where(self.b0, s, jnp.where(self.j < 3, lanes(s, 1), lanes(s, -3)))
-        s = lanes(x, 32)
-        t = rows(s, 4)
-        if x.ndim == 3:
-            t = jnp.where(self.low, t, jnp.concatenate([t[1:], t[:1]], axis=0))
-        return jnp.where(self.z < 3, s, t)
-
-    def prev(self, x, d):
-        if d == 0:
-            s = self.swap_x(x)
-            return jnp.where(self.a0, jnp.where(self.i > 0, lanes(s, -4), lanes(s, 28)), s)
-        if d == 1:
-            s = self.swap_y(x)
-            return jnp.where(self.b0, jnp.where(self.j > 0, lanes(s, -1), lanes(s, 3)), s)
-        s = lanes(x, -32)
-        t = rows(s, 4)
-        if x.ndim == 3:
-            t = jnp.where(self.low, jnp.concatenate([t[-1:], t[:-1]], axis=0), t)
-        return jnp.where(self.z > 0, s, t)
+def following(x, d):
+    return rows(x, 1) if d == 1 else lanes(x, 8 if d == 0 else 1)
+
+
+def preceding(x, d):
+    return rows(x, -1) if d == 1 else lanes(x, -8 if d == 0 else -1)
+
+
+def following3(x, d):
+    if d < 2:
+        return following(x, d)
+    return jnp.stack([x[1], x[2], lanes(x[0], 1)])
+
+
+def preceding3(x, d):
+    if d < 2:
+        return preceding(x, d)
+    return jnp.stack([lanes(x[2], -1), x[0], x[1]])
 
 
 def halves(x):
@@ -145,16 +121,24 @@
 
 
 def transpose_kernel(g_ref, u_ref, v_ref, x_ref, tuv_ref, tx_ref, halo_ref, uv_s, x_s):
-    zero = jnp.zeros((24, 384), jnp.float32)
-    uv_s[0:108, :] = u_ref[...]
-    uv_s[108:120, :] = v_ref[...]
-    uv_s[120:128, :] = zero[0:8, 0:128]
-    x_s[0:108, :] = x_ref[...]
-    x_s[108:128, :] = zero[0:20]
+    zero = jnp.zeros((16, 384), jnp.float32)
+    for a in range(2):
+        for m in range(27):
+            uv_s[64 * a + 2 * m : 64 * a + 2 * m + 2, :] = u_ref[m, a]
+        for d in range(3):
+            uv_s[64 * a + 54 + 2 * d : 64 * a + 56 + 2 * d, :] = v_ref[d, a]
+        uv_s[64 * a + 60 : 64 * a + 64, :] = zero[0:4, 0:128]
+        at = 64 * (1 - a)
+        for n in range(27):
+            c, kx, ky = n // 9, (n // 3) % 3, n % 3
+            for b in range(2):
+                x_s[at + 2 * n + b : at + 2 * n + b + 1, :] = x_ref[c, 3 * a + kx, ky + 3 * b : ky + 3 * b + 1, :]
+        x_s[at + 54 : at + 64, :] = zero[0:10]
     tuv_ref[...] = uv_s[...].T
     for n in range(3):
         tx_ref[128 * n : 128 * n + 128, :] = x_s[:, 128 * n : 128 * n + 128].T
-    speed = jnp.abs(v_ref[0:4, :]) + jnp.abs(v_ref[4:8, :]) + jnp.abs(v_ref[8:12, :])
+    speed = jnp.abs(v_ref[0]) + jnp.abs(v_ref[1]) + jnp.abs(v_ref[2])
+    speed = jnp.maximum(speed[0], speed[1])
     fastest = jnp.broadcast_to(jnp.max(speed, axis=(0, 1), keepdims=True), (1, 128))
     for n in range(NZ):
         halo_ref[n, :, :] = zero[0:16, 0:128]
@@ -167,7 +151,7 @@
     halo_ref[down, 9:13, :] = tx_ref[0:4, :]
 
 
-def pack_kernel(g_ref, tuv_ref, tx_ref, halo_ref, out_ref, uv_s, x_s):
+def pack_kernel(g_ref, tuv_ref, tx_ref, halo_ref, out_ref, uv_s, x_s, uv2_s, x2_s):
     below = lax.rem(g_ref[0] + NZ - 1, NZ)
     above = lax.rem(g_ref[0] + 1, NZ)
     uv_s[0:16, :] = jnp.zeros((16, 128), jnp.float32)
@@ -180,48 +164,52 @@
     uv_s[144:153, :] = halo_ref[above, 0:9, :]
     x_s[5:8, :] = halo_ref[below, 9:12, :]
     x_s[392:396, :] = halo_ref[above, 9:13, :]
+    uv2_s[...] = lanes(uv_s[...], 64)
+    x2_s[...] = lanes(x_s[...], 64)
     fastest = halo_ref[0, 13:14, :]
     for n in range(1, NZ):
         fastest = jnp.maximum(fastest, halo_ref[n, 13:14, :])
+    lane = iota((24, 128), 1)
     for k in range(NXY):
         at = IN_ROWS * k
-        out_ref[at : at + 24, :] = uv_s[4 * k + 7 : 4 * k + 31, :]
-        out_ref[at + 24 : at + 48, :] = x_s[12 * k + 5 : 12 * k + 29, :]
-        out_ref[at + MAX_ROW : at + MAX_ROW + 1, :] = fastest
-
-
-def corner_fill(ref, sh):
+        uv, x = pl.ds(4 * k + 7, 24), pl.ds(12 * k + 5, 24)
+        first = jnp.where(lane < 64, uv_s[uv, :], x_s[x, :])
+        out_ref[at : at + 24, :] = jnp.where(lane < 120, first, fastest)
+        out_ref[at + 24 : at + 48, :] = jnp.where(lane < 64, uv2_s[uv, :], x2_s[x, :])
+
+
+def corner_fill(ref):
     def one(c, carry):
         at = c * 64
         for kx in range(3):
             for ky in range(3):
-                ref[at + kx * 16 + ky * 4 + 3] = sh.next(ref[at + kx * 16 + ky * 4], 2)
+                ref[at + kx * 16 + ky * 4 + 3] = following(ref[at + kx * 16 + ky * 4], 2)
         for kx in range(3):
             for kz in range(4):
-                ref[at + kx * 16 + 12 + kz] = sh.next(ref[at + kx * 16 + kz], 1)
+                ref[at + kx * 16 + 12 + kz] = following(ref[at + kx * 16 + kz], 1)
         for ky in range(4):
             for kz in range(4):
-                ref[at + 48 + ky * 4 + kz] = sh.next(ref[at + ky * 4 + kz], 0)
+                ref[at + 48 + ky * 4 + kz] = following(ref[at + ky * 4 + kz], 0)
         return carry
 
     lax.fori_loop(0, 3, one, 0)
 
 
-def corner_fold(ref, sh):
+def corner_fold(ref):
     def one(c, carry):
         at = c * 64
         for ky in range(4):
             for kz in range(4):
                 n = at + ky * 4 + kz
-                ref[n] = ref[n] + sh.prev(ref[n + 48], 0)
+                ref[n] = ref[n] + preceding(ref[n + 48], 0)
         for kx in range(3):
             for kz in range(4):
                 n = at + kx * 16 + kz
-                ref[n] = ref[n] + sh.prev(ref[n + 12], 1)
+                ref[n] = ref[n] + preceding(ref[n + 12], 1)
         for kx in range(3):
             for ky in range(3):
                 n = at + kx * 16 + ky * 4
-                ref[n] = ref[n] + sh.prev(ref[n + 3], 2)
+                ref[n] = ref[n] + preceding(ref[n + 3], 2)
         return carry
 
     lax.fori_loop(0, 3, one, 0)
@@ -301,7 +289,7 @@
 
 def sample_sizes(u_s, size_s, a_s):
     for bc in range(9):
-        out = legendre_line([u_s[a * 9 + bc, 1] for a in range(3)])
+        out = legendre_line([u_s[8 * (a * 9 + bc) : 8 * (a * 9 + bc) + 8, :] for a in range(3)])
         for p in range(4):
             a_s[p * 9 + bc] = out[p]
     for p in range(4):
@@ -400,130 +388,167 @@
     return lax.fori_loop(0, 16, one, (zero, zero, zero))
 
 
-def remap(u_s, v_s, mid_s, face_s, time_step, sh):
+def remap(u_s, v_s, mid_s, face_s, time_step):
+    def mode(ref, m):
+        return ref[24 * m : 24 * m + 24, :].reshape(3, 8, 128)
+
+    def put(ref, m, value):
+        ref[24 * m : 24 * m + 24, :] = value.reshape(24, 128)
+
     for d in range(3):
-        v = v_s[d]
-        face = 0.5 * (v + sh.next(v, d))
-        face_s[4 * d] = 2.0 * time_step * jnp.maximum(face, 0.0)
-        face_s[4 * d + 1] = 2.0 * time_step * jnp.minimum(face, 0.0)
-        face_s[4 * d + 2] = (2.0 * root3) * time_step * v
-        face_s[4 * d + 3] = (2.0 * root15) * time_step * v
+        v = mode(v_s, d)
+        face = 0.5 * (v + following3(v, d))
+        put(face_s, 4 * d, 2.0 * time_step * jnp.maximum(face, 0.0))
+        put(face_s, 4 * d + 1, 2.0 * time_step * jnp.minimum(face, 0.0))
+        put(face_s, 4 * d + 2, (2.0 * root3) * time_step * v)
+        put(face_s, 4 * d + 3, (2.0 * root15) * time_step * v)
 
     def terms(src, d, m, step):
-        u0, u1, u2 = src[m], src[m + step], src[m + 2 * step]
+        u0, u1, u2 = mode(src, m), mode(src, m + step), mode(src, m + 2 * step)
         even = p0 * u0 + p2 * u2
         odd = p1 * u1
-        flux = face_s[4 * d] * (even + odd) + face_s[4 * d + 1] * sh.next(even - odd, d)
-        before = sh.prev(flux, d)
+        flux = mode(face_s, 4 * d) * (even + odd) + mode(face_s, 4 * d + 1) * following3(even - odd, d)
+        before = preceding3(flux, d)
         jump = before - flux
         return (
             p0 * jump,
-            face_s[4 * d + 2] * u0 - p1 * (flux + before),
-            face_s[4 * d + 3] * u1 + p2 * jump,
+            mode(face_s, 4 * d + 2) * u0 - p1 * (flux + before),
+            mode(face_s, 4 * d + 3) * u1 + p2 * jump,
         )
 
+    dims = (
+        (0, 9, range(9)),
+        (1, 3, (0, 1, 2, 9, 10, 11, 18, 19, 20)),
+        (2, 1, range(0, 27, 3)),
+    )
+
     def substep(_, carry):
-        for d, step, starts in (
-            (0, 9, range(9)),
-            (1, 3, (0, 1, 2, 9, 10, 11, 18, 19, 20)),
-            (2, 1, range(0, 27, 3)),
-        ):
+        for d, step, starts in dims:
             for m in starts:
                 for n, term in enumerate(terms(u_s, d, m, step)):
                     at = m + n * step
-                    mid_s[at] = (u_s[at] if d == 0 else mid_s[at]) + term
-        for d, step, starts in (
-            (0, 9, range(9)),
-            (1, 3, (0, 1, 2, 9, 10, 11, 18, 19, 20)),
-            (2, 1, range(0, 27, 3)),
-        ):
+                    put(mid_s, at, mode(u_s if d == 0 else mid_s, at) + term)
+        for d, step, starts in dims:
             for m in starts:
                 for n, term in enumerate(terms(mid_s, d, m, step)):
                     at = m + n * step
-                    old = 0.5 * (u_s[at] + mid_s[at]) if d == 0 else u_s[at]
-                    u_s[at] = old + 0.5 * term
+                    old = 0.5 * (mode(u_s, at) + mode(mid_s, at)) if d == 0 else mode(u_s, at)
+                    put(u_s, at, old + 0.5 * term)
         return carry
 
     lax.fori_loop(0, SUBSTEPS, substep, 0)
 
 
 def main_kernel(
-    in_ref, out_ref, t_s, u_s, v_s, mid_s, face_s, x_s, a_s, b_s, j_s, p_s, g_s, size_s
+    in_ref, out_ref, t_s, u_s, v_s, mid_s, face_s, uf_s, g3_s, x_s, a_s, b_s, j_s, p_s, g_s, size_s
 ):
-    sh = Shifts()
-    for zz in range(6):
-        stacked = jnp.concatenate(
-            [in_ref[pl.ds(4 * zz + z, NXY, stride=IN_ROWS), :] for z in range(4)], axis=0
-        )
-        t_s[...] = stacked.T
-        half = 4 * (zz % 2)
-        for m in range(27):
-            u_s[m, zz // 2, half : half + 4, :] = t_s[4 * m : 4 * m + 4, :]
-        for d in range(3):
-            v_s[d, zz // 2, half : half + 4, :] = t_s[108 + 4 * d : 112 + 4 * d, :]
-    for kz in range(3):
-        for part in range(2):
-            stacked = jnp.concatenate(
-                [
-                    in_ref[pl.ds(X_ROW + 3 * (4 * part + z) + kz, NXY, stride=IN_ROWS), :]
-                    for z in range(4)
-                ],
-                axis=0,
-            )
-            t_s[...] = stacked.T
-            half = 4 * part
-            for n in range(27):
-                c, kx, ky = n // 9, (n // 3) % 3, n % 3
-                x_s[c * 64 + kx * 16 + ky * 4 + kz, half : half + 4, :] = t_s[4 * n : 4 * n + 4, :]
-    fastest = jnp.max(in_ref[pl.ds(MAX_ROW, NXY, stride=IN_ROWS), :], axis=0, keepdims=True)
-    time_step = jnp.broadcast_to(courant / jnp.maximum(fastest, 0.25), (8, 128))
-    remap(u_s, v_s, mid_s, face_s, time_step, Shifts(3))
-
-    corner_fill(x_s, sh)
+    corners = [(n, kz, (n // 9) * 64 + ((n // 3) % 3) * 16 + (n % 3) * 4 + kz) for n in range(27) for kz in range(3)]
+    for t in range(3):
+        for j in range(4):
+            stacked = [
+                in_ref[pl.ds((4 * i + j) * IN_ROWS + 24 * a + t, 8, stride=3), :]
+                for i in range(8)
+                for a in range(2)
+            ]
+            t_s[...] = jnp.concatenate(stacked, axis=0).T
+            for b in range(2):
+                y = 2 * j + b
+                u_s[pl.ds(8 * t + y, 27, stride=24), :] = t_s[pl.ds(b, 27, stride=2), :]
+                v_s[pl.ds(8 * t + y, 3, stride=24), :] = t_s[pl.ds(54 + b, 3, stride=2), :]
+                g3_s[pl.ds(216 * t + y, 27, stride=8), :] = t_s[pl.ds(64 + b, 27, stride=2), :]
+    lane = iota((8, 128), 1)
+    fastest = jnp.max(in_ref[pl.ds(0, NXY, stride=IN_ROWS), :], axis=0, keepdims=True)
+    fastest = jnp.where(iota((1, 128), 1) < 120, 0.0, fastest)
+    fastest = jnp.broadcast_to(jnp.max(fastest, axis=1, keepdims=True), (8, 128))
+    remap(u_s, v_s, mid_s, face_s, courant / jnp.maximum(fastest, 0.25))
+
+    layer = lane & 7
+    for m in range(27):
+        u0, u1, u2 = (u_s[24 * m + 8 * t : 24 * m + 8 * t + 8, :] for t in range(3))
+        value = jnp.where(layer == 3, u2, u0)
+        value = jnp.where(layer < 2, lanes(jnp.where(layer == 2, u2, u0), 2), value)
+        value = jnp.where(layer == 2, lanes(u1, 1), value)
+        uf_s[8 * m : 8 * m + 8, :] = jnp.where(layer == 5, lanes(u1, -1), value)
+    for n, kz, at in corners:
+        x_s[at] = g3_s[216 * kz + 8 * n : 216 * kz + 8 * n + 8, :]
+    corner_fill(x_s)
     slopes_at_points(x_s, j_s, a_s, b_s)
-    sample_sizes(u_s, size_s, a_s)
+    sample_sizes(uf_s, size_s, a_s)
     energy = stress(j_s, size_s, g_s, p_s)
     points_to_corners(p_s, x_s, a_s, b_s)
-    corner_fold(x_s, sh)
-    own = jnp.where(sh.low, sh.z, 1 - sh.z) > 0
+    corner_fold(x_s)
     square = jnp.zeros((8, 128), jnp.float32)
-    for n in range(27):
-        for kz in range(3):
-            grad = x_s[(n // 9) * 64 + ((n // 3) % 3) * 16 + (n % 3) * 4 + kz]
-            square = square + grad * grad
-    corner_fill(x_s, sh)
+    for n, kz, at in corners:
+        grad = x_s[at]
+        g3_s[216 * kz + 8 * n : 216 * kz + 8 * n + 8, :] = grad
+        square = square + grad * grad
+    corner_fill(x_s)
     slopes_at_points(x_s, p_s, a_s, b_s)
     sums = (energy, square) + trial_terms(j_s, size_s, g_s, p_s)
-    t_s[108:128, :] = jnp.zeros((20, 128), jnp.float32)
+    own = jnp.abs(2 * layer - 5) < 4
+    t_s[...] = jnp.zeros((128, 128), jnp.float32)
     for n, part in enumerate(sums):
         total = jnp.sum(jnp.where(own, part, 0.0), axis=(0, 1), keepdims=True)
-        t_s[108 + n : 109 + n, :] = jnp.broadcast_to(total, (1, 128))
-    for part in range(2):
-        half = 4 * part
-        layers = ((1, 0), (2, 1), (3, 2)) if part == 0 else ((0, 3),)
+        t_s[SUM_LANE + n : SUM_LANE + 1 + n, :] = jnp.broadcast_to(total, (1, 128))
+    for p in range(2):
+        for j in range(4):
+            for b in range(2):
+                y = 2 * j + b
+                first = uf_s[pl.ds(y, 27, stride=8), :] if p == 0 else g3_s[pl.ds(216 + y, 27, stride=8), :]
+                t_s[pl.ds(b, 27, stride=2), :] = first
+                t_s[pl.ds(64 + b, 27, stride=2), :] = g3_s[pl.ds(432 * p + y, 27, stride=8), :]
+            back = t_s[...].T
+            for i in range(8):
+                for a in range(2):
+                    to = (4 * i + j) * OUT_ROWS + 8 * p + 4 * a
+                    at = (2 * i + a) * 8 + 1
+                    out_ref[to : to + 4, :] = back[at : at + 4, :]
+
+
+def unpack_kernel(in_ref, u_ref, g_ref, sums_ref, u_s, g_s):
+    def part(p, a, layer):
+        return in_ref[pl.ds(8 * p + 4 * a + layer, NXY, stride=OUT_ROWS), :]
+
+    low = iota((NXY, 128), 1) < 64
+    for layer in range(4):
+        for a in range(2):
+            u_s[pl.ds(128 * a + layer, NXY, stride=4), :] = part(0, a, layer)
+        for kz in range(3):
+            first, second = part((kz + 1) // 2, 0, layer), part((kz + 1) // 2, 1, layer)
+            if kz == 1:
+                both = jnp.where(low, first, lanes(second, 64))
+            else:
+                both = jnp.where(low, lanes(first, 64), second)
+            g_s[pl.ds(3 * layer + kz, NXY, stride=12), :] = both
+    sums_ref[...] = jnp.broadcast_to(jnp.sum(part(0, 0, 0), axis=0, keepdims=True)[None], (NZ, 1, 128))
+    for a in range(2):
+        back = u_s[128 * a : 128 * a + 128, :].T
         for m in range(27):
-            t_s[4 * m : 4 * m + 4, :] = u_s[m, 1, half : half + 4, :]
-        back = t_s[...].T
-        for z, layer in layers:
-            out_ref[pl.ds(layer, NXY, stride=OUT_ROWS), :] = back[32 * z : 32 * z + 32, :]
-        for kz in range(3):
-            for n in range(27):
-                c, kx, ky = n // 9, (n // 3) % 3, n % 3
-                t_s[4 * n : 4 * n + 4, :] = x_s[c * 64 + kx * 16 + ky * 4 + kz, half : half + 4, :]
-            back = t_s[...].T
-            for z, layer in layers:
-                out_ref[pl.ds(4 + 3 * layer + kz, NXY, stride=OUT_ROWS), :] = back[32 * z : 32 * z + 32, :]
-
-
-def unpack_kernel(in_ref, u_ref, g_ref, sums_ref, u_s, g_s):
-    for layer in range(4):
-        u_s[pl.ds(layer, NXY, stride=4), :] = in_ref[pl.ds(layer, NXY, stride=OUT_ROWS), :]
-    for r in range(12):
-        g_s[pl.ds(r, NXY, stride=12), :] = in_ref[pl.ds(4 + r, NXY, stride=OUT_ROWS), :]
-    sums_ref[...] = jnp.sum(in_ref[pl.ds(0, NXY, stride=OUT_ROWS), :], axis=0, keepdims=True)
-    u_ref[...] = u_s[...].T[0:108, :]
+            u_ref[m, a] = back[2 * m : 2 * m + 2, :]
     for n in range(3):
-        g_ref[:, 128 * n : 128 * n + 128] = g_s[128 * n : 128 * n + 128, :].T[0:108, :]
+        back = g_s[128 * n : 128 * n + 128, :].T
+        for a in range(2):
+            for q in range(27):
+                c, kx, ky = q // 9, (q // 3) % 3, q % 3
+                for b in range(2):
+                    at = 64 * a + 2 * q + b
+                    g_ref[c, 3 * a + kx, ky + 3 * b : ky + 3 * b + 1, 128 * n : 128 * n + 128] = back[at : at + 1, :]
+
+
+def checks_kernel(sums_ref, out_ref):
+    sums = sums_ref[0]
+    for n in range(1, NZ):
+        sums = sums + sums_ref[n]
+    lane = iota((1, 128), 1)
+    e0, square, e2, e3, e4 = (
+        jnp.sum(jnp.where(lane == SUM_LANE + n, sums, 0.0), axis=1, keepdims=True) for n in range(5)
+    )
+    elements = float(512 * NXY * NZ)
+    entries = 81.0 * elements
+    step = trial_step / jnp.sqrt(1.0 + square / entries)
+    trial = e0 + step * (-square + step * (e2 + step * (e3 + step * e4)))
+    for n, value in enumerate((e0 / elements, square / entries, trial / elements)):
+        out_ref[n] = value[0, 0]
 
 
 def shape(*dims):
@@ -534,15 +559,28 @@
     return pltpu.VMEM(dims, jnp.float32)
 
 
+MAIN_SCRATCH = [
+    vmem(128, 128),
+    vmem(27 * 24, 128),
+    vmem(3 * 24, 128),
+    vmem(27 * 24, 128),
+    vmem(12 * 24, 128),
+    vmem(27 * 8, 128),
+    vmem(81 * 8, 128),
+    vmem(192, 8, 128),
+    vmem(128, 8, 128),
+    vmem(192, 8, 128),
+    vmem(576, 8, 128),
+    vmem(576, 8, 128),
+    vmem(384, 8, 128),
+    vmem(64, 8, 128),
+]
 SMEM = pl.BlockSpec(memory_space=pltpu.SMEM)
 VMEM = pl.BlockSpec(memory_space=pltpu.VMEM)
 
 
 def on_device(displacement, size_field_modes, velocity):
     at_z = lax.axis_index(GZ).reshape(1).astype(jnp.int32)
-    u = size_field_modes.reshape(108, 128)
-    v = velocity.reshape(12, 128)
-    x = displacement.reshape(3, 2, 3, 2, 3, 384).transpose(0, 2, 4, 1, 3, 5).reshape(108, 384)
     tuv, tx, halo = pl.pallas_call(
         transpose_kernel,
         out_shape=(shape(128, 128), shape(384, 128), shape(NZ, HALO_ROWS, 128)),
@@ -550,14 +588,14 @@
         out_specs=(VMEM, VMEM, VMEM),
         scratch_shapes=[vmem(128, 128), vmem(128, 384)],
         name="transpose",
-    )(at_z, u, v, x)
+    )(at_z, size_field_modes, velocity, displacement)
     halo = lax.all_to_all(halo, GZ, 0, 0)
     packed = pl.pallas_call(
         pack_kernel,
         out_shape=shape(NXY * IN_ROWS, 128),
         in_specs=[SMEM, VMEM, VMEM, VMEM],
         out_specs=VMEM,
-        scratch_shapes=[vmem(160, 128), vmem(408, 128)],
+        scratch_shapes=[vmem(160, 128), vmem(408, 128), vmem(160, 128), vmem(408, 128)],
         name="pack",
     )(at_z, tuv, tx, halo)
     spread = lax.all_to_all(packed.reshape(NXY, IN_ROWS, 128), XY, 0, 0)
@@ -566,41 +604,23 @@
         out_shape=shape(NXY * OUT_ROWS, 128),
         in_specs=[VMEM],
         out_specs=VMEM,
-        scratch_shapes=[
-            vmem(128, 128),
-            vmem(27, 3, 8, 128),
-            vmem(3, 3, 8, 128),
-            vmem(27, 3, 8, 128),
-            vmem(12, 3, 8, 128),
-            vmem(192, 8, 128),
-            vmem(128, 8, 128),
-            vmem(192, 8, 128),
-            vmem(576, 8, 128),
-            vmem(576, 8, 128),
-            vmem(384, 8, 128),
-            vmem(64, 8, 128),
-        ],
+        scratch_shapes=MAIN_SCRATCH,
         name="remap_and_gradient",
     )(spread.reshape(NXY * IN_ROWS, 128))
     result = lax.all_to_all(result.reshape(NXY, OUT_ROWS, 128), XY, 0, 0)
     advected, gradient, sums = pl.pallas_call(
         unpack_kernel,
-        out_shape=(shape(108, 128), shape(108, 384), shape(1, 128)),
+        out_shape=(shape(27, 2, 2, 128), shape(3, 6, 6, 384), shape(NZ, 1, 128)),
         in_specs=[VMEM],
         out_specs=(VMEM, VMEM, VMEM),
-        scratch_shapes=[vmem(128, 128), vmem(384, 128)],
+        scratch_shapes=[vmem(256, 128), vmem(384, 128)],
         name="unpack",
     )(result.reshape(NXY * OUT_ROWS, 128))
-    sums = lax.all_to_all(jnp.broadcast_to(sums[None], (NZ, 1, 128)), GZ, 0, 0)
-    sums = jnp.sum(sums, axis=0)[0]
-    e0, square, e2, e3, e4 = (sums[108 + n] for n in range(5))
-    elements = float(512 * NXY * NZ)
-    entries = 81.0 * elements
-    step = trial_step / jnp.sqrt(1.0 + square / entries)
-    trial = e0 + step * (-square + step * (e2 + step * (e3 + step * e4)))
-    checks = jnp.stack([e0 / elements, square / entries, trial / elements])
-    gradient = gradient.reshape(3, 3, 3, 2, 2, 384).transpose(0, 3, 1, 4, 2, 5).reshape(3, 6, 6, 384)
-    return advected.reshape(27, 2, 2, 128), gradient, checks
+    sums = lax.all_to_all(sums, GZ, 0, 0)
+    checks = pl.pallas_call(
+        checks_kernel, out_shape=shape(3), in_specs=[VMEM], out_specs=SMEM, name="checks"
+    )(sums)
+    return advected, gradient, checks
 
 
 def solution(mesh):

time: 121 us -> 99.5 us (0.82)
  blocking collectives: 66.3 us -> 79.1 us
  Pallas kernels: 29.3 us -> 19.3 us
  local copies, waits for them, and re-layouts: 9.82 us -> 0 us
  waiting for transfers between devices: 5.6 us -> 0 us
  between operations: 5.23 us -> 0.64 us
  starting transfers between devices: 3.32 us -> 0 us
    all_to_all x0 -> x1, blocking collectives: none -> 12.8 us  [on_device(): sums = lax.all_to_all(sums, GZ, 0, 0)]
    pallas_call x1, Pallas kernels: 23.7 us -> 12.1 us  [on_device(): pl.pallas_call(main_kernel, out_shape=shape(NXY * OUT_ROWS, 128), in_spec...]
    all_to_all x1 -> x0, waiting for transfers between devices: 5.6 us -> none  [on_device(): sums = lax.all_to_all(jnp.broadcast_to(sums[None], (NZ, 1, 128)), GZ, 0, 0)]
    reshape x6 -> x0, local copies, waits for them, and re-layouts: 5.4 us -> none  [the longest x1 1.48 us: on_device(): u = size_field_modes.reshape(108, 128)]
    all_to_all x1 -> x0, starting transfers between devices: 3.32 us -> none  [on_device(): sums = lax.all_to_all(jnp.broadcast_to(sums[None], (NZ, 1, 128)), GZ, 0, 0)]
    unnamed x6 -> x0, local copies, waits for them, and re-layouts: 3.07 us -> none
    pallas_call x1 -> x2, Pallas kernels: 1.82 us -> 3.27 us  [the longest x1 1.93 us: on_device(): pl.pallas_call(unpack_kernel, out_shape=(shape(27, 2, 2, 128), shape(3, 6...]
  transfers between devices with their start and end apart: 1 -> 0, of which waited for: 1 -> 0; matrix products, arithmetic and copies ran while one was open for 3% -> 0% of each run, Pallas kernels for 0% -> 0%
where the time goes in v2:
time: 99.5 us; the launch traced here: 99 us
  blocking collectives  79.1 us (79%)
  Pallas kernels  19.3 us (19%)
    all_to_all x1, blocking collectives, on_device(): spread = lax.all_to_all(packed.reshape(NXY, IN_ROWS, 128), XY, 0, 0)  29.6 us
    all_to_all x1, blocking collectives, on_device(): halo = lax.all_to_all(halo, GZ, 0, 0)  20.8 us
    all_to_all x1, blocking collectives, on_device(): result = lax.all_to_all(result.reshape(NXY, OUT_ROWS, 128), XY, 0, 0)  15.9 us
    all_to_all x1, blocking collectives, on_device(): sums = lax.all_to_all(sums, GZ, 0, 0)  12.8 us
    pallas_call x1, Pallas kernels, on_device(): pl.pallas_call(main_kernel, out_shape=shape(NXY * OUT_ROWS, 128), in_spec...  12.1 us
    pallas_call x1, Pallas kernels, on_device(): pl.pallas_call(pack_kernel, out_shape=shape(NXY * IN_ROWS, 128), in_specs...  2.02 us

profile of v2, /device:TPU:1, one launch (start us, length us, event | category | flops | bytes accessed | tf_op | source)
XLA Modules:
  0.0 99.0 jit_solution(10529118526558859039)
XLA Ops:
  0.6 1.9 %transpose.1 = (f32[128,128]{1,0:T(8,128)}, f32[384,128]{1,0:T(8,128)}, f32[8,16,128]{2,1,0:T(8,128)}) custom-call(s32[1]{0:T(128)} %bitcast.g_ref, f32[27,2,2,128]{3,2,1,0:T(2,128)} %u_ref.1, f32[3,2,2,128]{3,2,1,0:T(2,128)} %v_ref.1, f32[3,6,6,384]{3,2,1,0:T(8,128)} %x_ref.1), custom_call_target="tpu_custom_call" | custom-call | tf_op jit(solution)/shard_map/transpose/pallas_call | solution.py:584
  2.5 20.8 %all_to_all.20.halo_ref = f32[8,16,128]{2,1,0:T(8,128)} all-to-all(f32[8,16,128]{2,1,0:T(8,128)} %get-tuple-element.11), channel_id=1, replica_groups=mesh['gx_0'=4,'gx_1'=2,'gy'=4,'gz_0'=4,'gz_1'=2] {'gz_0','gz_1'}, dimensions={0} | all-to-all | bytes 131072 | tf_op jit(solution)/shard_map/all_to_all | solution.py:592
  23.4 2.0 %pack.1 = f32[1536,128]{1,0:T(8,128)} custom-call(s32[1]{0:T(128)} %bitcast.g_ref, f32[128,128]{1,0:T(8,128)} %get-tuple-element.9.tuv_ref, f32[384,128]{1,0:T(8,128)} %get-tuple-element.10.tx_ref, f32[8,16,128]{2,1,0:T(8,128)} %all_to_all.20.halo_ref), custom_call_target="tpu_custom_call" | custom-call | tf_op jit(solution)/shard_map/pack/pallas_call | solution.py:593
  25.4 29.6 %all_to_all.21 = f32[32,48,128]{2,1,0:T(8,128)} all-to-all(f32[32,48,128]{2,1,0:T(8,128)} %bitcast.6), channel_id=1, replica_groups=mesh['gx_0'=4,'gx_1'=2,'gy'=4,'gz_0'=4,'gz_1'=2] {'gx_0','gx_1','gy'}, dimensions={0} | all-to-all | bytes 1572864 | tf_op jit(solution)/shard_map/all_to_all | solution.py:601
  55.0 12.1 %remap_and_gradient.1 = f32[512,128]{1,0:T(8,128)} custom-call(f32[1536,128]{1,0:T(8,128)} %bitcast.5), custom_call_target="tpu_custom_call" | custom-call | tf_op jit(solution)/shard_map/remap_and_gradient/pallas_call | solution.py:602
  67.1 15.9 %all_to_all.22 = f32[32,16,128]{2,1,0:T(8,128)} all-to-all(f32[32,16,128]{2,1,0:T(8,128)} %bitcast.8), channel_id=1, replica_groups=mesh['gx_0'=4,'gx_1'=2,'gy'=4,'gz_0'=4,'gz_1'=2] {'gx_0','gx_1','gy'}, dimensions={0} | all-to-all | bytes 524288 | tf_op jit(solution)/shard_map/all_to_all | solution.py:610
  83.0 1.9 %unpack.1 = (f32[27,2,2,128]{3,2,1,0:T(2,128)}, f32[3,6,6,384]{3,2,1,0:T(8,128)}, f32[8,1,128]{2,1,0:T(1,128)}) custom-call(f32[512,128]{1,0:T(8,128)} %bitcast.7), custom_call_target="tpu_custom_call" | custom-call | tf_op jit(solution)/shard_map/unpack/pallas_call | solution.py:611
  84.9 12.8 %all_to_all.23.sums_ref = f32[8,1,128]{2,1,0:T(1,128)} all-to-all(f32[8,1,128]{2,1,0:T(1,128)} %get-tuple-element.14), channel_id=1, replica_groups=mesh['gx_0'=4,'gx_1'=2,'gy'=4,'gz_0'=4,'gz_1'=2] {'gz_0','gz_1'}, dimensions={0} | all-to-all | bytes 8192 | tf_op jit(solution)/shard_map/all_to_all | solution.py:619
  97.7 1.3 %checks.1 = f32[3]{0:T(128)} custom-call(f32[8,1,128]{2,1,0:T(1,128)} %all_to_all.23.sums_ref), custom_call_target="tpu_custom_call" | custom-call | tf_op jit(solution)/shard_map/checks/pallas_call | solution.py:620

commit v3 on v2

--- a/solution.py
+++ b/solution.py
@@ -555,6 +555,14 @@
     return jax.ShapeDtypeStruct(dims, jnp.float32)
 
 
+def on_chip(*dims):
+    return pltpu.VMEM(dims, jnp.float32)
+
+
+def keep(x):
+    return pltpu.with_memory_space_constraint(x, pltpu.VMEM)
+
+
 def vmem(*dims):
     return pltpu.VMEM(dims, jnp.float32)
 
@@ -583,7 +591,7 @@
     at_z = lax.axis_index(GZ).reshape(1).astype(jnp.int32)
     tuv, tx, halo = pl.pallas_call(
         transpose_kernel,
-        out_shape=(shape(128, 128), shape(384, 128), shape(NZ, HALO_ROWS, 128)),
+        out_shape=(on_chip(128, 128), on_chip(384, 128), on_chip(NZ, HALO_ROWS, 128)),
         in_specs=[SMEM, VMEM, VMEM, VMEM],
         out_specs=(VMEM, VMEM, VMEM),
         scratch_shapes=[vmem(128, 128), vmem(128, 384)],
@@ -592,34 +600,34 @@
     halo = lax.all_to_all(halo, GZ, 0, 0)
     packed = pl.pallas_call(
         pack_kernel,
-        out_shape=shape(NXY * IN_ROWS, 128),
+        out_shape=on_chip(NXY * IN_ROWS, 128),
         in_specs=[SMEM, VMEM, VMEM, VMEM],
         out_specs=VMEM,
         scratch_shapes=[vmem(160, 128), vmem(408, 128), vmem(160, 128), vmem(408, 128)],
         name="pack",
-    )(at_z, tuv, tx, halo)
+    )(at_z, keep(tuv), keep(tx), keep(halo))
     spread = lax.all_to_all(packed.reshape(NXY, IN_ROWS, 128), XY, 0, 0)
     result = pl.pallas_call(
         main_kernel,
-        out_shape=shape(NXY * OUT_ROWS, 128),
+        out_shape=on_chip(NXY * OUT_ROWS, 128),
         in_specs=[VMEM],
         out_specs=VMEM,
         scratch_shapes=MAIN_SCRATCH,
         name="remap_and_gradient",
-    )(spread.reshape(NXY * IN_ROWS, 128))
+    )(keep(spread.reshape(NXY * IN_ROWS, 128)))
     result = lax.all_to_all(result.reshape(NXY, OUT_ROWS, 128), XY, 0, 0)
     advected, gradient, sums = pl.pallas_call(
         unpack_kernel,
-        out_shape=(shape(27, 2, 2, 128), shape(3, 6, 6, 384), shape(NZ, 1, 128)),
+        out_shape=(shape(27, 2, 2, 128), shape(3, 6, 6, 384), on_chip(NZ, 1, 128)),
         in_specs=[VMEM],
         out_specs=(VMEM, VMEM, VMEM),
         scratch_shapes=[vmem(256, 128), vmem(384, 128)],
         name="unpack",
-    )(result.reshape(NXY * OUT_ROWS, 128))
+    )(keep(result.reshape(NXY * OUT_ROWS, 128)))
     sums = lax.all_to_all(sums, GZ, 0, 0)
     checks = pl.pallas_call(
         checks_kernel, out_shape=shape(3), in_specs=[VMEM], out_specs=SMEM, name="checks"
-    )(sums)
+    )(keep(sums))
     return advected, gradient, checks
 
 

time: 99.5 us -> 90.8 us (0.913)
  Pallas kernels: 19.3 us -> 13.3 us
  blocking collectives: 79.1 us -> 76.6 us
    pallas_call x3, Pallas kernels: 16 us -> 11.7 us  [the longest x1 10.3 us: on_device(): pl.pallas_call(main_kernel, out_shape=on_chip(NXY * OUT_ROWS, 128), in_sp...]
    all_to_all x1, blocking collectives: 12.8 us -> 11.3 us  [on_device(): sums = lax.all_to_all(sums, GZ, 0, 0)]
where the time goes in v3:
time: 90.8 us; the launch traced here: 90.5 us
  blocking collectives  76.6 us (84%)
  Pallas kernels  13.3 us (15%)
    all_to_all x1, blocking collectives, on_device(): spread = lax.all_to_all(packed.reshape(NXY, IN_ROWS, 128), XY, 0, 0)  29.3 us
    all_to_all x1, blocking collectives, on_device(): halo = lax.all_to_all(halo, GZ, 0, 0)  20.5 us
    all_to_all x1, blocking collectives, on_device(): result = lax.all_to_all(result.reshape(NXY, OUT_ROWS, 128), XY, 0, 0)  15.5 us
    all_to_all x1, blocking collectives, on_device(): sums = lax.all_to_all(sums, GZ, 0, 0)  11.3 us
    pallas_call x1, Pallas kernels, on_device(): pl.pallas_call(main_kernel, out_shape=on_chip(NXY * OUT_ROWS, 128), in_sp...  10.3 us

profile of v3, /device:TPU:1, one launch (start us, length us, event | category | flops | bytes accessed | tf_op | source)
XLA Modules:
  0.0 90.5 jit_solution(1642760842287522557)
XLA Ops:
  0.6 1.2 %transpose.1 = (f32[128,128]{1,0:T(8,128)S(1)}, f32[384,128]{1,0:T(8,128)S(1)}, f32[8,16,128]{2,1,0:T(8,128)S(1)}) custom-call(s32[1]{0:T(128)} %bitcast.g_ref, f32[27,2,2,128]{3,2,1,0:T(2,128)} %u_ref.1, f32[3,2,2,128]{3,2,1,0:T(2,128)} %v_ref.1, f32[3,6,6,384]{3,2,1,0:T(8,128)} %x_ref.1), custom_call_target="tpu_custom_call" | custom-call | tf_op jit(solution)/shard_map/transpose/pallas_call | solution.py:592
  1.8 20.5 %all_to_all.20.halo_ref = f32[8,16,128]{2,1,0:T(8,128)S(1)} all-to-all(f32[8,16,128]{2,1,0:T(8,128)S(1)} %get-tuple-element.11), channel_id=1, replica_groups=mesh['gx_0'=4,'gx_1'=2,'gy'=4,'gz_0'=4,'gz_1'=2] {'gz_0','gz_1'}, dimensions={0} | all-to-all | bytes 131072 | tf_op jit(solution)/shard_map/all_to_all | solution.py:600
  22.4 0.2 pack.1
  22.6 29.3 %all_to_all.21 = f32[32,48,128]{2,1,0:T(8,128)S(1)} all-to-all(f32[32,48,128]{2,1,0:T(8,128)S(1)} %bitcast.6), channel_id=1, replica_groups=mesh['gx_0'=4,'gx_1'=2,'gy'=4,'gz_0'=4,'gz_1'=2] {'gx_0','gx_1','gy'}, dimensions={0} | all-to-all | bytes 1572864 | tf_op jit(solution)/shard_map/all_to_all | solution.py:609
  51.8 10.3 %remap_and_gradient.1 = f32[512,128]{1,0:T(8,128)S(1)} custom-call(f32[1536,128]{1,0:T(8,128)S(1)} %bitcast.5), custom_call_target="tpu_custom_call" | custom-call | tf_op jit(solution)/shard_map/remap_and_gradient/pallas_call | solution.py:610
  62.1 15.5 %all_to_all.22 = f32[32,16,128]{2,1,0:T(8,128)S(1)} all-to-all(f32[32,16,128]{2,1,0:T(8,128)S(1)} %bitcast.8), channel_id=1, replica_groups=mesh['gx_0'=4,'gx_1'=2,'gy'=4,'gz_0'=4,'gz_1'=2] {'gx_0','gx_1','gy'}, dimensions={0} | all-to-all | bytes 524288 | tf_op jit(solution)/shard_map/all_to_all | solution.py:618
  77.6 1.0 %unpack.1 = (f32[27,2,2,128]{3,2,1,0:T(2,128)}, f32[3,6,6,384]{3,2,1,0:T(8,128)}, f32[8,1,128]{2,1,0:T(1,128)S(1)}) custom-call(f32[512,128]{1,0:T(8,128)S(1)} %bitcast.7), custom_call_target="tpu_custom_call" | custom-call | tf_op jit(solution)/shard_map/unpack/pallas_call | solution.py:619
  78.6 11.3 %all_to_all.23.sums_ref = f32[8,1,128]{2,1,0:T(1,128)S(1)} all-to-all(f32[8,1,128]{2,1,0:T(1,128)S(1)} %get-tuple-element.14), channel_id=1, replica_groups=mesh['gx_0'=4,'gx_1'=2,'gy'=4,'gz_0'=4,'gz_1'=2] {'gz_0','gz_1'}, dimensions={0} | all-to-all | bytes 8192 | tf_op jit(solution)/shard_map/all_to_all | solution.py:627
  89.9 0.7 checks.1

commit v4 on v3

--- a/solution.py
+++ b/solution.py
@@ -15,7 +15,7 @@
 NZ = 8
 NXY = 32
 HALO_ROWS = 16
-IN_ROWS = 48
+IN_ROWS = 40
 SUM_LANE = 120
 OUT_ROWS = 16
 
@@ -151,7 +151,7 @@
     halo_ref[down, 9:13, :] = tx_ref[0:4, :]
 
 
-def pack_kernel(g_ref, tuv_ref, tx_ref, halo_ref, out_ref, uv_s, x_s, uv2_s, x2_s):
+def pack_kernel(g_ref, tuv_ref, tx_ref, halo_ref, out_ref, uv_s, x_s, uv2_s, x2_s, plus_s, minus_s):
     below = lax.rem(g_ref[0] + NZ - 1, NZ)
     above = lax.rem(g_ref[0] + 1, NZ)
     uv_s[0:16, :] = jnp.zeros((16, 128), jnp.float32)
@@ -164,18 +164,33 @@
     uv_s[144:153, :] = halo_ref[above, 0:9, :]
     x_s[5:8, :] = halo_ref[below, 9:12, :]
     x_s[392:396, :] = halo_ref[above, 9:13, :]
-    uv2_s[...] = lanes(uv_s[...], 64)
+    uv = uv_s[...]
+    uv2_s[...] = lanes(uv, 64)
     x2_s[...] = lanes(x_s[...], 64)
+    lane = iota((160, 128), 1) & 63
+    along_z = (lane >> 1) % 3
+    even = uv + (p2 / p0) * lanes(uv, 4)
+    odd = (p1 / p0) * lanes(uv, 2)
+    field = lane < 54
+    plus_s[...] = jnp.where(field, jnp.where(along_z == 0, even + odd, 0.0), jnp.where(lane >= 58, uv, 0.0))
+    minus = lanes(even - odd, -2)
+    minus_s[...] = jnp.where(field, jnp.where(along_z == 1, minus, 0.0), jnp.where(lane < 56, lanes(uv, 4), 0.0))
     fastest = halo_ref[0, 13:14, :]
     for n in range(1, NZ):
         fastest = jnp.maximum(fastest, halo_ref[n, 13:14, :])
-    lane = iota((24, 128), 1)
+    lane, row = iota((20, 128), 1), iota((20, 128), 0)
+    at_speed = jnp.where(row == 0, lane, 0) >= SUM_LANE
     for k in range(NXY):
         at = IN_ROWS * k
-        uv, x = pl.ds(4 * k + 7, 24), pl.ds(12 * k + 5, 24)
+        uv, x = pl.ds(4 * k + 8, 20), pl.ds(12 * k + 5, 20)
         first = jnp.where(lane < 64, uv_s[uv, :], x_s[x, :])
-        out_ref[at : at + 24, :] = jnp.where(lane < 120, first, fastest)
-        out_ref[at + 24 : at + 48, :] = jnp.where(lane < 64, uv2_s[uv, :], x2_s[x, :])
+        out_ref[at : at + 20, :] = jnp.where(at_speed, fastest, first)
+        out_ref[at + 20 : at + 40, :] = jnp.where(lane < 64, uv2_s[uv, :], x2_s[x, :])
+    outer = plus_s[pl.ds(7, NXY, stride=4), :] + minus_s[pl.ds(28, NXY, stride=4), :]
+    low = iota((NXY, 128), 1) < 64
+    last = pl.ds(27, NXY, stride=4)
+    out_ref[pl.ds(19, NXY, stride=IN_ROWS), :] = jnp.where(low, uv_s[last, :], lanes(outer, 64))
+    out_ref[pl.ds(39, NXY, stride=IN_ROWS), :] = jnp.where(low, uv2_s[last, :], outer)
 
 
 def corner_fill(ref):
@@ -215,31 +230,65 @@
     lax.fori_loop(0, 3, one, 0)
 
 
+def parts(x):
+    ea, eb = x[0] + x[3], x[1] + x[2]
+    return ea - eb, 0.5 * eb, x[0] - x[3], x[1] - x[2]
+
+
+def values_of(part):
+    d, half, oa, ob = part
+    out = [None] * 4
+    for p in range(2):
+        even = float(0.5 * (VALUES[p, 0] + VALUES[p, 3])) * d + half
+        odd = float(0.5 * (VALUES[p, 0] - VALUES[p, 3])) * oa + float(0.5 * (VALUES[p, 1] - VALUES[p, 2])) * ob
+        out[p], out[3 - p] = even + odd, even - odd
+    return out
+
+
+def slopes_of(part):
+    d, _, oa, ob = part
+    out = [None] * 4
+    for p in range(2):
+        even = float(0.5 * (SLOPES[p, 0] + SLOPES[p, 3])) * d
+        odd = float(0.5 * (SLOPES[p, 0] - SLOPES[p, 3])) * oa + float(0.5 * (SLOPES[p, 1] - SLOPES[p, 2])) * ob
+        out[p], out[3 - p] = even + odd, odd - even
+    return out
+
+
+def both_back(v, s):
+    (va, vb, wa, wb), (sa, sb, ta, tb) = halves(v), halves(s)
+    out = [None] * 4
+    for k in range(2):
+        first = float(0.5 * (VALUES[0, k] + VALUES[3, k])) * va + float(0.5 * (VALUES[1, k] + VALUES[2, k])) * vb
+        first = first + float(0.5 * (SLOPES[0, k] - SLOPES[3, k])) * ta + float(0.5 * (SLOPES[1, k] - SLOPES[2, k])) * tb
+        second = float(0.5 * (VALUES[0, k] - VALUES[3, k])) * wa + float(0.5 * (VALUES[1, k] - VALUES[2, k])) * wb
+        second = second + float(0.5 * (SLOPES[0, k] + SLOPES[3, k])) * sa + float(0.5 * (SLOPES[1, k] + SLOPES[2, k])) * sb
+        out[k], out[3 - k] = first + second, first - second
+    return out
+
+
 def slopes_at_points(src, dst, a_s, b_s):
     def one(c, carry):
         at = c * 64
         for line in range(16):
-            h = halves([src[at + k * 16 + line] for k in range(4)])
-            v = apply_table(VALUES, 1, h)
-            s = apply_table(SLOPES, -1, h)
+            part = parts([src[at + k * 16 + line] for k in range(4)])
+            v, s = values_of(part), slopes_of(part)
             for p in range(4):
                 a_s[p * 16 + line] = v[p]
                 a_s[64 + p * 16 + line] = s[p]
         for p in range(4):
             for kz in range(4):
-                hv = halves([a_s[p * 16 + k * 4 + kz] for k in range(4)])
-                hs = halves([a_s[64 + p * 16 + k * 4 + kz] for k in range(4)])
-                sv = apply_table(VALUES, 1, hs)
-                vs = apply_table(SLOPES, -1, hv)
-                vv = apply_table(VALUES, 1, hv)
+                pv = parts([a_s[p * 16 + k * 4 + kz] for k in range(4)])
+                ps = parts([a_s[64 + p * 16 + k * 4 + kz] for k in range(4)])
+                sv, vs, vv = values_of(ps), slopes_of(pv), values_of(pv)
                 for r in range(4):
                     b_s[p * 16 + r * 4 + kz] = sv[r]
                     b_s[64 + p * 16 + r * 4 + kz] = vs[r]
                     b_s[128 + p * 16 + r * 4 + kz] = vv[r]
         for pr in range(16):
             for col in range(3):
-                h = halves([b_s[64 * col + pr * 4 + k] for k in range(4)])
-                out = apply_table(SLOPES, -1, h) if col == 2 else apply_table(VALUES, 1, h)
+                part = parts([b_s[64 * col + pr * 4 + k] for k in range(4)])
+                out = slopes_of(part) if col == 2 else values_of(part)
                 for t in range(4):
                     dst[c * 192 + 64 * col + pr * 4 + t] = out[t]
         return carry
@@ -261,16 +310,15 @@
         for p in range(4):
             for kz in range(4):
                 sv = apply_table(values_t, 1, halves([b_s[p * 16 + r * 4 + kz] for r in range(4)]))
-                vs = apply_table(slopes_t, -1, halves([b_s[64 + p * 16 + r * 4 + kz] for r in range(4)]))
-                vv = apply_table(values_t, 1, halves([b_s[128 + p * 16 + r * 4 + kz] for r in range(4)]))
+                vs = [b_s[64 + p * 16 + r * 4 + kz] for r in range(4)]
+                v = both_back([b_s[128 + p * 16 + r * 4 + kz] for r in range(4)], vs)
                 for k in range(4):
-                    a_s[p * 16 + k * 4 + kz] = vv[k] + vs[k]
+                    a_s[p * 16 + k * 4 + kz] = v[k]
                     a_s[64 + p * 16 + k * 4 + kz] = sv[k]
         for line in range(16):
-            v = apply_table(values_t, 1, halves([a_s[p * 16 + line] for p in range(4)]))
-            s = apply_table(slopes_t, -1, halves([a_s[64 + p * 16 + line] for p in range(4)]))
+            out = both_back([a_s[p * 16 + line] for p in range(4)], [a_s[64 + p * 16 + line] for p in range(4)])
             for k in range(4):
-                dst[at + k * 16 + line] = v[k] + s[k]
+                dst[at + k * 16 + line] = out[k]
         return carry
 
     lax.fori_loop(0, 3, one, 0)
@@ -308,8 +356,12 @@
 AT = {pair: n for n, pair in enumerate(PAIRS)} | {(b, a): n for n, (a, b) in enumerate(PAIRS)}
 
 
+def dot3(x, y, at):
+    return x[at] * y[at] + x[at + 1] * y[at + 1] + x[at + 2] * y[at + 2]
+
+
 def dot6(x, y):
-    return x[0] * y[0] + x[1] * y[1] + x[2] * y[2] + 2.0 * (x[3] * y[3] + x[4] * y[4] + x[5] * y[5])
+    return dot3(x, y, 0) + 2.0 * dot3(x, y, 3)
 
 
 def weight_of(pr):
@@ -320,10 +372,7 @@
 
 
 def jacobian(j_s, q):
-    jac = [[j_s[c * 192 + col * 64 + q] for col in range(3)] for c in range(3)]
-    for c in range(3):
-        jac[c][c] = jac[c][c] + 1.0
-    return jac
+    return [[j_s[c * 192 + col * 64 + q] for col in range(3)] for c in range(3)]
 
 
 def stress(j_s, size_s, g_s, p_s):
@@ -332,6 +381,9 @@
         for t in range(4):
             q = pr * 4 + t
             jac = jacobian(j_s, q)
+            for c in range(3):
+                jac[c][c] = jac[c][c] + 1.0
+                j_s[c * 192 + c * 64 + q] = jac[c][c]
             size = size_s[q]
             inverse = 1.0 / size
             inverse2 = inverse * inverse
@@ -362,30 +414,28 @@
         for t in range(4):
             q = pr * 4 + t
             jac = jacobian(j_s, q)
-            der = [[d_s[c * 192 + col * 64 + q] for col in range(3)] for c in range(3)]
+            der = jacobian(d_s, q)
             size = size_s[q]
-            inverse = 1.0 / size
-            inverse2 = inverse * inverse
-            weighted = (pair_weight * float(WEIGHTS[t])) * size * size * size
+            point_weight = pair_weight * float(WEIGHTS[t])
             dev, first, second = [], [], []
             for n, (a, b) in enumerate(PAIRS):
                 dev.append(g_s[n * 64 + q])
-                if a == b:
-                    f = 2.0 * (jac[0][a] * der[0][a] + jac[1][a] * der[1][a] + jac[2][a] * der[2][a])
-                else:
-                    f = (
-                        jac[0][a] * der[0][b] + jac[1][a] * der[1][b] + jac[2][a] * der[2][b]
-                        + jac[0][b] * der[0][a] + jac[1][b] * der[1][a] + jac[2][b] * der[2][a]
-                    )
-                first.append(f * inverse2)
-                second.append((der[0][a] * der[0][b] + der[1][a] * der[1][b] + der[2][a] * der[2][b]) * inverse2)
-            e2 = e2 + weighted * (dot6(first, first) + 2.0 * dot6(dev, second))
-            e3 = e3 - 2.0 * weighted * dot6(first, second)
-            e4 = e4 + weighted * dot6(second, second)
+                cross = jac[0][a] * der[0][b] + jac[1][a] * der[1][b] + jac[2][a] * der[2][b]
+                if a != b:
+                    cross = cross + (jac[0][b] * der[0][a] + jac[1][b] * der[1][a] + jac[2][b] * der[2][a])
+                first.append(cross)
+                second.append(der[0][a] * der[0][b] + der[1][a] * der[1][b] + der[2][a] * der[2][b])
+            square = 2.0 * dot3(first, first, 0) + dot3(first, first, 3)
+            mixed = dot3(first, second, 0) + dot3(first, second, 3)
+            low, high = point_weight * size, point_weight / size
+            e2 = e2 + (high * square + low * dot6(dev, second))
+            e3 = e3 + high * mixed
+            e4 = e4 + high * dot6(second, second)
         return e2, e3, e4
 
     zero = jnp.zeros((8, 128), jnp.float32)
-    return lax.fori_loop(0, 16, one, (zero, zero, zero))
+    e2, e3, e4 = lax.fori_loop(0, 16, one, (zero, zero, zero))
+    return 2.0 * e2, -4.0 * e3, e4
 
 
 def remap(u_s, v_s, mid_s, face_s, time_step):
@@ -440,25 +490,42 @@
 
 
 def main_kernel(
-    in_ref, out_ref, t_s, u_s, v_s, mid_s, face_s, uf_s, g3_s, x_s, a_s, b_s, j_s, p_s, g_s, size_s
+    in_ref, out_ref, in_s, outer_s, t_s, u_s, v_s, mid_s, face_s, uf_s, g3_s, x_s, a_s, b_s, j_s, p_s, g_s, size_s
 ):
     corners = [(n, kz, (n // 9) * 64 + ((n // 3) % 3) * 16 + (n % 3) * 4 + kz) for n in range(27) for kz in range(3)]
+    in_s[0:8, :] = jnp.zeros((8, 128), jnp.float32)
+    in_s[8 : 8 + NXY * IN_ROWS, :] = in_ref[...]
+    in_s[8 + NXY * IN_ROWS : 16 + NXY * IN_ROWS, :] = jnp.zeros((8, 128), jnp.float32)
+    outer = lanes(in_ref[pl.ds(19, 2 * NXY, stride=20), :], 64)
+    lane = iota((2 * NXY, 128), 1)
+    trace = jnp.where(lane < 54, (lane >> 1) % 3, 1) == 0
+    speed = jnp.abs(2 * lane - 117) < 2
+    outer_s[0:64, :] = jnp.where(trace, outer, jnp.where(speed, outer, 0.0))
+    outer_s[64:128, :] = jnp.where(trace, lanes(outer, 2), jnp.where(speed, lanes(outer, -4), 0.0))
+    row = iota((8, 128), 0)
     for t in range(3):
         for j in range(4):
-            stacked = [
-                in_ref[pl.ds((4 * i + j) * IN_ROWS + 24 * a + t, 8, stride=3), :]
-                for i in range(8)
-                for a in range(2)
-            ]
+            stacked = []
+            for i in range(8):
+                for a in range(2):
+                    n = 2 * (4 * i + j) + a
+                    block = in_s[pl.ds(8 + 20 * n + t - 1, 8, stride=3), :]
+                    if t == 0:
+                        block = jnp.where(row == 0, outer_s[n : n + 1, :], block)
+                        block = jnp.where(row == 7, outer_s[64 + n : 65 + n, :], block)
+                    stacked.append(block)
             t_s[...] = jnp.concatenate(stacked, axis=0).T
             for b in range(2):
                 y = 2 * j + b
                 u_s[pl.ds(8 * t + y, 27, stride=24), :] = t_s[pl.ds(b, 27, stride=2), :]
                 v_s[pl.ds(8 * t + y, 3, stride=24), :] = t_s[pl.ds(54 + b, 3, stride=2), :]
-                g3_s[pl.ds(216 * t + y, 27, stride=8), :] = t_s[pl.ds(64 + b, 27, stride=2), :]
+                nodes = t_s[pl.ds(64 + b, 27, stride=2), :]
+                if t == 0:
+                    nodes = lanes(nodes, 1)
+                g3_s[pl.ds(216 * ((t + 2) % 3) + y, 27, stride=8), :] = nodes
     lane = iota((8, 128), 1)
     fastest = jnp.max(in_ref[pl.ds(0, NXY, stride=IN_ROWS), :], axis=0, keepdims=True)
-    fastest = jnp.where(iota((1, 128), 1) < 120, 0.0, fastest)
+    fastest = jnp.where(iota((1, 128), 1) < SUM_LANE, 0.0, fastest)
     fastest = jnp.broadcast_to(jnp.max(fastest, axis=1, keepdims=True), (8, 128))
     remap(u_s, v_s, mid_s, face_s, courant / jnp.maximum(fastest, 0.25))
 
@@ -482,14 +549,24 @@
         grad = x_s[at]
         g3_s[216 * kz + 8 * n : 216 * kz + 8 * n + 8, :] = grad
         square = square + grad * grad
+    own = jnp.abs(2 * layer - 5) < 4
+
+    def own_sum(x):
+        return jnp.sum(jnp.where(own, x, 0.0), axis=(0, 1), keepdims=True)
+
+    square = own_sum(square)
+    length = jnp.sqrt(1.0 + square * (1.0 / (512.0 * 81.0)))
+    shorter = jnp.broadcast_to(1.0 / length, (8, 128))
+    for n, kz, at in corners:
+        x_s[at] = x_s[at] * shorter
     corner_fill(x_s)
     slopes_at_points(x_s, p_s, a_s, b_s)
-    sums = (energy, square) + trial_terms(j_s, size_s, g_s, p_s)
-    own = jnp.abs(2 * layer - 5) < 4
+    e2, e3, e4 = trial_terms(j_s, size_s, g_s, p_s)
     t_s[...] = jnp.zeros((128, 128), jnp.float32)
-    for n, part in enumerate(sums):
-        total = jnp.sum(jnp.where(own, part, 0.0), axis=(0, 1), keepdims=True)
-        t_s[SUM_LANE + n : SUM_LANE + 1 + n, :] = jnp.broadcast_to(total, (1, 128))
+    length = jnp.broadcast_to(length, (8, 128))
+    t_s[SUM_LANE:128, :] = length
+    for n, total in enumerate((own_sum(energy), square, own_sum(e2), own_sum(e3), own_sum(e4))):
+        t_s[SUM_LANE + n : SUM_LANE + 1 + n, :] = jnp.where(layer[0:1] == 1, total, length[0:1])
     for p in range(2):
         for j in range(4):
             for b in range(2):
@@ -520,7 +597,16 @@
             else:
                 both = jnp.where(low, lanes(first, 64), second)
             g_s[pl.ds(3 * layer + kz, NXY, stride=12), :] = both
-    sums_ref[...] = jnp.broadcast_to(jnp.sum(part(0, 0, 0), axis=0, keepdims=True)[None], (NZ, 1, 128))
+    lane = iota((NXY, 128), 1)
+    length = jnp.where(lane < SUM_LANE, 1.0, part(0, 0, 1))
+    longest = jnp.max(length, axis=0, keepdims=True)
+    ratio = length / longest
+    ratio2 = ratio * ratio
+    power = jnp.where(lane < SUM_LANE + 3, ratio2, jnp.where(lane < SUM_LANE + 4, ratio2 * ratio, ratio2 * ratio2))
+    power = jnp.where(lane < SUM_LANE + 2, 1.0, power)
+    total = jnp.sum(part(0, 0, 0) * power, axis=0, keepdims=True)
+    total = jnp.where(lane[0:1] < SUM_LANE + 5, total, longest)
+    sums_ref[...] = jnp.broadcast_to(total[None], (NZ, 1, 128))
     for a in range(2):
         back = u_s[128 * a : 128 * a + 128, :].T
         for m in range(27):
@@ -536,17 +622,18 @@
 
 
 def checks_kernel(sums_ref, out_ref):
-    sums = sums_ref[0]
-    for n in range(1, NZ):
-        sums = sums + sums_ref[n]
-    lane = iota((1, 128), 1)
-    e0, square, e2, e3, e4 = (
-        jnp.sum(jnp.where(lane == SUM_LANE + n, sums, 0.0), axis=1, keepdims=True) for n in range(5)
+    sums = jnp.concatenate([sums_ref[n] for n in range(NZ)], axis=0)
+    lane = iota((NZ, 128), 1)
+    e0, square, e2, e3, e4, length = (
+        jnp.sum(jnp.where(lane == SUM_LANE + n, sums, 0.0), axis=1, keepdims=True) for n in range(6)
     )
+    e0 = jnp.sum(e0, axis=0, keepdims=True)
+    square = jnp.sum(square, axis=0, keepdims=True)
     elements = float(512 * NXY * NZ)
     entries = 81.0 * elements
     step = trial_step / jnp.sqrt(1.0 + square / entries)
-    trial = e0 + step * (-square + step * (e2 + step * (e3 + step * e4)))
+    x = step * length
+    trial = e0 - step * square + jnp.sum(x * x * (e2 + x * (e3 + x * e4)), axis=0, keepdims=True)
     for n, value in enumerate((e0 / elements, square / entries, trial / elements)):
         out_ref[n] = value[0, 0]
 
@@ -568,6 +655,8 @@
 
 
 MAIN_SCRATCH = [
+    vmem(16 + NXY * IN_ROWS, 128),
+    vmem(128, 128),
     vmem(128, 128),
     vmem(27 * 24, 128),
     vmem(3 * 24, 128),
@@ -603,7 +692,14 @@
         out_shape=on_chip(NXY * IN_ROWS, 128),
         in_specs=[SMEM, VMEM, VMEM, VMEM],
         out_specs=VMEM,
-        scratch_shapes=[vmem(160, 128), vmem(408, 128), vmem(160, 128), vmem(408, 128)],
+        scratch_shapes=[
+            vmem(160, 128),
+            vmem(408, 128),
+            vmem(160, 128),
+            vmem(408, 128),
+            vmem(160, 128),
+            vmem(160, 128),
+        ],
         name="pack",
     )(at_z, keep(tuv), keep(tx), keep(halo))
     spread = lax.all_to_all(packed.reshape(NXY, IN_ROWS, 128), XY, 0, 0)

time: 90.8 us -> 88 us (0.969)
  blocking collectives: 76.6 us -> 73.8 us
    all_to_all x1, blocking collectives: 29.3 us -> 26.7 us  [on_device(): spread = lax.all_to_all(packed.reshape(NXY, IN_ROWS, 128), XY, 0, 0)]
where the time goes in v4:
time: 88 us; the launch traced here: 87.8 us
  blocking collectives  73.8 us (84%)
  Pallas kernels  13.4 us (15%)
    all_to_all x1, blocking collectives, on_device(): spread = lax.all_to_all(packed.reshape(NXY, IN_ROWS, 128), XY, 0, 0)  26.7 us
    all_to_all x1, blocking collectives, on_device(): halo = lax.all_to_all(halo, GZ, 0, 0)  20.5 us
    all_to_all x1, blocking collectives, on_device(): result = lax.all_to_all(result.reshape(NXY, OUT_ROWS, 128), XY, 0, 0)  15.2 us
    all_to_all x1, blocking collectives, on_device(): sums = lax.all_to_all(sums, GZ, 0, 0)  11.3 us
    pallas_call x1, Pallas kernels, on_device(): pl.pallas_call(main_kernel, out_shape=on_chip(NXY * OUT_ROWS, 128), in_sp...  10.2 us

profile of v4, /device:TPU:1, one launch (start us, length us, event | category | flops | bytes accessed | tf_op | source)
XLA Modules:
  0.0 87.8 jit_solution(11041274630323055580)
XLA Ops:
  0.6 1.2 %transpose.1 = (f32[128,128]{1,0:T(8,128)S(1)}, f32[384,128]{1,0:T(8,128)S(1)}, f32[8,16,128]{2,1,0:T(8,128)S(1)}) custom-call(s32[1]{0:T(128)} %bitcast.g_ref, f32[27,2,2,128]{3,2,1,0:T(2,128)} %u_ref.1, f32[3,2,2,128]{3,2,1,0:T(2,128)} %v_ref.1, f32[3,6,6,384]{3,2,1,0:T(8,128)} %x_ref.1), custom_call_target="tpu_custom_call" | custom-call | tf_op jit(solution)/shard_map/transpose/pallas_call | solution.py:681
  1.8 20.5 %all_to_all.20.halo_ref = f32[8,16,128]{2,1,0:T(8,128)S(1)} all-to-all(f32[8,16,128]{2,1,0:T(8,128)S(1)} %get-tuple-element.11), channel_id=1, replica_groups=mesh['gx_0'=4,'gx_1'=2,'gy'=4,'gz_0'=4,'gz_1'=2] {'gz_0','gz_1'}, dimensions={0} | all-to-all | bytes 131072 | tf_op jit(solution)/shard_map/all_to_all | solution.py:689
  22.4 0.3 pack.1
  22.7 26.7 %all_to_all.21 = f32[32,40,128]{2,1,0:T(8,128)S(1)} all-to-all(f32[32,40,128]{2,1,0:T(8,128)S(1)} %bitcast.5), channel_id=1, replica_groups=mesh['gx_0'=4,'gx_1'=2,'gy'=4,'gz_0'=4,'gz_1'=2] {'gx_0','gx_1','gy'}, dimensions={0} | all-to-all | bytes 1310720 | tf_op jit(solution)/shard_map/all_to_all | solution.py:705
  49.4 10.2 %remap_and_gradient.1 = f32[512,128]{1,0:T(8,128)S(1)} custom-call(f32[1280,128]{1,0:T(8,128)S(1)} %bitcast.6), custom_call_target="tpu_custom_call" | custom-call | tf_op jit(solution)/shard_map/remap_and_gradient/pallas_call | solution.py:706
  59.6 15.2 %all_to_all.22 = f32[32,16,128]{2,1,0:T(8,128)S(1)} all-to-all(f32[32,16,128]{2,1,0:T(8,128)S(1)} %bitcast.7), channel_id=1, replica_groups=mesh['gx_0'=4,'gx_1'=2,'gy'=4,'gz_0'=4,'gz_1'=2] {'gx_0','gx_1','gy'}, dimensions={0} | all-to-all | bytes 524288 | tf_op jit(solution)/shard_map/all_to_all | solution.py:714
  74.8 1.0 %unpack.1 = (f32[27,2,2,128]{3,2,1,0:T(2,128)}, f32[3,6,6,384]{3,2,1,0:T(8,128)}, f32[8,1,128]{2,1,0:T(1,128)S(1)}) custom-call(f32[512,128]{1,0:T(8,128)S(1)} %bitcast.8), custom_call_target="tpu_custom_call" | custom-call | tf_op jit(solution)/shard_map/unpack/pallas_call | solution.py:715
  75.8 11.3 %all_to_all.23.sums_ref = f32[8,1,128]{2,1,0:T(1,128)S(1)} all-to-all(f32[8,1,128]{2,1,0:T(1,128)S(1)} %get-tuple-element.14), channel_id=1, replica_groups=mesh['gx_0'=4,'gx_1'=2,'gy'=4,'gz_0'=4,'gz_1'=2] {'gz_0','gz_1'}, dimensions={0} | all-to-all | bytes 8192 | tf_op jit(solution)/shard_map/all_to_all | solution.py:723
  87.1 0.7 checks.1

commit v5 on v4

--- a/solution.py
+++ b/solution.py
@@ -199,12 +199,12 @@
         for kx in range(3):
             for ky in range(3):
                 ref[at + kx * 16 + ky * 4 + 3] = following(ref[at + kx * 16 + ky * 4], 2)
-        for kx in range(3):
+        for ky in range(3):
+            for kz in range(4):
+                ref[at + 48 + ky * 4 + kz] = following(ref[at + ky * 4 + kz], 0)
+        for kx in range(4):
             for kz in range(4):
                 ref[at + kx * 16 + 12 + kz] = following(ref[at + kx * 16 + kz], 1)
-        for ky in range(4):
-            for kz in range(4):
-                ref[at + 48 + ky * 4 + kz] = following(ref[at + ky * 4 + kz], 0)
         return carry
 
     lax.fori_loop(0, 3, one, 0)
@@ -213,14 +213,14 @@
 def corner_fold(ref):
     def one(c, carry):
         at = c * 64
-        for ky in range(4):
+        for kx in range(4):
+            for kz in range(4):
+                n = at + kx * 16 + kz
+                ref[n] = ref[n] + preceding(ref[n + 12], 1)
+        for ky in range(3):
             for kz in range(4):
                 n = at + ky * 4 + kz
                 ref[n] = ref[n] + preceding(ref[n + 48], 0)
-        for kx in range(3):
-            for kz in range(4):
-                n = at + kx * 16 + kz
-                ref[n] = ref[n] + preceding(ref[n + 12], 1)
         for kx in range(3):
             for ky in range(3):
                 n = at + kx * 16 + ky * 4
@@ -674,6 +674,20 @@
 ]
 SMEM = pl.BlockSpec(memory_space=pltpu.SMEM)
 VMEM = pl.BlockSpec(memory_space=pltpu.VMEM)
+
+
+def near_groups():
+    groups = []
+    for z in range(4):
+        for core in range(2):
+            for x in range(4):
+                group = []
+                for y in range(4):
+                    for half in range(2):
+                        at = z if half == 0 else 3 - z
+                        group.append((((at * 2 + core) * 4 + x) * 4 + y) * 2 + half)
+                groups.append(group)
+    return groups
 
 
 def on_device(displacement, size_field_modes, velocity):
@@ -720,7 +734,7 @@
         scratch_shapes=[vmem(256, 128), vmem(384, 128)],
         name="unpack",
     )(keep(result.reshape(NXY * OUT_ROWS, 128)))
-    sums = lax.all_to_all(sums, GZ, 0, 0)
+    sums = lax.all_to_all(sums, XY + GZ, 0, 0, axis_index_groups=near_groups())
     checks = pl.pallas_call(
         checks_kernel, out_shape=shape(3), in_specs=[VMEM], out_specs=SMEM, name="checks"
     )(keep(sums))

time: 88 us -> 86 us (0.977)
  blocking collectives: 73.8 us -> 71.1 us
    all_to_all x1, blocking collectives: 11.3 us -> 8.59 us  [on_device(): sums = lax.all_to_all(sums, XY + GZ, 0, 0, axis_index_groups=near_groups())]
where the time goes in v5:
time: 86 us; the launch traced here: 85.1 us
  blocking collectives  71.1 us (83%)
  Pallas kernels  13.4 us (16%)
    all_to_all x1, blocking collectives, on_device(): spread = lax.all_to_all(packed.reshape(NXY, IN_ROWS, 128), XY, 0, 0)  26.7 us
    all_to_all x1, blocking collectives, on_device(): halo = lax.all_to_all(halo, GZ, 0, 0)  20.5 us
    all_to_all x1, blocking collectives, on_device(): result = lax.all_to_all(result.reshape(NXY, OUT_ROWS, 128), XY, 0, 0)  15.2 us
    pallas_call x1, Pallas kernels, on_device(): pl.pallas_call(main_kernel, out_shape=on_chip(NXY * OUT_ROWS, 128), in_sp...  10.2 us
    all_to_all x1, blocking collectives, on_device(): sums = lax.all_to_all(sums, XY + GZ, 0, 0, axis_index_groups=near_groups())  8.59 us

profile of v5, /device:TPU:1, one launch (start us, length us, event | category | flops | bytes accessed | tf_op | source)
XLA Modules:
  0.0 85.1 jit_solution(1294591465612336085)
XLA Ops:
  0.6 1.2 %transpose.1 = (f32[128,128]{1,0:T(8,128)S(1)}, f32[384,128]{1,0:T(8,128)S(1)}, f32[8,16,128]{2,1,0:T(8,128)S(1)}) custom-call(s32[1]{0:T(128)} %bitcast.g_ref, f32[27,2,2,128]{3,2,1,0:T(2,128)} %u_ref.1, f32[3,2,2,128]{3,2,1,0:T(2,128)} %v_ref.1, f32[3,6,6,384]{3,2,1,0:T(8,128)} %x_ref.1), custom_call_target="tpu_custom_call" | custom-call | tf_op jit(solution)/shard_map/transpose/pallas_call | solution.py:695
  1.8 20.5 %all_to_all.20.halo_ref = f32[8,16,128]{2,1,0:T(8,128)S(1)} all-to-all(f32[8,16,128]{2,1,0:T(8,128)S(1)} %get-tuple-element.11), channel_id=1, replica_groups=mesh['gx_0'=4,'gx_1'=2,'gy'=4,'gz_0'=4,'gz_1'=2] {'gz_0','gz_1'}, dimensions={0} | all-to-all | bytes 131072 | tf_op jit(solution)/shard_map/all_to_all | solution.py:703
  22.4 0.3 pack.1
  22.7 26.7 %all_to_all.21 = f32[32,40,128]{2,1,0:T(8,128)S(1)} all-to-all(f32[32,40,128]{2,1,0:T(8,128)S(1)} %bitcast.5), channel_id=1, replica_groups=mesh['gx_0'=4,'gx_1'=2,'gy'=4,'gz_0'=4,'gz_1'=2] {'gx_0','gx_1','gy'}, dimensions={0} | all-to-all | bytes 1310720 | tf_op jit(solution)/shard_map/all_to_all | solution.py:719
  49.4 10.2 %remap_and_gradient.1 = f32[512,128]{1,0:T(8,128)S(1)} custom-call(f32[1280,128]{1,0:T(8,128)S(1)} %bitcast.6), custom_call_target="tpu_custom_call" | custom-call | tf_op jit(solution)/shard_map/remap_and_gradient/pallas_call | solution.py:720
  59.6 15.2 %all_to_all.22 = f32[32,16,128]{2,1,0:T(8,128)S(1)} all-to-all(f32[32,16,128]{2,1,0:T(8,128)S(1)} %bitcast.7), channel_id=1, replica_groups=mesh['gx_0'=4,'gx_1'=2,'gy'=4,'gz_0'=4,'gz_1'=2] {'gx_0','gx_1','gy'}, dimensions={0} | all-to-all | bytes 524288 | tf_op jit(solution)/shard_map/all_to_all | solution.py:728
  74.8 1.0 %unpack.1 = (f32[27,2,2,128]{3,2,1,0:T(2,128)}, f32[3,6,6,384]{3,2,1,0:T(8,128)}, f32[8,1,128]{2,1,0:T(1,128)S(1)}) custom-call(f32[512,128]{1,0:T(8,128)S(1)} %bitcast.8), custom_call_target="tpu_custom_call" | custom-call | tf_op jit(solution)/shard_map/unpack/pallas_call | solution.py:729
  75.8 8.6 %all_to_all.23.sums_ref = f32[8,1,128]{2,1,0:T(1,128)S(1)} all-to-all(f32[8,1,128]{2,1,0:T(1,128)S(1)} %get-tuple-element.14), channel_id=1, replica_groups={{0,193,2,195,4,197,6,199},{8,201,10,203,12,205,14,207},{16,209,18,211,2..., dimensions={0} | all-to-all | bytes 8192 | tf_op jit(solution)/shard_map/all_to_all | solution.py:737
  84.4 0.7 checks.1

commit v6 on v5

--- a/solution.py
+++ b/solution.py
@@ -1,3 +1,5 @@
+from functools import partial
+
 import jax
 import jax.numpy as jnp
 import numpy as np
@@ -17,13 +19,13 @@
 HALO_ROWS = 16
 IN_ROWS = 40
 SUM_LANE = 120
+FAR_SENDER = (2, 3, 0, 1)
 OUT_ROWS = 16
 
 p0 = 0.7071067811865476
 p1 = 1.224744871391589
 p2 = 1.5811388300841898
-root3 = 1.7320508075688772
-root15 = 3.872983346207417
+SCALES = [a * b * c for a in (p0, p1, p2) for b in (p0, p1, p2) for c in (p0, p1, p2)]
 courant = 0.1
 theta_size = 0.3
 trial_step = 0.05
@@ -124,7 +126,7 @@
     zero = jnp.zeros((16, 384), jnp.float32)
     for a in range(2):
         for m in range(27):
-            uv_s[64 * a + 2 * m : 64 * a + 2 * m + 2, :] = u_ref[m, a]
+            uv_s[64 * a + 2 * m : 64 * a + 2 * m + 2, :] = SCALES[m] * u_ref[m, a]
         for d in range(3):
             uv_s[64 * a + 54 + 2 * d : 64 * a + 56 + 2 * d, :] = v_ref[d, a]
         uv_s[64 * a + 60 : 64 * a + 64, :] = zero[0:4, 0:128]
@@ -143,8 +145,9 @@
     for n in range(NZ):
         halo_ref[n, :, :] = zero[0:16, 0:128]
         halo_ref[n, 13:14, :] = fastest
-    up = lax.rem(g_ref[0] + 1, NZ)
-    down = lax.rem(g_ref[0] + NZ - 1, NZ)
+    at_z = lax.rem(g_ref[0], NZ)
+    up = lax.rem(at_z + 1, NZ)
+    down = lax.rem(at_z + NZ - 1, NZ)
     halo_ref[up, 0:9, :] = tuv_ref[119:128, :]
     halo_ref[up, 9:12, :] = tx_ref[381:384, :]
     halo_ref[down, 0:9, :] = tuv_ref[0:9, :]
@@ -152,8 +155,9 @@
 
 
 def pack_kernel(g_ref, tuv_ref, tx_ref, halo_ref, out_ref, uv_s, x_s, uv2_s, x2_s, plus_s, minus_s):
-    below = lax.rem(g_ref[0] + NZ - 1, NZ)
-    above = lax.rem(g_ref[0] + 1, NZ)
+    at_z = lax.rem(g_ref[0], NZ)
+    below = lax.rem(at_z + NZ - 1, NZ)
+    above = lax.rem(at_z + 1, NZ)
     uv_s[0:16, :] = jnp.zeros((16, 128), jnp.float32)
     uv_s[144:160, :] = jnp.zeros((16, 128), jnp.float32)
     x_s[0:8, :] = jnp.zeros((8, 128), jnp.float32)
@@ -169,8 +173,8 @@
     x2_s[...] = lanes(x_s[...], 64)
     lane = iota((160, 128), 1) & 63
     along_z = (lane >> 1) % 3
-    even = uv + (p2 / p0) * lanes(uv, 4)
-    odd = (p1 / p0) * lanes(uv, 2)
+    even = uv + lanes(uv, 4)
+    odd = lanes(uv, 2)
     field = lane < 54
     plus_s[...] = jnp.where(field, jnp.where(along_z == 0, even + odd, 0.0), jnp.where(lane >= 58, uv, 0.0))
     minus = lanes(even - odd, -2)
@@ -267,30 +271,40 @@
     return out
 
 
+def slope_pieces(src, dst, a_s, b_s, c):
+    def first(line):
+        part = parts([src[c * 64 + k * 16 + line] for k in range(4)])
+        v, s = values_of(part), slopes_of(part)
+        for p in range(4):
+            a_s[p * 16 + line] = v[p]
+            a_s[64 + p * 16 + line] = s[p]
+
+    def second(p, kz):
+        pv = parts([a_s[p * 16 + k * 4 + kz] for k in range(4)])
+        ps = parts([a_s[64 + p * 16 + k * 4 + kz] for k in range(4)])
+        sv, vs, vv = values_of(ps), slopes_of(pv), values_of(pv)
+        for r in range(4):
+            b_s[p * 16 + r * 4 + kz] = sv[r]
+            b_s[64 + p * 16 + r * 4 + kz] = vs[r]
+            b_s[128 + p * 16 + r * 4 + kz] = vv[r]
+
+    def third(pr, col):
+        part = parts([b_s[64 * col + pr * 4 + k] for k in range(4)])
+        out = slopes_of(part) if col == 2 else values_of(part)
+        for t in range(4):
+            dst[c * 192 + 64 * col + pr * 4 + t] = out[t]
+
+    return (
+        [partial(first, line) for line in range(16)]
+        + [partial(second, p, kz) for p in range(4) for kz in range(4)]
+        + [partial(third, pr, col) for pr in range(16) for col in range(3)]
+    )
+
+
 def slopes_at_points(src, dst, a_s, b_s):
     def one(c, carry):
-        at = c * 64
-        for line in range(16):
-            part = parts([src[at + k * 16 + line] for k in range(4)])
-            v, s = values_of(part), slopes_of(part)
-            for p in range(4):
-                a_s[p * 16 + line] = v[p]
-                a_s[64 + p * 16 + line] = s[p]
-        for p in range(4):
-            for kz in range(4):
-                pv = parts([a_s[p * 16 + k * 4 + kz] for k in range(4)])
-                ps = parts([a_s[64 + p * 16 + k * 4 + kz] for k in range(4)])
-                sv, vs, vv = values_of(ps), slopes_of(pv), values_of(pv)
-                for r in range(4):
-                    b_s[p * 16 + r * 4 + kz] = sv[r]
-                    b_s[64 + p * 16 + r * 4 + kz] = vs[r]
-                    b_s[128 + p * 16 + r * 4 + kz] = vv[r]
-        for pr in range(16):
-            for col in range(3):
-                part = parts([b_s[64 * col + pr * 4 + k] for k in range(4)])
-                out = slopes_of(part) if col == 2 else values_of(part)
-                for t in range(4):
-                    dst[c * 192 + 64 * col + pr * 4 + t] = out[t]
+        for piece in slope_pieces(src, dst, a_s, b_s, c):
+            piece()
         return carry
 
     lax.fori_loop(0, 3, one, 0)
@@ -325,11 +339,10 @@
 
 
 def legendre_line(u):
-    base = p0 * u[0]
     out = [None] * 4
     for p in range(2):
-        even = base + float(LEGENDRE[p, 2]) * u[2]
-        odd = float(LEGENDRE[p, 1]) * u[1]
+        even = u[0] + float(LEGENDRE[p, 2] / p2) * u[2]
+        odd = float(LEGENDRE[p, 1] / p1) * u[1]
         out[p] = even + odd
         out[3 - p] = even - odd
     return out
@@ -438,7 +451,7 @@
     return 2.0 * e2, -4.0 * e3, e4
 
 
-def remap(u_s, v_s, mid_s, face_s, time_step):
+def remap(u_s, v_s, mid_s, face_s, time_step, pieces):
     def mode(ref, m):
         return ref[24 * m : 24 * m + 24, :].reshape(3, 8, 128)
 
@@ -448,55 +461,73 @@
     for d in range(3):
         v = mode(v_s, d)
         face = 0.5 * (v + following3(v, d))
-        put(face_s, 4 * d, 2.0 * time_step * jnp.maximum(face, 0.0))
-        put(face_s, 4 * d + 1, 2.0 * time_step * jnp.minimum(face, 0.0))
-        put(face_s, 4 * d + 2, (2.0 * root3) * time_step * v)
-        put(face_s, 4 * d + 3, (2.0 * root15) * time_step * v)
-
-    def terms(src, d, m, step):
-        u0, u1, u2 = mode(src, m), mode(src, m + step), mode(src, m + 2 * step)
-        even = p0 * u0 + p2 * u2
-        odd = p1 * u1
-        flux = mode(face_s, 4 * d) * (even + odd) + mode(face_s, 4 * d + 1) * following3(even - odd, d)
+        for stage, part in ((0, time_step), (1, 0.5 * time_step)):
+            at = 12 * stage + 4 * d
+            put(face_s, at, part * jnp.maximum(face, 0.0))
+            put(face_s, at + 1, part * jnp.minimum(face, 0.0))
+            put(face_s, at + 2, 6.0 * part * v)
+            put(face_s, at + 3, 10.0 * part * v)
+
+    def terms(w, d, stage):
+        at = 12 * stage + 4 * d
+        even = w[0] + w[2]
+        flux = mode(face_s, at) * (even + w[1]) + mode(face_s, at + 1) * following3(even - w[1], d)
         before = preceding3(flux, d)
         jump = before - flux
         return (
-            p0 * jump,
-            mode(face_s, 4 * d + 2) * u0 - p1 * (flux + before),
-            mode(face_s, 4 * d + 3) * u1 + p2 * jump,
+            jump,
+            mode(face_s, at + 2) * w[0] - 3.0 * (flux + before),
+            mode(face_s, at + 3) * w[1] + 5.0 * jump,
         )
 
-    dims = (
-        (0, 9, range(9)),
-        (1, 3, (0, 1, 2, 9, 10, 11, 18, 19, 20)),
-        (2, 1, range(0, 27, 3)),
-    )
-
-    def substep(_, carry):
-        for d, step, starts in dims:
-            for m in starts:
-                for n, term in enumerate(terms(u_s, d, m, step)):
-                    at = m + n * step
-                    put(mid_s, at, mode(u_s if d == 0 else mid_s, at) + term)
-        for d, step, starts in dims:
-            for m in starts:
-                for n, term in enumerate(terms(mid_s, d, m, step)):
-                    at = m + n * step
-                    old = 0.5 * (mode(u_s, at) + mode(mid_s, at)) if d == 0 else mode(u_s, at)
-                    put(u_s, at, old + 0.5 * term)
-        return carry
-
-    lax.fori_loop(0, SUBSTEPS, substep, 0)
+    def spare(upto):
+        while done[0] < upto * len(pieces):
+            pieces[done[0]]()
+            done[0] += 1
+
+    done = [0]
+    for n in range(SUBSTEPS):
+        for stage, src, dst in ((0, u_s, mid_s), (1, mid_s, u_s)):
+            at = (2 * n + stage) / (2.0 * SUBSTEPS)
+            for m in range(9):
+                w = [mode(src, m + 9 * k) for k in range(3)]
+                for k, term in enumerate(terms(w, 0, stage)):
+                    old = w[k] if stage == 0 else 0.5 * (mode(u_s, m + 9 * k) + w[k])
+                    put(dst, m + 9 * k, old + term)
+                spare(at + (m + 1) / 27.0 / (2.0 * SUBSTEPS))
+            for a in range(3):
+                w = [[mode(src, 9 * a + 3 * b + c) for c in range(3)] for b in range(3)]
+                acc = [list(terms(w[b], 2, stage)) for b in range(3)]
+                spare(at + (9 + 6 * a + 3) / 27.0 / (2.0 * SUBSTEPS))
+                for c in range(3):
+                    for b, term in enumerate(terms([w[b][c] for b in range(3)], 1, stage)):
+                        acc[b][c] = acc[b][c] + term
+                for b in range(3):
+                    for c in range(3):
+                        m = 9 * a + 3 * b + c
+                        put(dst, m, mode(dst, m) + acc[b][c])
+                spare(at + (9 + 6 * a + 6) / 27.0 / (2.0 * SUBSTEPS))
+    spare(1.0)
 
 
 def main_kernel(
-    in_ref, out_ref, in_s, outer_s, t_s, u_s, v_s, mid_s, face_s, uf_s, g3_s, x_s, a_s, b_s, j_s, p_s, g_s, size_s
+    g_ref, in_ref, out_ref, in_s, outer_s, t_s, u_s, v_s, mid_s, face_s, uf_s, g3_s, x_s, a_s, b_s, j_s, p_s, g_s, size_s
 ):
     corners = [(n, kz, (n // 9) * 64 + ((n // 3) % 3) * 16 + (n % 3) * 4 + kz) for n in range(27) for kz in range(3)]
     in_s[0:8, :] = jnp.zeros((8, 128), jnp.float32)
-    in_s[8 : 8 + NXY * IN_ROWS, :] = in_ref[...]
+    chunk = lax.div(g_ref[0], NZ)
+    lane, row = iota((IN_ROWS, 128), 1), iota((IN_ROWS, 128), 0) % 20
+    high = lane - 64
+    layer = jnp.where(lane < 64, 4 * chunk - 8 + row, (12 * chunk - 3 + row + 384) // 3 - 128)
+    upper = jnp.where(high < 54, (high >> 1) % 3, jnp.where(high < 56, 1, 0)) == 1
+    layer = jnp.where((row == 19) & (lane >= 64), jnp.where(upper, 4 * chunk + 12, 4 * chunk - 9), layer)
+    beyond = jnp.abs(2 * layer - 127) > 128
+    for n in range(NXY):
+        other = (2 * FAR_SENDER[n // 8] + (n // 4) % 2) * 4 + n % 4
+        own, far = in_ref[IN_ROWS * n : IN_ROWS * n + IN_ROWS, :], in_ref[IN_ROWS * other : IN_ROWS * other + IN_ROWS, :]
+        in_s[8 + IN_ROWS * n : 8 + IN_ROWS * n + IN_ROWS, :] = jnp.where(beyond, far, own)
     in_s[8 + NXY * IN_ROWS : 16 + NXY * IN_ROWS, :] = jnp.zeros((8, 128), jnp.float32)
-    outer = lanes(in_ref[pl.ds(19, 2 * NXY, stride=20), :], 64)
+    outer = lanes(in_s[pl.ds(8 + 19, 2 * NXY, stride=20), :], 64)
     lane = iota((2 * NXY, 128), 1)
     trace = jnp.where(lane < 54, (lane >> 1) % 3, 1) == 0
     speed = jnp.abs(2 * lane - 117) < 2
@@ -527,7 +558,11 @@
     fastest = jnp.max(in_ref[pl.ds(0, NXY, stride=IN_ROWS), :], axis=0, keepdims=True)
     fastest = jnp.where(iota((1, 128), 1) < SUM_LANE, 0.0, fastest)
     fastest = jnp.broadcast_to(jnp.max(fastest, axis=1, keepdims=True), (8, 128))
-    remap(u_s, v_s, mid_s, face_s, courant / jnp.maximum(fastest, 0.25))
+    for n, kz, at in corners:
+        x_s[at] = g3_s[216 * kz + 8 * n : 216 * kz + 8 * n + 8, :]
+    corner_fill(x_s)
+    pieces = [piece for c in range(3) for piece in slope_pieces(x_s, j_s, a_s, b_s, c)]
+    remap(u_s, v_s, mid_s, face_s, courant / jnp.maximum(fastest, 0.25), pieces)
 
     layer = lane & 7
     for m in range(27):
@@ -536,11 +571,9 @@
         value = jnp.where(layer < 2, lanes(jnp.where(layer == 2, u2, u0), 2), value)
         value = jnp.where(layer == 2, lanes(u1, 1), value)
         uf_s[8 * m : 8 * m + 8, :] = jnp.where(layer == 5, lanes(u1, -1), value)
-    for n, kz, at in corners:
-        x_s[at] = g3_s[216 * kz + 8 * n : 216 * kz + 8 * n + 8, :]
-    corner_fill(x_s)
-    slopes_at_points(x_s, j_s, a_s, b_s)
     sample_sizes(uf_s, size_s, a_s)
+    for m in range(27):
+        uf_s[8 * m : 8 * m + 8, :] = (1.0 / SCALES[m]) * uf_s[8 * m : 8 * m + 8, :]
     energy = stress(j_s, size_s, g_s, p_s)
     points_to_corners(p_s, x_s, a_s, b_s)
     corner_fold(x_s)
@@ -661,7 +694,7 @@
     vmem(27 * 24, 128),
     vmem(3 * 24, 128),
     vmem(27 * 24, 128),
-    vmem(12 * 24, 128),
+    vmem(24 * 24, 128),
     vmem(27 * 8, 128),
     vmem(81 * 8, 128),
     vmem(192, 8, 128),
@@ -676,7 +709,7 @@
 VMEM = pl.BlockSpec(memory_space=pltpu.VMEM)
 
 
-def near_groups():
+def near_groups(partner):
     groups = []
     for z in range(4):
         for core in range(2):
@@ -684,14 +717,14 @@
                 group = []
                 for y in range(4):
                     for half in range(2):
-                        at = z if half == 0 else 3 - z
+                        at = z if half == 0 else partner[z]
                         group.append((((at * 2 + core) * 4 + x) * 4 + y) * 2 + half)
                 groups.append(group)
     return groups
 
 
 def on_device(displacement, size_field_modes, velocity):
-    at_z = lax.axis_index(GZ).reshape(1).astype(jnp.int32)
+    place = (lax.axis_index(XY) * NZ + lax.axis_index(GZ)).reshape(1).astype(jnp.int32)
     tuv, tx, halo = pl.pallas_call(
         transpose_kernel,
         out_shape=(on_chip(128, 128), on_chip(384, 128), on_chip(NZ, HALO_ROWS, 128)),
@@ -699,8 +732,8 @@
         out_specs=(VMEM, VMEM, VMEM),
         scratch_shapes=[vmem(128, 128), vmem(128, 384)],
         name="transpose",
-    )(at_z, size_field_modes, velocity, displacement)
-    halo = lax.all_to_all(halo, GZ, 0, 0)
+    )(place, size_field_modes, velocity, displacement)
+    halo = lax.all_to_all(halo, XY + GZ, 0, 0, axis_index_groups=near_groups(FAR_SENDER))
     packed = pl.pallas_call(
         pack_kernel,
         out_shape=on_chip(NXY * IN_ROWS, 128),
@@ -715,16 +748,16 @@
             vmem(160, 128),
         ],
         name="pack",
-    )(at_z, keep(tuv), keep(tx), keep(halo))
+    )(place, keep(tuv), keep(tx), keep(halo))
     spread = lax.all_to_all(packed.reshape(NXY, IN_ROWS, 128), XY, 0, 0)
     result = pl.pallas_call(
         main_kernel,
         out_shape=on_chip(NXY * OUT_ROWS, 128),
-        in_specs=[VMEM],
+        in_specs=[SMEM, VMEM],
         out_specs=VMEM,
         scratch_shapes=MAIN_SCRATCH,
         name="remap_and_gradient",
-    )(keep(spread.reshape(NXY * IN_ROWS, 128)))
+    )(place, keep(spread.reshape(NXY * IN_ROWS, 128)))
     result = lax.all_to_all(result.reshape(NXY, OUT_ROWS, 128), XY, 0, 0)
     advected, gradient, sums = pl.pallas_call(
         unpack_kernel,
@@ -734,7 +767,7 @@
         scratch_shapes=[vmem(256, 128), vmem(384, 128)],
         name="unpack",
     )(keep(result.reshape(NXY * OUT_ROWS, 128)))
-    sums = lax.all_to_all(sums, XY + GZ, 0, 0, axis_index_groups=near_groups())
+    sums = lax.all_to_all(sums, XY + GZ, 0, 0, axis_index_groups=near_groups((3, 2, 1, 0)))
     checks = pl.pallas_call(
         checks_kernel, out_shape=shape(3), in_specs=[VMEM], out_specs=SMEM, name="checks"
     )(keep(sums))

time: 86 us -> 82.9 us (0.964)
  blocking collectives: 71.1 us -> 68.3 us
    all_to_all x2, blocking collectives: 29.1 us -> 26.4 us  [the longest x1 17.8 us: on_device(): lax.all_to_all(halo, XY + GZ, 0, 0, axis_index_groups=near_groups(FAR_SEN...]
where the time goes in v6:
time: 82.9 us; the launch traced here: 82 us
  blocking collectives  68.3 us (82%)
  Pallas kernels  12.9 us (16%)
    all_to_all x1, blocking collectives, on_device(): spread = lax.all_to_all(packed.reshape(NXY, IN_ROWS, 128), XY, 0, 0)  26.7 us
    all_to_all x1, blocking collectives, on_device(): lax.all_to_all(halo, XY + GZ, 0, 0, axis_index_groups=near_groups(FAR_SEN...  17.8 us
    all_to_all x1, blocking collectives, on_device(): result = lax.all_to_all(result.reshape(NXY, OUT_ROWS, 128), XY, 0, 0)  15.2 us
    pallas_call x1, Pallas kernels, on_device(): pl.pallas_call(main_kernel, out_shape=on_chip(NXY * OUT_ROWS, 128), in_sp...  9.76 us
    all_to_all x1, blocking collectives, on_device(): lax.all_to_all(sums, XY + GZ, 0, 0, axis_index_groups=near_groups((3, 2,...  8.59 us

profile of v6, /device:TPU:1, one launch (start us, length us, event | category | flops | bytes accessed | tf_op | source)
XLA Modules:
  0.0 82.0 jit_solution(11087792845642241111)
XLA Ops:
  0.6 1.2 %transpose.1 = (f32[128,128]{1,0:T(8,128)S(1)}, f32[384,128]{1,0:T(8,128)S(1)}, f32[8,16,128]{2,1,0:T(8,128)S(1)}) custom-call(s32[1]{0:T(128)} %bitcast.g_ref, f32[27,2,2,128]{3,2,1,0:T(2,128)} %u_ref.1, f32[3,2,2,128]{3,2,1,0:T(2,128)} %v_ref.1, f32[3,6,6,384]{3,2,1,0:T(8,128)} %x_ref.1), custom_call_target="tpu_custom_call" | custom-call | tf_op jit(solution)/shard_map/transpose/pallas_call | solution.py:728
  1.8 17.8 %all_to_all.20.halo_ref = f32[8,16,128]{2,1,0:T(8,128)S(1)} all-to-all(f32[8,16,128]{2,1,0:T(8,128)S(1)} %get-tuple-element.11), channel_id=1, replica_groups={{0,129,2,131,4,133,6,135},{8,137,10,139,12,141,14,143},{16,145,18,147,2..., dimensions={0} | all-to-all | bytes 131072 | tf_op jit(solution)/shard_map/all_to_all | solution.py:736
  19.7 0.3 pack.1
  20.0 26.7 %all_to_all.21 = f32[32,40,128]{2,1,0:T(8,128)S(1)} all-to-all(f32[32,40,128]{2,1,0:T(8,128)S(1)} %bitcast.5), channel_id=1, replica_groups=mesh['gx_0'=4,'gx_1'=2,'gy'=4,'gz_0'=4,'gz_1'=2] {'gx_0','gx_1','gy'}, dimensions={0} | all-to-all | bytes 1310720 | tf_op jit(solution)/shard_map/all_to_all | solution.py:752
  46.7 9.8 %remap_and_gradient.1 = f32[512,128]{1,0:T(8,128)S(1)} custom-call(s32[1]{0:T(128)} %bitcast.g_ref, f32[1280,128]{1,0:T(8,128)S(1)} %bitcast.6), custom_call_target="tpu_custom_call" | custom-call | tf_op jit(solution)/shard_map/remap_and_gradient/pallas_call | solution.py:753
  56.5 15.2 %all_to_all.22 = f32[32,16,128]{2,1,0:T(8,128)S(1)} all-to-all(f32[32,16,128]{2,1,0:T(8,128)S(1)} %bitcast.7), channel_id=1, replica_groups=mesh['gx_0'=4,'gx_1'=2,'gy'=4,'gz_0'=4,'gz_1'=2] {'gx_0','gx_1','gy'}, dimensions={0} | all-to-all | bytes 524288 | tf_op jit(solution)/shard_map/all_to_all | solution.py:761
  71.7 1.0 %unpack.1 = (f32[27,2,2,128]{3,2,1,0:T(2,128)}, f32[3,6,6,384]{3,2,1,0:T(8,128)}, f32[8,1,128]{2,1,0:T(1,128)S(1)}) custom-call(f32[512,128]{1,0:T(8,128)S(1)} %bitcast.8), custom_call_target="tpu_custom_call" | custom-call | tf_op jit(solution)/shard_map/unpack/pallas_call | solution.py:762
  72.7 8.6 %all_to_all.23.sums_ref = f32[8,1,128]{2,1,0:T(1,128)S(1)} all-to-all(f32[8,1,128]{2,1,0:T(1,128)S(1)} %get-tuple-element.14), channel_id=1, replica_groups={{0,193,2,195,4,197,6,199},{8,201,10,203,12,205,14,207},{16,209,18,211,2..., dimensions={0} | all-to-all | bytes 8192 | tf_op jit(solution)/shard_map/all_to_all | solution.py:770
  81.3 0.7 checks.1

commit v7 on v6

--- a/solution.py
+++ b/solution.py
@@ -259,12 +259,21 @@
     return out
 
 
+def slopes_back(s):
+    sa, sb, ta, tb = halves(s)
+    odd = float(0.5 * (SLOPES[0, 0] - SLOPES[3, 0])) * ta + float(0.5 * (SLOPES[1, 0] - SLOPES[2, 0])) * tb
+    e0 = float(0.5 * (SLOPES[0, 0] + SLOPES[3, 0])) * sa + float(0.5 * (SLOPES[1, 0] + SLOPES[2, 0])) * sb
+    e1 = float(0.5 * (SLOPES[0, 1] + SLOPES[3, 1])) * sa + float(0.5 * (SLOPES[1, 1] + SLOPES[2, 1])) * sb
+    return [odd + e0, e1 - odd, -odd - e1, odd - e0]
+
+
 def both_back(v, s):
     (va, vb, wa, wb), (sa, sb, ta, tb) = halves(v), halves(s)
+    odd = float(0.5 * (SLOPES[0, 0] - SLOPES[3, 0])) * ta + float(0.5 * (SLOPES[1, 0] - SLOPES[2, 0])) * tb
     out = [None] * 4
     for k in range(2):
         first = float(0.5 * (VALUES[0, k] + VALUES[3, k])) * va + float(0.5 * (VALUES[1, k] + VALUES[2, k])) * vb
-        first = first + float(0.5 * (SLOPES[0, k] - SLOPES[3, k])) * ta + float(0.5 * (SLOPES[1, k] - SLOPES[2, k])) * tb
+        first = first + odd if k == 0 else first - odd
         second = float(0.5 * (VALUES[0, k] - VALUES[3, k])) * wa + float(0.5 * (VALUES[1, k] - VALUES[2, k])) * wb
         second = second + float(0.5 * (SLOPES[0, k] + SLOPES[3, k])) * sa + float(0.5 * (SLOPES[1, k] + SLOPES[2, k])) * sb
         out[k], out[3 - k] = first + second, first - second
@@ -301,24 +310,15 @@
     )
 
 
-def slopes_at_points(src, dst, a_s, b_s):
-    def one(c, carry):
-        for piece in slope_pieces(src, dst, a_s, b_s, c):
-            piece()
-        return carry
-
-    lax.fori_loop(0, 3, one, 0)
-
-
 def points_to_corners(src, dst, a_s, b_s):
-    values_t, slopes_t = VALUES.T, SLOPES.T
+    values_t = VALUES.T
 
     def one(c, carry):
         at = c * 64
         for pr in range(16):
             for col in range(3):
-                h = halves([src[c * 192 + 64 * col + pr * 4 + t] for t in range(4)])
-                out = apply_table(slopes_t, -1, h) if col == 2 else apply_table(values_t, 1, h)
+                at_points = [src[c * 192 + 64 * col + pr * 4 + t] for t in range(4)]
+                out = slopes_back(at_points) if col == 2 else apply_table(values_t, 1, halves(at_points))
                 for k in range(4):
                     b_s[64 * col + pr * 4 + k] = out[k]
         for p in range(4):
@@ -390,9 +390,10 @@
 
 def stress(j_s, size_s, g_s, p_s):
     def one(pr, energy):
-        pair_weight = weight_of(pr)
-        for t in range(4):
-            q = pr * 4 + t
+        weights = [weight_of(2 * pr), weight_of(2 * pr + 1)]
+        for t in range(8):
+            q = pr * 8 + t
+            pair_weight = weights[t // 4]
             jac = jacobian(j_s, q)
             for c in range(3):
                 jac[c][c] = jac[c][c] + 1.0
@@ -400,7 +401,7 @@
             size = size_s[q]
             inverse = 1.0 / size
             inverse2 = inverse * inverse
-            weighted = (pair_weight * float(WEIGHTS[t])) * size
+            weighted = (pair_weight * float(WEIGHTS[t % 4])) * size
             dev = []
             for n, (a, b) in enumerate(PAIRS):
                 gram = (jac[0][a] * jac[0][b] + jac[1][a] * jac[1][b] + jac[2][a] * jac[2][b]) * inverse2
@@ -417,19 +418,20 @@
                     )
         return energy
 
-    return lax.fori_loop(0, 16, one, jnp.zeros((8, 128), jnp.float32))
+    return lax.fori_loop(0, 8, one, jnp.zeros((8, 128), jnp.float32))
 
 
 def trial_terms(j_s, size_s, g_s, d_s):
     def one(pr, sums):
         e2, e3, e4 = sums
-        pair_weight = weight_of(pr)
-        for t in range(4):
-            q = pr * 4 + t
+        weights = [weight_of(2 * pr), weight_of(2 * pr + 1)]
+        for t in range(8):
+            q = pr * 8 + t
+            pair_weight = weights[t // 4]
             jac = jacobian(j_s, q)
             der = jacobian(d_s, q)
             size = size_s[q]
-            point_weight = pair_weight * float(WEIGHTS[t])
+            point_weight = pair_weight * float(WEIGHTS[t % 4])
             dev, first, second = [], [], []
             for n, (a, b) in enumerate(PAIRS):
                 dev.append(g_s[n * 64 + q])
@@ -447,7 +449,7 @@
         return e2, e3, e4
 
     zero = jnp.zeros((8, 128), jnp.float32)
-    e2, e3, e4 = lax.fori_loop(0, 16, one, (zero, zero, zero))
+    e2, e3, e4 = lax.fori_loop(0, 8, one, (zero, zero, zero))
     return 2.0 * e2, -4.0 * e3, e4
 
 
@@ -593,26 +595,33 @@
     for n, kz, at in corners:
         x_s[at] = x_s[at] * shorter
     corner_fill(x_s)
-    slopes_at_points(x_s, p_s, a_s, b_s)
+
+    def pack_back(p, j):
+        for b in range(2):
+            y = 2 * j + b
+            first = uf_s[pl.ds(y, 27, stride=8), :] if p == 0 else g3_s[pl.ds(216 + y, 27, stride=8), :]
+            t_s[pl.ds(b, 27, stride=2), :] = first
+            t_s[pl.ds(64 + b, 27, stride=2), :] = g3_s[pl.ds(432 * p + y, 27, stride=8), :]
+        back = t_s[...].T
+        for i in range(8):
+            for a in range(2):
+                to = (4 * i + j) * OUT_ROWS + 8 * p + 4 * a
+                at = (2 * i + a) * 8 + 1
+                out_ref[to : to + 4, :] = back[at : at + 4, :]
+
+    pieces = [piece for c in range(3) for piece in slope_pieces(x_s, p_s, a_s, b_s, c)]
+    for n, piece in enumerate(pieces):
+        piece()
+        if n % 60 == 30:
+            pack_back(1, n // 60)
     e2, e3, e4 = trial_terms(j_s, size_s, g_s, p_s)
     t_s[...] = jnp.zeros((128, 128), jnp.float32)
     length = jnp.broadcast_to(length, (8, 128))
     t_s[SUM_LANE:128, :] = length
     for n, total in enumerate((own_sum(energy), square, own_sum(e2), own_sum(e3), own_sum(e4))):
         t_s[SUM_LANE + n : SUM_LANE + 1 + n, :] = jnp.where(layer[0:1] == 1, total, length[0:1])
-    for p in range(2):
-        for j in range(4):
-            for b in range(2):
-                y = 2 * j + b
-                first = uf_s[pl.ds(y, 27, stride=8), :] if p == 0 else g3_s[pl.ds(216 + y, 27, stride=8), :]
-                t_s[pl.ds(b, 27, stride=2), :] = first
-                t_s[pl.ds(64 + b, 27, stride=2), :] = g3_s[pl.ds(432 * p + y, 27, stride=8), :]
-            back = t_s[...].T
-            for i in range(8):
-                for a in range(2):
-                    to = (4 * i + j) * OUT_ROWS + 8 * p + 4 * a
-                    at = (2 * i + a) * 8 + 1
-                    out_ref[to : to + 4, :] = back[at : at + 4, :]
+    for j in range(4):
+        pack_back(0, j)
 
 
 def unpack_kernel(in_ref, u_ref, g_ref, sums_ref, u_s, g_s):

time: 82.9 us -> 82.7 us (level)
  no operation moved by 1% of the time
where the time goes in v7:
time: 82.7 us; the launch traced here: 81.7 us
  blocking collectives  68.3 us (83%)
  Pallas kernels  12.7 us (15%)
    all_to_all x1, blocking collectives, on_device(): spread = lax.all_to_all(packed.reshape(NXY, IN_ROWS, 128), XY, 0, 0)  26.7 us
    all_to_all x1, blocking collectives, on_device(): lax.all_to_all(halo, XY + GZ, 0, 0, axis_index_groups=near_groups(FAR_SEN...  17.8 us
    all_to_all x1, blocking collectives, on_device(): result = lax.all_to_all(result.reshape(NXY, OUT_ROWS, 128), XY, 0, 0)  15.2 us
    pallas_call x1, Pallas kernels, on_device(): pl.pallas_call(main_kernel, out_shape=on_chip(NXY * OUT_ROWS, 128), in_sp...  9.56 us
    all_to_all x1, blocking collectives, on_device(): lax.all_to_all(sums, XY + GZ, 0, 0, axis_index_groups=near_groups((3, 2,...  8.59 us

profile of v7, /device:TPU:1, one launch (start us, length us, event | category | flops | bytes accessed | tf_op | source)
XLA Modules:
  0.0 81.7 jit_solution(6896966994692620314)
XLA Ops:
  0.6 1.2 %transpose.1 = (f32[128,128]{1,0:T(8,128)S(1)}, f32[384,128]{1,0:T(8,128)S(1)}, f32[8,16,128]{2,1,0:T(8,128)S(1)}) custom-call(s32[1]{0:T(128)} %bitcast.g_ref, f32[27,2,2,128]{3,2,1,0:T(2,128)} %u_ref.1, f32[3,2,2,128]{3,2,1,0:T(2,128)} %v_ref.1, f32[3,6,6,384]{3,2,1,0:T(8,128)} %x_ref.1), custom_call_target="tpu_custom_call" | custom-call | tf_op jit(solution)/shard_map/transpose/pallas_call | solution.py:737
  1.8 17.8 %all_to_all.20.halo_ref = f32[8,16,128]{2,1,0:T(8,128)S(1)} all-to-all(f32[8,16,128]{2,1,0:T(8,128)S(1)} %get-tuple-element.11), channel_id=1, replica_groups={{0,129,2,131,4,133,6,135},{8,137,10,139,12,141,14,143},{16,145,18,147,2..., dimensions={0} | all-to-all | bytes 131072 | tf_op jit(solution)/shard_map/all_to_all | solution.py:745
  19.7 0.3 pack.1
  20.0 26.7 %all_to_all.21 = f32[32,40,128]{2,1,0:T(8,128)S(1)} all-to-all(f32[32,40,128]{2,1,0:T(8,128)S(1)} %bitcast.5), channel_id=1, replica_groups=mesh['gx_0'=4,'gx_1'=2,'gy'=4,'gz_0'=4,'gz_1'=2] {'gx_0','gx_1','gy'}, dimensions={0} | all-to-all | bytes 1310720 | tf_op jit(solution)/shard_map/all_to_all | solution.py:761
  46.7 9.6 %remap_and_gradient.1 = f32[512,128]{1,0:T(8,128)S(1)} custom-call(s32[1]{0:T(128)} %bitcast.g_ref, f32[1280,128]{1,0:T(8,128)S(1)} %bitcast.6), custom_call_target="tpu_custom_call" | custom-call | tf_op jit(solution)/shard_map/remap_and_gradient/pallas_call | solution.py:762
  56.3 15.2 %all_to_all.22 = f32[32,16,128]{2,1,0:T(8,128)S(1)} all-to-all(f32[32,16,128]{2,1,0:T(8,128)S(1)} %bitcast.7), channel_id=1, replica_groups=mesh['gx_0'=4,'gx_1'=2,'gy'=4,'gz_0'=4,'gz_1'=2] {'gx_0','gx_1','gy'}, dimensions={0} | all-to-all | bytes 524288 | tf_op jit(solution)/shard_map/all_to_all | solution.py:770
  71.5 1.0 %unpack.1 = (f32[27,2,2,128]{3,2,1,0:T(2,128)}, f32[3,6,6,384]{3,2,1,0:T(8,128)}, f32[8,1,128]{2,1,0:T(1,128)S(1)}) custom-call(f32[512,128]{1,0:T(8,128)S(1)} %bitcast.8), custom_call_target="tpu_custom_call" | custom-call | tf_op jit(solution)/shard_map/unpack/pallas_call | solution.py:771
  72.5 8.6 %all_to_all.23.sums_ref = f32[8,1,128]{2,1,0:T(1,128)S(1)} all-to-all(f32[8,1,128]{2,1,0:T(1,128)S(1)} %get-tuple-element.14), channel_id=1, replica_groups={{0,193,2,195,4,197,6,199},{8,201,10,203,12,205,14,207},{16,209,18,211,2..., dimensions={0} | all-to-all | bytes 8192 | tf_op jit(solution)/shard_map/all_to_all | solution.py:779
  81.1 0.7 checks.1

commit v8 on v7

--- a/solution.py
+++ b/solution.py
@@ -335,7 +335,8 @@
                 dst[at + k * 16 + line] = out[k]
         return carry
 
-    lax.fori_loop(0, 3, one, 0)
+    for c in range(3):
+        one(c, 0)
 
 
 def legendre_line(u):
@@ -390,9 +391,9 @@
 
 def stress(j_s, size_s, g_s, p_s):
     def one(pr, energy):
-        weights = [weight_of(2 * pr), weight_of(2 * pr + 1)]
-        for t in range(8):
-            q = pr * 8 + t
+        weights = [weight_of(4 * pr + n) for n in range(4)]
+        for t in range(16):
+            q = pr * 16 + t
             pair_weight = weights[t // 4]
             jac = jacobian(j_s, q)
             for c in range(3):
@@ -418,15 +419,15 @@
                     )
         return energy
 
-    return lax.fori_loop(0, 8, one, jnp.zeros((8, 128), jnp.float32))
+    return lax.fori_loop(0, 4, one, jnp.zeros((8, 128), jnp.float32))
 
 
 def trial_terms(j_s, size_s, g_s, d_s):
     def one(pr, sums):
         e2, e3, e4 = sums
-        weights = [weight_of(2 * pr), weight_of(2 * pr + 1)]
-        for t in range(8):
-            q = pr * 8 + t
+        weights = [weight_of(4 * pr + n) for n in range(4)]
+        for t in range(16):
+            q = pr * 16 + t
             pair_weight = weights[t // 4]
             jac = jacobian(j_s, q)
             der = jacobian(d_s, q)
@@ -449,7 +450,7 @@
         return e2, e3, e4
 
     zero = jnp.zeros((8, 128), jnp.float32)
-    e2, e3, e4 = lax.fori_loop(0, 8, one, (zero, zero, zero))
+    e2, e3, e4 = lax.fori_loop(0, 4, one, (zero, zero, zero))
     return 2.0 * e2, -4.0 * e3, e4
 
 

time: 82.7 us -> 82.6 us (level)
  no operation moved by 1% of the time
where the time goes in v8:
time: 82.6 us; the launch traced here: 81.7 us
  blocking collectives  68.3 us (83%)
  Pallas kernels  12.7 us (15%)
    all_to_all x1, blocking collectives, on_device(): spread = lax.all_to_all(packed.reshape(NXY, IN_ROWS, 128), XY, 0, 0)  26.7 us
    all_to_all x1, blocking collectives, on_device(): lax.all_to_all(halo, XY + GZ, 0, 0, axis_index_groups=near_groups(FAR_SEN...  17.8 us
    all_to_all x1, blocking collectives, on_device(): result = lax.all_to_all(result.reshape(NXY, OUT_ROWS, 128), XY, 0, 0)  15.2 us
    pallas_call x1, Pallas kernels, on_device(): pl.pallas_call(main_kernel, out_shape=on_chip(NXY * OUT_ROWS, 128), in_sp...  9.48 us
    all_to_all x1, blocking collectives, on_device(): lax.all_to_all(sums, XY + GZ, 0, 0, axis_index_groups=near_groups((3, 2,...  8.59 us

profile of v8, /device:TPU:1, one launch (start us, length us, event | category | flops | bytes accessed | tf_op | source)
XLA Modules:
  0.0 81.7 jit_solution(3951610465318923860)
XLA Ops:
  0.6 1.2 %transpose.1 = (f32[128,128]{1,0:T(8,128)S(1)}, f32[384,128]{1,0:T(8,128)S(1)}, f32[8,16,128]{2,1,0:T(8,128)S(1)}) custom-call(s32[1]{0:T(128)} %bitcast.g_ref, f32[27,2,2,128]{3,2,1,0:T(2,128)} %u_ref.1, f32[3,2,2,128]{3,2,1,0:T(2,128)} %v_ref.1, f32[3,6,6,384]{3,2,1,0:T(8,128)} %x_ref.1), custom_call_target="tpu_custom_call" | custom-call | tf_op jit(solution)/shard_map/transpose/pallas_call | solution.py:738
  1.8 17.8 %all_to_all.20.halo_ref = f32[8,16,128]{2,1,0:T(8,128)S(1)} all-to-all(f32[8,16,128]{2,1,0:T(8,128)S(1)} %get-tuple-element.11), channel_id=1, replica_groups={{0,129,2,131,4,133,6,135},{8,137,10,139,12,141,14,143},{16,145,18,147,2..., dimensions={0} | all-to-all | bytes 131072 | tf_op jit(solution)/shard_map/all_to_all | solution.py:746
  19.7 0.3 pack.1
  20.0 26.7 %all_to_all.21 = f32[32,40,128]{2,1,0:T(8,128)S(1)} all-to-all(f32[32,40,128]{2,1,0:T(8,128)S(1)} %bitcast.5), channel_id=1, replica_groups=mesh['gx_0'=4,'gx_1'=2,'gy'=4,'gz_0'=4,'gz_1'=2] {'gx_0','gx_1','gy'}, dimensions={0} | all-to-all | bytes 1310720 | tf_op jit(solution)/shard_map/all_to_all | solution.py:762
  46.7 9.5 %remap_and_gradient.1 = f32[512,128]{1,0:T(8,128)S(1)} custom-call(s32[1]{0:T(128)} %bitcast.g_ref, f32[1280,128]{1,0:T(8,128)S(1)} %bitcast.6), custom_call_target="tpu_custom_call" | custom-call | tf_op jit(solution)/shard_map/remap_and_gradient/pallas_call | solution.py:763
  56.2 15.2 %all_to_all.22 = f32[32,16,128]{2,1,0:T(8,128)S(1)} all-to-all(f32[32,16,128]{2,1,0:T(8,128)S(1)} %bitcast.7), channel_id=1, replica_groups=mesh['gx_0'=4,'gx_1'=2,'gy'=4,'gz_0'=4,'gz_1'=2] {'gx_0','gx_1','gy'}, dimensions={0} | all-to-all | bytes 524288 | tf_op jit(solution)/shard_map/all_to_all | solution.py:771
  71.4 1.0 %unpack.1 = (f32[27,2,2,128]{3,2,1,0:T(2,128)}, f32[3,6,6,384]{3,2,1,0:T(8,128)}, f32[8,1,128]{2,1,0:T(1,128)S(1)}) custom-call(f32[512,128]{1,0:T(8,128)S(1)} %bitcast.8), custom_call_target="tpu_custom_call" | custom-call | tf_op jit(solution)/shard_map/unpack/pallas_call | solution.py:772
  72.4 8.6 %all_to_all.23.sums_ref = f32[8,1,128]{2,1,0:T(1,128)S(1)} all-to-all(f32[8,1,128]{2,1,0:T(1,128)S(1)} %get-tuple-element.14), channel_id=1, replica_groups={{0,193,2,195,4,197,6,199},{8,201,10,203,12,205,14,207},{16,209,18,211,2..., dimensions={0} | all-to-all | bytes 8192 | tf_op jit(solution)/shard_map/all_to_all | solution.py:780
  81.0 0.7 checks.1
